TPU v7x, 8 devices: a whole 2x2x1 slice. The times are simulated.
8 devices in a mesh: tp: 2 (over z, y), ep: 4 (over x, core).
Axes of the slice: x: 2, y: 2, z: 1, core: 2. Of those that a mesh axis runs over, the one named last changes fastest.
Arguments:
- x_tok: bfloat16 [32768, 768], P('ep')
- dy_tok: bfloat16 [32768, 768], P('ep')
- route_idx: int32 [32768, 2], P('ep')
- norm_scale: float32 [768], replicated
- w_router: float32 [768, 32], replicated
- w_gate: bfloat16 [32, 768, 3072], P('ep', None, 'tp')
- w_lin: bfloat16 [32, 768, 3072], P('ep', None, 'tp')
- w_out: bfloat16 [32, 3072, 768], P('ep', 'tp')
Outputs:
- output 1: bfloat16 [32768, 768], P('ep')
- output 2: float32 [2], replicated
- output 3: bfloat16 [32768, 768], P('ep')
- output 4: float32 [768], replicated
- output 5: float32 [768, 32], replicated
- output 6: float32 [32, 768, 3072], P('ep', None, 'tp')
- output 7: float32 [32, 768, 3072], P('ep', None, 'tp')
- output 8: float32 [32, 3072, 768], P('ep', 'tp')
All inputs are finite; a program needn't handle non-finite values.
Results may differ from a plain program's by a relative error of at most 0.015982.
Values are sent between devices in bfloat16 or wider.
A program may use at most 1 GiB of HBM per device.

v0:
```python
import jax
import jax.numpy as jnp
from jax import lax
from jax.sharding import PartitionSpec as P

NORM_EPS = 1e-6
Z_COEF = 0.001
AUX_COEF = 0.01


def gelu_fn(pre_act):
    return jax.nn.gelu(pre_act, approximate=True)


def route_slots(route_ids, experts, slot_cap, stride):
    expert_ids = jnp.arange(experts, dtype=jnp.int32)
    hit_first = (route_ids[:, 0:1] == expert_ids).astype(jnp.int32)
    hit_second = (route_ids[:, 1:2] == expert_ids).astype(jnp.int32)
    rank_first = jnp.cumsum(hit_first, axis=0) - hit_first
    rank_second = jnp.cumsum(hit_second, axis=0) - hit_second + jnp.sum(hit_first, axis=0)
    pos_first = jnp.sum(rank_first * hit_first, axis=1)
    pos_second = jnp.sum(rank_second * hit_second, axis=1)
    overflow = experts * stride
    slot_first = jnp.where(pos_first < slot_cap, route_ids[:, 0] * stride + pos_first, overflow)
    slot_second = jnp.where(pos_second < slot_cap, route_ids[:, 1] * stride + pos_second, overflow)
    return slot_first, slot_second


def slot_tables(slot_first, slot_second, gate_first, gate_second, slot_total):
    tok_count = slot_first.shape[0]
    tok_ids = jnp.arange(tok_count, dtype=jnp.int32)
    slot_tok = jnp.full((slot_total + 1,), tok_count, jnp.int32)
    slot_tok = slot_tok.at[slot_first].set(tok_ids).at[slot_second].set(tok_ids)
    slot_gate = jnp.zeros((slot_total + 1,), jnp.float32)
    slot_gate = slot_gate.at[slot_first].set(gate_first).at[slot_second].set(gate_second)
    return slot_tok[:slot_total], slot_gate[:slot_total]


def pick_rows(row_data, slot_index):
    return jnp.take(row_data, slot_index, axis=0, mode='fill', fill_value=0)


def solution(mesh):
    ep_size = mesh.shape['ep']

    def device_block(x_loc, dy_loc, idx_loc, norm_scale, w_router, gate_loc, lin_loc, out_loc):
        tok_count, model_width = x_loc.shape
        experts = w_router.shape[1]
        local_exp = gate_loc.shape[0]
        tokens = tok_count * ep_size
        slot_cap = (5 * tok_count + 2 * experts - 1) // (2 * experts)
        x_wide = x_loc.astype(jnp.float32)
        inv_rms = lax.rsqrt(jnp.mean(x_wide * x_wide, axis=-1, keepdims=True) + NORM_EPS)
        x_norm = x_wide * inv_rms
        u_tok = (x_norm * norm_scale).astype(jnp.bfloat16)
        u_wide = u_tok.astype(jnp.float32)
        logits = jnp.dot(u_wide, w_router, preferred_element_type=jnp.float32)
        log_norm = jax.nn.logsumexp(logits, axis=-1)
        router_prob = jnp.exp(logits - log_norm[:, None])
        expert_ids = jnp.arange(experts, dtype=jnp.int32)
        one_first = (idx_loc[:, 0:1] == expert_ids).astype(jnp.float32)
        one_second = (idx_loc[:, 1:2] == expert_ids).astype(jnp.float32)
        first_count = lax.psum(jnp.sum(one_first, axis=0), 'ep')
        prob_sum = lax.psum(jnp.sum(router_prob, axis=0), 'ep')
        norm_sq = lax.psum(jnp.sum(log_norm * log_norm), 'ep')
        frac_first = first_count / tokens
        z_loss = Z_COEF * norm_sq / tokens
        aux_loss = AUX_COEF * experts * jnp.sum(frac_first * prob_sum) / tokens
        gate_first = jnp.sum(router_prob * one_first, axis=-1)
        gate_second = jnp.sum(router_prob * one_second, axis=-1)
        gate_total = gate_first + gate_second
        norm_first = gate_first / gate_total
        norm_second = gate_second / gate_total
        slot_first, slot_second = route_slots(idx_loc, experts, slot_cap, slot_cap)
        slot_tok, slot_gate = slot_tables(slot_first, slot_second, norm_first, norm_second, experts * slot_cap)
        disp_rows = pick_rows(u_tok, slot_tok).reshape(experts, slot_cap, model_width)
        recv_rows = lax.all_to_all(disp_rows, 'ep', 0, 0, tiled=True).reshape(ep_size, local_exp, slot_cap, model_width)
        a_gate = jnp.einsum('sxcd,xdf->sxcf', recv_rows, gate_loc, preferred_element_type=jnp.float32)
        a_lin = jnp.einsum('sxcd,xdf->sxcf', recv_rows, lin_loc, preferred_element_type=jnp.float32)
        gelu_val, gelu_back = jax.vjp(gelu_fn, a_gate)
        hidden = (gelu_val * a_lin).astype(jnp.bfloat16)
        part_out = jnp.einsum('sxcf,xfd->sxcd', hidden, out_loc, preferred_element_type=jnp.float32).astype(jnp.bfloat16)
        exp_out = lax.psum(part_out, 'tp')
        back_rows = lax.all_to_all(exp_out.reshape(experts, slot_cap, model_width), 'ep', 0, 0, tiled=True).reshape(experts * slot_cap, model_width)
        out_first = pick_rows(back_rows, slot_first).astype(jnp.float32)
        out_second = pick_rows(back_rows, slot_second).astype(jnp.float32)
        y_loc = (x_wide + norm_first[:, None] * out_first + norm_second[:, None] * out_second).astype(jnp.bfloat16)
        dy_wide = dy_loc.astype(jnp.float32)
        dn_first = jnp.sum(dy_wide * out_first, axis=-1)
        dn_second = jnp.sum(dy_wide * out_second, axis=-1)
        do_slot = (pick_rows(dy_loc, slot_tok).astype(jnp.float32) * slot_gate[:, None]).astype(jnp.bfloat16)
        do_recv = lax.all_to_all(do_slot.reshape(experts, slot_cap, model_width), 'ep', 0, 0, tiled=True).reshape(ep_size, local_exp, slot_cap, model_width)
        d_hidden = jnp.einsum('sxcd,xfd->sxcf', do_recv, out_loc, preferred_element_type=jnp.float32)
        da_gate = gelu_back(d_hidden * a_lin)[0].astype(jnp.bfloat16)
        da_lin = (d_hidden * gelu_val).astype(jnp.bfloat16)
        d_out = jnp.einsum('sxcf,sxcd->xfd', hidden, do_recv, preferred_element_type=jnp.float32)
        d_gate = jnp.einsum('sxcd,sxcf->xdf', recv_rows, da_gate, preferred_element_type=jnp.float32)
        d_lin = jnp.einsum('sxcd,sxcf->xdf', recv_rows, da_lin, preferred_element_type=jnp.float32)
        du_part = jnp.einsum('sxcf,xdf->sxcd', da_gate, gate_loc, preferred_element_type=jnp.float32) + jnp.einsum('sxcf,xdf->sxcd', da_lin, lin_loc, preferred_element_type=jnp.float32)
        du_slot = lax.psum(du_part.astype(jnp.bfloat16), 'tp')
        du_back = lax.all_to_all(du_slot.reshape(experts, slot_cap, model_width), 'ep', 0, 0, tiled=True).reshape(experts * slot_cap, model_width)
        du_exp = pick_rows(du_back, slot_first).astype(jnp.float32) + pick_rows(du_back, slot_second).astype(jnp.float32)
        gate_mix = norm_first * dn_first + norm_second * dn_second
        aux_coef = AUX_COEF * experts * frac_first
        d_logits = router_prob * (aux_coef - jnp.sum(aux_coef * router_prob, axis=-1, keepdims=True))
        d_logits = d_logits + (2.0 * Z_COEF) * log_norm[:, None] * router_prob
        d_logits = d_logits + one_first * (norm_first * (dn_first - gate_mix))[:, None]
        d_logits = d_logits + one_second * (norm_second * (dn_second - gate_mix))[:, None]
        d_router = lax.psum(jnp.einsum('td,te->de', u_wide, d_logits, preferred_element_type=jnp.float32), 'ep')
        du_all = du_exp + jnp.einsum('te,de->td', d_logits, w_router, preferred_element_type=jnp.float32)
        d_scale = lax.psum(jnp.sum(du_all * x_norm, axis=0), 'ep')
        dx_norm = du_all * norm_scale
        dx_loc = (dy_wide + inv_rms * (dx_norm - x_norm * jnp.mean(dx_norm * x_norm, axis=-1, keepdims=True))).astype(jnp.bfloat16)
        losses = jnp.stack([z_loss, aux_loss])
        return (y_loc, losses, dx_loc, d_scale, d_router, d_gate, d_lin, d_out)

    tok_spec = P('ep', None)
    in_spec = P('ep', None, 'tp')
    out_spec = P('ep', 'tp', None)
    return jax.shard_map(device_block, mesh=mesh, in_specs=(tok_spec, tok_spec, tok_spec, P(), P(), in_spec, in_spec, out_spec), out_specs=(tok_spec, P(), tok_spec, P(), P(), in_spec, in_spec, out_spec), check_vma=False)
```

profile of v0, /device:TPU:0, one launch (start us, length us, event | category | flops | bytes accessed | tf_op | source)
XLA Modules:
  0.0 4103.0 jit_solution(15865049810454729772)
XLA Ops:
  7.2 1.0 fusion.75
  8.2 0.1 fusion.62
  8.3 9.5 reduce-window.14
  17.8 0.9 slice_reduce_fusion.1
  18.8 0.2 reduce-window.15
  19.0 0.3 broadcast_add_fusion.1
  19.3 0.1 fusion.63
  19.4 9.5 reduce-window.16
  29.0 0.9 slice_reduce_fusion
  29.9 0.2 reduce-window.19
  30.1 0.3 broadcast_add_fusion
  30.4 0.9 convert_reduce_fusion
  31.4 0.9 fusion.60
  32.3 1.1 compare_select_fusion.1
  33.4 30.5 scatter_custom_fusion
  63.9 31.0 scatter_fusion
  95.0 7.1 fusion.35
  102.2 11.8 fusion.30
  114.0 97.2 %gather_fusion = bf16[20480,768]{1,0:T(8,128)(2,1)} fusion(bf16[8192,768]{1,0:T(8,128)(2,1)} %fusion.30, s32[20480]{0:T(1024)S(1)} %fusion.65), kind=kCustom, calls=%fused_computation.clone | custom fusion | bytes 62996480 | tf_op jit(solution)/shard_map/jit(_take)/gather | solution.py:40
  211.2 21.7 broadcast_select_fusion
  232.9 9.4 all-to-all-start
  242.3 0.3 convert_reduce_fusion.1
  242.5 341.3 %psum.51 = f32[32]{0:T(128)S(1)} all-reduce(f32[32]{0:T(128)S(1)} %convert_reduce_fusion.1), channel_id=1, replica_groups=mesh['tp'=2,'ep'=4] {'ep'}, use_global_device_ids=true, to_apply=%region_18.21 | all-reduce | flops 32 | bytes 256 | tf_op jit(solution)/shard_map/psum | solution.py:63
  583.8 8.3 fusion.76
  592.2 0.2 exponential_reduce_fusion
  592.4 0.7 broadcast_multiply_fusion
  593.1 1.3 multiply_reduce_fusion
  594.5 30.5 scatter_custom_fusion.2
  625.0 30.7 scatter_fusion.1
  655.7 97.2 %gather_fusion.3 = bf16[20480,768]{1,0:T(8,128)(2,1)} fusion(bf16[8192,768]{1,0:T(8,128)(2,1)} %param.13, s32[20480]{0:T(1024)S(1)} %fusion.65), kind=kCustom, calls=%fused_computation.2.clone | custom fusion | bytes 62996480 | tf_op jit(solution)/shard_map/jit(_take)/gather | solution.py:40
  752.9 21.4 multiply_convert_fusion
  774.3 9.5 all-to-all-start.2
  783.9 65.1 %fusion.24 = f32[8,4,640,1536]{3,2,1,0:T(8,128)} fusion(bf16[4,8,640,768]{3,2,1,0:T(8,128)(2,1)} %bitcast.11, bf16[8,768,1536]{2,1,0:T(8,128)(2,1)} %param.18), kind=kOutput, calls=%fused_computation.53 | convolution fusion | flops 48318382080 | bytes 176160768 | tf_op jit(solution)/shard_map/sxcd,xdf->sxcf/dot_general | solution.py:79
  849.0 65.1 %fusion.26 = f32[8,4,640,1536]{3,2,1,0:T(8,128)} fusion(bf16[4,8,640,768]{3,2,1,0:T(8,128)(2,1)} %bitcast.11, bf16[8,768,1536]{2,1,0:T(8,128)(2,1)} %param.17), kind=kOutput, calls=%fused_computation.55 | convolution fusion | flops 48318382080 | bytes 176160768 | tf_op jit(solution)/shard_map/sxcd,xdf->sxcf/dot_general | solution.py:78
  914.1 209.8 %all-to-all-done.2 = bf16[32,640,768]{2,1,0:T(8,128)(2,1)} async-done(((bf16[32,640,768]{2,1,0:T(8,128)(2,1)}), bf16[32,640,768]{2,1,0:T(8,128)(2,1)}, u32[]{:S(2)}, u32[]{:S(2)}) %all-to-all-start.2) | async-done | bytes 31457312 | tf_op jit(solution)/shard_map/all_to_all | solution.py:92
  1123.8 173.8 %fusion.7 = (bf16[4,8,640,1536]{3,2,0,1:T(8,128)(2,1)}, bf16[4,8,640,1536]{3,2,0,1:T(8,128)(2,1)}, bf16[4,8,640,1536]{3,2,0,1:T(8,128)(2,1)}) fusion(f32[8,4,640,1536]{3,2,1,0:T(8,128)} %fusion.26, f32[8,4,640,1536]{3,2,1,0:T(8,128)} %fusion.24, bf16[8,1536,768]{2,1,0:T(8,128)(2,1)} %param.19, bf16[4,8,640,768]{3,2,1,0:T(8,128)(2,1)} %bitcast.26), kind=kOutput, calls=%fused_computation.21 | convolution fusion | flops 49136271360 | bytes 490733568 | tf_op jit(solution)/shard_map/sxcd,xfd->sxcf/dot_general | solution.py:93
  1297.6 62.3 %fusion.41 = f32[8,4,640,768]{3,2,1,0:T(8,128)} fusion(bf16[4,8,640,1536]{3,2,0,1:T(8,128)(2,1)} %get-tuple-element.28, bf16[8,768,1536]{2,1,0:T(8,128)(2,1)} %param.17), kind=kOutput, calls=%fused_computation.71 | convolution fusion | flops 48318382080 | bytes 144703488 | tf_op jit(solution)/shard_map/sxcf,xdf->sxcd/dot_general | solution.py:99
  1359.9 64.8 %fusion.19 = bf16[4,8,640,768]{3,2,0,1:T(8,128)(2,1)} fusion(f32[8,4,640,768]{3,2,1,0:T(8,128)} %fusion.41, bf16[4,8,640,1536]{3,2,0,1:T(8,128)(2,1)} %get-tuple-element.27, bf16[8,768,1536]{2,1,0:T(8,128)(2,1)} %param.18), kind=kOutput, calls=%fused_computation.44 | convolution fusion | flops 48349839360 | bytes 176160768 | tf_op jit(solution)/shard_map/sxcf,xdf->sxcd/dot_general | solution.py:99
  1424.7 21.6 copy.23
  1446.3 60.7 %convert_bitcast_fusion = bf16[4,8,640,768]{3,2,0,1:T(8,128)(2,1)} fusion(bf16[4,8,640,1536]{3,2,0,1:T(8,128)(2,1)} %get-tuple-element.29, bf16[8,1536,768]{2,1,0:T(8,128)(2,1)} %param.19), kind=kOutput, calls=%fused_computation.47 | convolution fusion | flops 48334110720 | bytes 113246208 | tf_op jit(solution)/shard_map/sxcf,xfd->sxcd/dot_general | solution.py:82
  1507.0 21.6 copy.21
  1528.6 1363.2 %all-reduce.7.cloned.1.call-done = (bf16[32,640,768]{2,1,0:T(8,128)(2,1)}, bf16[32,640,768]{2,1,0:T(8,128)(2,1)}) async-done(((bf16[32,640,768]{2,1,0:T(8,128)(2,1)}, bf16[32,640,768]{2,1,0:T(8,128)(2,1)}), (bf16[32,640,768]{2,1,0:T(8,128)(2,1)}, bf16[32,640,768]{2,1,0:T(8,128)(2,1)})) %all-reduce.7.cloned.1.call-update) | async-done | bytes 62914576 | tf_op jit(solution)/shard_map/psum | solution.py:83
  2891.8 9.6 all-to-all-start.1
  2901.4 0.7 multiply_reduce_fusion.1
  2902.1 0.6 broadcast_clamp_fusion
  2902.8 0.6 broadcast_clamp_fusion.1
  2903.4 0.6 compare_and_fusion.1
  2904.0 337.4 %all-to-all-done.1 = bf16[32,640,768]{2,1,0:T(8,128)(2,1)} async-done(((bf16[32,640,768]{2,1,0:T(8,128)(2,1)}), bf16[32,640,768]{2,1,0:T(8,128)(2,1)}, u32[]{:S(2)}, u32[]{:S(2)}) %all-to-all-start.1) | async-done | bytes 31457312 | tf_op jit(solution)/shard_map/all_to_all | solution.py:84
  3241.4 9.4 all-to-all-start.3
  3250.9 57.7 %fusion.46 = f32[8,768,1536]{2,1,0:T(8,128)} fusion(bf16[4,8,640,768]{3,2,1,0:T(8,128)(2,1)} %bitcast.11, bf16[4,8,640,1536]{3,2,0,1:T(8,128)(2,1)} %get-tuple-element.28), kind=kOutput, calls=%fused_computation.76 | convolution fusion | flops 48318382080 | bytes 132120576 | tf_op jit(solution)/shard_map/sxcd,sxcf->xdf/dot_general | solution.py:97
  3308.5 57.5 %fusion.49 = f32[8,768,1536]{2,1,0:T(8,128)} fusion(bf16[4,8,640,768]{3,2,1,0:T(8,128)(2,1)} %bitcast.11, bf16[4,8,640,1536]{3,2,0,1:T(8,128)(2,1)} %get-tuple-element.27), kind=kOutput, calls=%fused_computation.77 | convolution fusion | flops 48318382080 | bytes 132120576 | tf_op jit(solution)/shard_map/sxcd,sxcf->xdf/dot_general | solution.py:98
  3366.0 58.5 %fusion.52 = f32[8,1536,768]{2,1,0:T(8,128)} fusion(bf16[4,8,640,1536]{3,2,0,1:T(8,128)(2,1)} %get-tuple-element.29, bf16[4,8,640,768]{3,2,1,0:T(8,128)(2,1)} %bitcast.26), kind=kOutput, calls=%fused_computation.78 | convolution fusion | flops 48318382080 | bytes 132120576 | tf_op jit(solution)/shard_map/sxcf,sxcd->xfd/dot_general | solution.py:96
  3424.5 146.4 %gather_fusion.2 = bf16[8192,768]{1,0:T(8,128)(2,1)} fusion(bf16[20480,768]{1,0:T(8,128)(2,1)} %bitcast.22, s32[8192]{0:T(1024)S(1)} %copy-done.23), kind=kCustom, calls=%fused_computation.3.clone | custom fusion | bytes 25198592 | tf_op jit(solution)/shard_map/jit(_take)/gather | solution.py:40
  3570.8 141.3 %gather_fusion.1 = bf16[8192,768]{1,0:T(8,128)(2,1)} fusion(bf16[20480,768]{1,0:T(8,128)(2,1)} %bitcast.22, s32[8192]{0:T(1024)S(1)} %copy-done.22), kind=kCustom, calls=%fused_computation.1.clone | custom fusion | bytes 25198592 | tf_op jit(solution)/shard_map/jit(_take)/gather | solution.py:40
  3712.1 146.6 %gather_fusion.5 = bf16[8192,768]{1,0:T(8,128)(2,1)} fusion(bf16[20480,768]{1,0:T(8,128)(2,1)} %bitcast.33, s32[8192]{0:T(1024)S(1)} %copy-done.23), kind=kCustom, calls=%fused_computation.5.clone | custom fusion | bytes 25198592 | tf_op jit(solution)/shard_map/jit(_take)/gather | solution.py:40
  3858.8 141.4 %gather_fusion.4 = bf16[8192,768]{1,0:T(8,128)(2,1)} fusion(bf16[20480,768]{1,0:T(8,128)(2,1)} %bitcast.33, s32[8192]{0:T(1024)S(1)} %copy-done.22), kind=kCustom, calls=%fused_computation.4.clone | custom fusion | bytes 25198592 | tf_op jit(solution)/shard_map/jit(_take)/gather | solution.py:40
  4000.3 26.4 fusion.36
  4026.7 7.2 fusion.70
  4034.0 21.9 fusion.34
  4055.9 14.5 all-reduce
  4070.4 0.6 multiply_reduce_fusion.2
  4071.0 21.3 fusion.38
  4093.6 0.6 pad_maximum_fusion
  4094.2 1.5 copy.66
  (88 shorter events, 0.4 us)
Async XLA Ops:
  7.2 576.7 %copy-start = (f32[768,32]{0,1:T(8,128)S(1)}, f32[768,32]{0,1:T(8,128)}, u32[]{:S(2)}) copy-start(f32[768,32]{0,1:T(8,128)} %param.16) | copy-start | bytes 294916
  8.2 585.0 %copy-start.3 = (s32[8192,1]{0,1:T(1,128)}, s32[8192,1]{0,1:T(1,128)S(1)}, u32[]{:S(2)}) copy-start(s32[8192,1]{0,1:T(1,128)S(1)} %get-tuple-element.38) | copy-start | bytes 98308
  8.2 585.0 %copy-start.6 = (s32[8192,1]{0,1:T(1,128)}, s32[8192,1]{0,1:T(1,128)S(1)}, u32[]{:S(2)}) copy-start(s32[8192,1]{0,1:T(1,128)S(1)} %get-tuple-element.37) | copy-start | bytes 98308
  31.4 2.0 copy-start.14
  32.3 62.7 %copy-start.16 = (s32[8192]{0:T(1024)}, s32[8192]{0:T(1024)S(1)}, u32[]{:S(2)}) copy-start(s32[8192]{0:T(1024)S(1)} %fusion.60) | copy-start | bytes 98308
  63.9 38.3 copy-start.28
  102.2 109.0 %copy-start.18 = (f32[8192]{0:T(1024)}, f32[8192]{0:T(1024)S(1)}, u32[]{:S(2)}) copy-start(f32[8192]{0:T(1024)S(1)} %add_rsqrt_fusion) | copy-start | bytes 98308
  232.9 541.4 %all-to-all-start = ((bf16[32,640,768]{2,1,0:T(8,128)(2,1)}), bf16[32,640,768]{2,1,0:T(8,128)(2,1)}, u32[]{:S(2)}, u32[]{:S(2)}) async-start(bf16[32,640,768]{2,1,0:T(8,128)(2,1)} %bitcast.127), calls=%async_computation | async-start | bytes 62914560 | tf_op jit(solution)/shard_map/all_to_all | solution.py:77
  583.8 10.6 copy-start.33
  592.2 2.3 copy-start.1
  592.4 63.3 %copy-start.30 = (f32[32]{0:T(128)}, f32[32]{0:T(128)S(1)}, u32[]{:S(2)}) copy-start(f32[32]{0:T(128)S(1)} %broadcast_multiply_fusion.2) | copy-start | bytes 388
  593.1 1.3 copy-start.11
  594.5 30.5 copy-start.20
  594.5 61.2 %copy-start.9 = (f32[8192]{0:T(1024)}, f32[8192]{0:T(1024)S(1)}, u32[]{:S(2)}) copy-start(f32[8192]{0:T(1024)S(1)} %get-tuple-element.36) | copy-start | bytes 98308
  774.3 349.5 %all-to-all-start.2 = ((bf16[32,640,768]{2,1,0:T(8,128)(2,1)}), bf16[32,640,768]{2,1,0:T(8,128)(2,1)}, u32[]{:S(2)}, u32[]{:S(2)}) async-start(bf16[32,640,768]{2,1,0:T(8,128)(2,1)} %bitcast.128), calls=%async_computation.2 | async-start | bytes 62914560 | tf_op jit(solution)/shard_map/all_to_all | solution.py:92
  783.8 2108.0 %all-reduce.7.cloned.1.call-start = ((), (), s32[]{:S(2)}) async-start(), calls=%async_computation.5 | async-start | bytes 125829120 | tf_op jit(solution)/shard_map/psum | solution.py:83
  2891.8 9.6 copy-start.12
  2891.8 10.3 copy-start.7
  2891.8 10.3 copy-start.17
  2891.8 11.0 copy-start.4
  2891.8 11.0 copy-start.15
  2891.8 349.6 %all-to-all-start.1 = ((bf16[32,640,768]{2,1,0:T(8,128)(2,1)}), bf16[32,640,768]{2,1,0:T(8,128)(2,1)}, u32[]{:S(2)}, u32[]{:S(2)}) async-start(bf16[32,640,768]{2,1,0:T(8,128)(2,1)} %get-tuple-element.23), calls=%async_computation.1 | async-start | bytes 62914560 | tf_op jit(solution)/shard_map/all_to_all | solution.py:84
  3241.4 470.7 %all-to-all-start.3 = ((bf16[32,640,768]{2,1,0:T(8,128)(2,1)}), bf16[32,640,768]{2,1,0:T(8,128)(2,1)}, u32[]{:S(2)}, u32[]{:S(2)}) async-start(bf16[32,640,768]{2,1,0:T(8,128)(2,1)} %get-tuple-element.24), calls=%async_computation.3 | async-start | bytes 62914560 | tf_op jit(solution)/shard_map/all_to_all | solution.py:101
  3250.8 843.3 %all-reduce.5.cloned.1.call-start = ((), (), s32[]{:S(2)}) async-start(), calls=%async_computation.4 | async-start | bytes 196608 | tf_op jit(solution)/shard_map/psum | solution.py:109
  3366.0 58.5 %copy-start.23 = (s32[8192]{0:T(1024)S(1)}, s32[8192]{0:T(1024)}, u32[]{:S(2)}) copy-start(s32[8192]{0:T(1024)} %broadcast_clamp_fusion) | copy-start | bytes 98308
  3424.5 146.4 %copy-start.22 = (s32[8192]{0:T(1024)S(1)}, s32[8192]{0:T(1024)}, u32[]{:S(2)}) copy-start(s32[8192]{0:T(1024)} %broadcast_clamp_fusion.1) | copy-start | bytes 98308
  3858.8 141.4 %copy-start.10 = (f32[8192]{0:T(1024)S(1)}, f32[8192]{0:T(1024)}, u32[]{:S(2)}) copy-start(f32[8192]{0:T(1024)} %copy-done.9) | copy-start | bytes 98308
  3858.8 141.4 %copy-start.21 = (f32[8192]{0:T(1024)S(1)}, f32[8192]{0:T(1024)}, u32[]{:S(2)}) copy-start(f32[8192]{0:T(1024)} %copy-done.20) | copy-start | bytes 98308
  3858.8 141.4 %copy-start.26 = (pred[8192]{0:T(1024)(128)(4,1)S(1)}, pred[8192]{0:T(1024)(128)(4,1)}, u32[]{:S(2)}) copy-start(pred[8192]{0:T(1024)(128)(4,1)} %get-tuple-element.42) | copy-start | bytes 24580
  3858.8 141.4 %copy-start.27 = (pred[8192]{0:T(1024)(128)(4,1)S(1)}, pred[8192]{0:T(1024)(128)(4,1)}, u32[]{:S(2)}) copy-start(pred[8192]{0:T(1024)(128)(4,1)} %get-tuple-element.43) | copy-start | bytes 24580
  4000.2 26.5 copy-start.2
  4000.2 26.5 copy-start.5
  4000.2 26.5 copy-start.8
  4000.2 26.5 copy-start.13
  4000.2 26.5 copy-start.24
  4000.2 26.5 copy-start.25
  4000.2 26.5 copy-start.31
  4000.2 33.7 copy-start.19
  4000.2 33.7 copy-start.29
  4033.9 21.9 copy-start.32
  4034.0 36.4 copy-start.34
Sparse Core Ops, SparseCore 0:
  1528.7 1363.0 all-reduce.6
  4034.1 32.7 all-reduce.4
where the time goes:
time: 4120 us; the launch traced here: 4100 us
  waiting for transfers between devices  1910 us (46%)
  local copies, waits for them, and re-layouts  940 us (23%)
  matrix products  703 us (17%)
  blocking collectives  356 us (9%)
  other arithmetic  139 us (3%)
    psum x1, waiting for transfers between devices, device_block(): exp_out = lax.psum(part_out, 'tp')  1360 us
    gather x6, local copies, waits for them, and re-layouts, pick_rows(): return jnp.take(row_data, slot_index, axis=0, mode='fill', fill_value=0)  770 us
    psum x1, blocking collectives, device_block(): first_count = lax.psum(jnp.sum(one_first, axis=0), 'ep')  341 us
    all_to_all x1, waiting for transfers between devices, device_block(): lax.all_to_all(exp_out.reshape(experts, slot_cap, model_width), 'ep', 0,...  337 us
    all_to_all x1, waiting for transfers between devices, device_block(): lax.all_to_all(do_slot.reshape(experts, slot_cap, model_width), 'ep', 0,...  210 us
    dot_general x1, matrix products, device_block(): jnp.einsum('sxcd,xfd->sxcf', do_recv, out_loc, preferred_element_type=jnp...  174 us
  transfers between devices with their start and end apart: 6, of which 3 were waited for; matrix products, arithmetic and copies ran while one was open for 20% of the time, Pallas kernels for 0%

commit v1 on v0

v1 whole, which is shorter than its diff:
```python
import functools

import jax
import jax.numpy as jnp
from jax import lax
from jax.experimental import pallas as pl
from jax.experimental.pallas import tpu as pltpu
from jax.sharding import PartitionSpec as P


NORM_EPS = 1e-6
Z_COEF = 0.001
AUX_COEF = 0.01
GELU_A = 0.7978845608028654
GELU_B = 0.044715


def ffn_kernel(tp_ref, x_ref, dy_ref, gate_ref, scale_ref, wg_ref, wl_ref, wo_ref, *refs):
    (u_out, do_out, h_out, da_out, db_out, ok_out, os_out, dk_out, ds_out, u_s, do_s, o_acc, du_acc) = refs[-13:]
    f_id = pl.program_id(1)
    half = ok_out.shape[-1]

    @pl.when(f_id == 0)
    def _():
        gate = gate_ref[0]
        live = jnp.logical_not(gate < 0.0)
        x_wide = x_ref[0].astype(jnp.float32)
        inv = lax.rsqrt(jnp.mean(x_wide * x_wide, axis=-1, keepdims=True) + NORM_EPS)
        u_val = jnp.where(live, (x_wide * inv) * scale_ref[...], 0.0).astype(jnp.bfloat16)
        do_val = jnp.where(live, dy_ref[0].astype(jnp.float32) * gate, 0.0).astype(jnp.bfloat16)
        u_s[...] = u_val
        do_s[...] = do_val
        u_out[0, 0] = u_val
        do_out[0, 0] = do_val

    u_val = u_s[...]
    do_val = do_s[...]
    wg = wg_ref[0]
    wl = wl_ref[0]
    wo = wo_ref[0]
    nn = (((1,), (0,)), ((), ()))
    nt = (((1,), (1,)), ((), ()))
    dot = functools.partial(lax.dot_general, preferred_element_type=jnp.float32)
    a0 = dot(u_val, wg, nn)
    a1 = dot(u_val, wl, nn)
    dh = dot(do_val, wo, nt)
    sq = a0 * a0
    th = jnp.tanh(GELU_A * (a0 + GELU_B * (a0 * sq)))
    cdf = 0.5 + 0.5 * th
    ge = a0 * cdf
    slope = cdf + 0.5 * a0 * ((1.0 - th * th) * (GELU_A + (3.0 * GELU_A * GELU_B) * sq))
    h_val = (ge * a1).astype(jnp.bfloat16)
    da = (dh * a1 * slope).astype(jnp.bfloat16)
    db = (dh * ge).astype(jnp.bfloat16)
    h_out[0, 0] = h_val
    da_out[0, 0] = da
    db_out[0, 0] = db
    o_new = dot(h_val, wo, nn)
    du_new = dot(da, wg, nt) + dot(db, wl, nt)

    o_acc[...] = jnp.where(f_id == 0, 0.0, o_acc[...]) + o_new
    du_acc[...] = jnp.where(f_id == 0, 0.0, du_acc[...]) + du_new

    @pl.when(f_id == pl.num_programs(1) - 1)
    def _():
        first = tp_ref[0] == 0
        for acc, keep, send in ((o_acc, ok_out, os_out), (du_acc, dk_out, ds_out)):
            low = acc[:, :half].astype(jnp.bfloat16)
            high = acc[:, half:].astype(jnp.bfloat16)
            keep[0] = jnp.where(first, low, high)
            send[0] = jnp.where(first, high, low)


def router_kernel(blocks, cap, experts, local_exp, ep_ref, x_ref, idx_ref, scale_ref, wr_ref, prob_ref, col_ref, row_ref, tab_ref, sum_ref, carry, prob_acc, sq_acc):
    step = pl.program_id(0)
    rows = x_ref.shape[0]
    first = idx_ref[:, 0:1]
    second = idx_ref[:, 1:2]
    pair_lane = lax.broadcasted_iota(jnp.int32, (rows, 2 * experts), 1)

    @pl.when(step == 0)
    def _():
        carry[...] = jnp.zeros_like(carry)
        prob_acc[...] = jnp.zeros_like(prob_acc)
        sq_acc[...] = jnp.zeros_like(sq_acc)
        tab_ref[...] = jnp.zeros_like(tab_ref)

    @pl.when(step < blocks)
    def _():
        carry[...] += jnp.sum(jnp.where(first + experts == pair_lane, 1.0, 0.0), axis=0, keepdims=True)

    @pl.when(step >= blocks)
    def _():
        x_wide = x_ref[...].astype(jnp.float32)
        inv = lax.rsqrt(jnp.mean(x_wide * x_wide, axis=-1, keepdims=True) + NORM_EPS)
        u_val = ((x_wide * inv) * scale_ref[...]).astype(jnp.bfloat16)
        logits = jnp.dot(u_val.astype(jnp.float32), wr_ref[...], preferred_element_type=jnp.float32)
        top = jnp.max(logits, axis=-1, keepdims=True)
        log_norm = top + jnp.log(jnp.sum(jnp.exp(logits - top), axis=-1, keepdims=True))
        prob = jnp.exp(logits - log_norm)
        prob_ref[...] = prob
        prob_acc[...] += jnp.sum(prob, axis=0, keepdims=True)
        sq_acc[...] += jnp.sum(log_norm * log_norm, axis=0, keepdims=True)
        lane = lax.broadcasted_iota(jnp.int32, (rows, experts), 1)
        p_first = jnp.sum(jnp.where(first == lane, prob, 0.0), axis=-1, keepdims=True)
        p_second = jnp.sum(jnp.where(second == lane, prob, 0.0), axis=-1, keepdims=True)
        total = p_first + p_second
        n_first = p_first / total
        n_second = p_second / total
        sel_first = first == pair_lane
        sel_second = second + experts == pair_lane
        hits = jnp.where(sel_first | sel_second, 1.0, 0.0)
        below = lax.broadcasted_iota(jnp.int32, (rows, rows), 1) < lax.broadcasted_iota(jnp.int32, (rows, rows), 0)
        ranks = jnp.dot(jnp.where(below, 1.0, 0.0).astype(jnp.bfloat16), hits.astype(jnp.bfloat16), preferred_element_type=jnp.float32) + carry[...]
        carry[...] += jnp.sum(hits, axis=0, keepdims=True)
        pos_first = jnp.sum(jnp.where(sel_first, ranks, 0.0), axis=-1, keepdims=True).astype(jnp.int32)
        pos_second = jnp.sum(jnp.where(sel_second, ranks, 0.0), axis=-1, keepdims=True).astype(jnp.int32)
        for c, (route, pos) in enumerate(((first, pos_first), (second, pos_second))):
            kept = pos < cap
            owner = route // local_exp
            spot = (owner ^ ep_ref[0]) * (local_exp * cap) + (route - owner * local_exp) * cap + pos
            row_ref[:, c:c + 1] = jnp.where(kept, spot, 0)
            col_ref[:, 2 + c:3 + c] = jnp.where(kept, 1.0, 0.0)
        col_ref[:, 0:1] = n_first
        col_ref[:, 1:2] = n_second
        col_ref[:, 4:5] = inv
        col_ref[:, 5:6] = log_norm
        col_ref[:, 6:8] = jnp.zeros((rows, 2), jnp.float32)
        token = lax.broadcasted_iota(jnp.int32, (rows, 1), 0) + ((step - blocks) * rows + 1)
        tok_hi = (token // 128).astype(jnp.float32)
        tok_lo = (token % 128).astype(jnp.float32)
        wide = lax.broadcasted_iota(jnp.int32, (rows, 5 * experts), 1)
        expert = wide % experts
        place = lax.broadcasted_iota(jnp.int32, (rows, cap), 1)
        for route, pos, gate in ((first, pos_first, n_first), (second, pos_second, n_second)):
            hi = gate.astype(jnp.bfloat16).astype(jnp.float32)
            rest = gate - hi
            mid = rest.astype(jnp.bfloat16).astype(jnp.float32)
            vals = jnp.where(wide < experts, tok_hi, jnp.where(wide < 2 * experts, tok_lo, jnp.where(wide < 3 * experts, hi, jnp.where(wide < 4 * experts, mid, rest - mid))))
            left = jnp.where(expert == route, vals, 0.0).astype(jnp.bfloat16)
            right = jnp.where(place == pos, 1.0, 0.0).astype(jnp.bfloat16)
            tab_ref[...] += lax.dot_general(left, right, (((0,), (0,)), ((), ())), preferred_element_type=jnp.float32)

    @pl.when(step == 2 * blocks - 1)
    def _():
        sum_ref[...] = jnp.zeros_like(sum_ref)
        sum_ref[0:1, 0:experts] = carry[:, :experts]
        sum_ref[1:2, 0:experts] = prob_acc[...]
        sum_ref[2:3, 0:1] = sq_acc[...]


def router_call(ep_vec, x_loc, idx_loc, scale_row, w_router, cap, local_exp, block):
    rows, width = x_loc.shape
    experts = w_router.shape[1]
    blocks = rows // block

    def late(i, ep):
        return jnp.maximum(i - blocks, 0), 0

    def fixed(i, ep):
        return 0, 0

    return pl.pallas_call(
        functools.partial(router_kernel, blocks, cap, experts, local_exp),
        grid_spec=pltpu.PrefetchScalarGridSpec(
            num_scalar_prefetch=1,
            grid=(2 * blocks,),
            in_specs=[
                pl.BlockSpec((block, width), late),
                pl.BlockSpec((block, 2), lambda i, ep: (jnp.where(i < blocks, i, i - blocks), 0)),
                pl.BlockSpec((1, width), fixed),
                pl.BlockSpec((width, experts), fixed),
            ],
            out_specs=[pl.BlockSpec((block, experts), late), pl.BlockSpec((block, 8), late), pl.BlockSpec((block, 2), late), pl.BlockSpec((5 * experts, cap), fixed), pl.BlockSpec((8, 128), fixed)],
            scratch_shapes=[pltpu.VMEM((1, 2 * experts), jnp.float32), pltpu.VMEM((1, experts), jnp.float32), pltpu.VMEM((1, 1), jnp.float32)],
        ),
        out_shape=[
            jax.ShapeDtypeStruct((rows, experts), jnp.float32),
            jax.ShapeDtypeStruct((rows, 8), jnp.float32),
            jax.ShapeDtypeStruct((rows, 2), jnp.int32),
            jax.ShapeDtypeStruct((5 * experts, cap), jnp.float32),
            jax.ShapeDtypeStruct((8, 128), jnp.float32),
        ],
        compiler_params=pltpu.CompilerParams(dimension_semantics=("arbitrary",)),
        cost_estimate=pl.CostEstimate(flops=10_000_000_000, bytes_accessed=4 * rows * width, transcendentals=0),
        name="router",
    )(ep_vec, x_loc, idx_loc, scale_row, w_router)


def gather_kernel(parts, fills, blk, rows, group, cols, idx_ref, *refs):
    srcs, out_ref, store, stage = refs[:parts], refs[parts], refs[parts + 1], refs[parts + 2]
    step = pl.program_id(0)
    for p in range(parts):

        @pl.when((step >= p * fills) & (step < (p + 1) * fills))
        def _(p=p):
            val = srcs[p][...].astype(jnp.float32)
            base = pl.multiple_of(step * (blk * 8), blk * 8)
            for j in range(cols):
                store[pl.ds(base + j, blk, stride=8), :] = val[:, j * 128:(j + 1) * 128]

    @pl.when(step >= parts * fills)
    def _():
        start = (step - parts * fills) * rows

        def body(q, carry):
            base = q * group
            vals = [store[pl.ds(pl.multiple_of(idx_ref[start + base + r] * 8, 8), 8), :] for r in range(group)]
            for r in range(group):
                stage[pl.ds(pl.multiple_of((base + r) * 8, 8), 8), :] = vals[r]
            return carry

        lax.fori_loop(0, rows // group, body, 0)
        for j in range(cols):
            out_ref[:, j * 128:(j + 1) * 128] = stage[pl.ds(j, rows, stride=8), :].astype(out_ref.dtype)


def gather_rows(srcs, idx, blk, rows, group):
    parts = len(srcs)
    count, width = srcs[0].shape
    fills = count // blk
    total = parts * fills

    def src_map(p, i):
        return jnp.clip(i - p * fills, 0, fills - 1), 0

    return pl.pallas_call(
        functools.partial(gather_kernel, parts, fills, blk, rows, group, width // 128),
        grid=(total + idx.shape[0] // rows,),
        in_specs=[pl.BlockSpec(memory_space=pltpu.SMEM)] + [pl.BlockSpec((blk, width), functools.partial(src_map, p)) for p in range(parts)],
        out_specs=pl.BlockSpec((rows, width), lambda i: (jnp.maximum(i - total, 0), 0)),
        out_shape=jax.ShapeDtypeStruct((idx.shape[0], width), jnp.bfloat16),
        scratch_shapes=[pltpu.VMEM((parts * count * 8, 128), jnp.float32), pltpu.VMEM((rows * 8, 128), jnp.float32)],
        compiler_params=pltpu.CompilerParams(dimension_semantics=("arbitrary",), vmem_limit_bytes=60 * 1024 * 1024),
        cost_estimate=pl.CostEstimate(flops=40_000_000_000, bytes_accessed=4 * width * idx.shape[0], transcendentals=0),
        name="gather_rows",
    )(idx, *srcs)


def combine_kernel(tp_ref, x_ref, dy_ref, o1_ref, o2_ref, col_ref, y_ref, dn_ref):
    col = col_ref[...]
    o1 = jnp.where(col[:, 2:3] > 0.0, o1_ref[...].astype(jnp.float32), 0.0)
    o2 = jnp.where(col[:, 3:4] > 0.0, o2_ref[...].astype(jnp.float32), 0.0)
    y_ref[...] = (x_ref[...].astype(jnp.float32) + col[:, 0:1] * o1 + col[:, 1:2] * o2).astype(y_ref.dtype)
    dy = dy_ref[...].astype(jnp.float32)
    dn_ref[:, 0:1] = jnp.sum(dy * o1, axis=-1, keepdims=True)
    dn_ref[:, 1:2] = jnp.sum(dy * o2, axis=-1, keepdims=True)


def norm_kernel(tp_ref, x_ref, d1_ref, d2_ref, prob_ref, idx_ref, dn_ref, aux_ref, wr_ref, scale_ref, col_ref, dxn_ref, mix_ref, ds_ref, dr_ref):
    col = col_ref[...]
    n_first, n_second = col[:, 0:1], col[:, 1:2]
    dn_first, dn_second = dn_ref[:, 0:1], dn_ref[:, 1:2]
    prob = prob_ref[...]
    aux = aux_ref[...]
    lane = lax.broadcasted_iota(jnp.int32, prob.shape, 1)
    gate_mix = n_first * dn_first + n_second * dn_second
    dl = prob * (aux - jnp.sum(aux * prob, axis=-1, keepdims=True))
    dl = dl + (2.0 * Z_COEF) * col[:, 5:6] * prob
    dl = dl + jnp.where(idx_ref[:, 0:1] == lane, n_first * (dn_first - gate_mix), 0.0)
    dl = dl + jnp.where(idx_ref[:, 1:2] == lane, n_second * (dn_second - gate_mix), 0.0)
    du = jnp.where(col[:, 2:3] > 0.0, d1_ref[...].astype(jnp.float32), 0.0) + jnp.where(col[:, 3:4] > 0.0, d2_ref[...].astype(jnp.float32), 0.0)
    du = du + lax.dot_general(dl, wr_ref[...], (((1,), (1,)), ((), ())), preferred_element_type=jnp.float32)
    xn = x_ref[...].astype(jnp.float32) * col[:, 4:5]
    dxn = du * scale_ref[...]
    dxn_ref[...] = dxn
    mix_ref[...] = jnp.sum(dxn * xn, axis=-1, keepdims=True)
    u_wide = (xn * scale_ref[...]).astype(jnp.bfloat16).astype(jnp.float32)
    ds = jnp.sum(du * xn, axis=0, keepdims=True)
    dr = lax.dot_general(u_wide, dl, (((0,), (0,)), ((), ())), preferred_element_type=jnp.float32)

    @pl.when(pl.program_id(0) == 0)
    def _():
        ds_ref[...] = ds
        dr_ref[...] = dr

    @pl.when(pl.program_id(0) > 0)
    def _():
        ds_ref[...] += ds
        dr_ref[...] += dr


def dx_kernel(tp_ref, x_ref, dy_ref, dxn_ref, col_ref, mix_ref, dx_ref):
    inv = col_ref[:, 4:5]
    xn = x_ref[...].astype(jnp.float32) * inv
    dx_ref[...] = (dy_ref[...].astype(jnp.float32) + inv * (dxn_ref[...] - xn * mix_ref[...])).astype(dx_ref.dtype)


def join_kernel(tp_ref, own_ref, other_ref, out_ref):
    half = own_ref.shape[1]
    own, other = own_ref[...], other_ref[...]
    first = tp_ref[0] == 0
    out_ref[:, :half] = jnp.where(first, own, other)
    out_ref[:, half:] = jnp.where(first, other, own)


def rows_call(kernel, tp_vec, ins, outs, rows, block):
    specs, args = [], []
    for kind, arr in ins:
        if kind == 'half':
            specs.append(pl.BlockSpec((block, arr.shape[1] // 2), lambda i, tp: (i, tp[0])))
        elif kind == 'row':
            specs.append(pl.BlockSpec((block, arr.shape[1]), lambda i, tp: (i, 0)))
        elif kind == 'same':
            specs.append(pl.BlockSpec(arr.shape, lambda i, tp: (0, 0)))
        elif kind == 'lanes':
            specs.append(pl.BlockSpec((1, arr.shape[1] // 2), lambda i, tp: (0, tp[0])))
        else:
            specs.append(pl.BlockSpec((arr.shape[0] // 2, arr.shape[1]), lambda i, tp: (tp[0], 0)))
        args.append(arr)
    out_specs = [pl.BlockSpec((block if o.shape[0] == rows else o.shape[0], o.shape[1]), (lambda i, tp: (i, 0)) if o.shape[0] == rows else (lambda i, tp: (0, 0))) for o in outs]
    return pl.pallas_call(
        kernel,
        grid_spec=pltpu.PrefetchScalarGridSpec(num_scalar_prefetch=1, grid=(rows // block,), in_specs=specs, out_specs=out_specs),
        out_shape=outs,
        compiler_params=pltpu.CompilerParams(dimension_semantics=("arbitrary",)),
        cost_estimate=pl.CostEstimate(flops=10_000_000_000, bytes_accessed=sum(a.size * 2 for _, a in ins), transcendentals=0),
    )(tp_vec, *args)


def ffn_call(k, base, count, chunks, tp_id, x_rows, dy_rows, gate, scale, wg, wl, wo, bufs, tile):
    experts, rows, width = x_rows.shape
    ff = wg.shape[2]
    steps = ff // tile
    half = width // 2
    row_spec = pl.BlockSpec((1, rows, width), lambda e, f: (base + e, 0, 0))
    in_specs = [
        pl.BlockSpec(memory_space=pltpu.SMEM),
        row_spec,
        row_spec,
        pl.BlockSpec((1, rows, 1), lambda e, f: (base + e, 0, 0)),
        pl.BlockSpec((1, width), lambda e, f: (0, 0)),
        pl.BlockSpec((1, width, tile), lambda e, f: (base + e, 0, f)),
        pl.BlockSpec((1, width, tile), lambda e, f: (base + e, 0, f)),
        pl.BlockSpec((1, tile, width), lambda e, f: (base + e, f, 0)),
    ]
    wide_spec = pl.BlockSpec((1, 1, rows, width), lambda e, f: (k, base + e, 0, 0))
    tile_spec = pl.BlockSpec((1, 1, rows, tile), lambda e, f: (k, base + e, 0, f))
    half_spec = pl.BlockSpec((1, rows, half), lambda e, f: (e, 0, 0))
    wide = jax.ShapeDtypeStruct((chunks, experts, rows, width), jnp.bfloat16)
    deep = jax.ShapeDtypeStruct((chunks, experts, rows, ff), jnp.bfloat16)
    part = jax.ShapeDtypeStruct((count, rows, half), jnp.bfloat16)
    aliases = {}
    if bufs is None:
        bufs = ()
    else:
        aliases = {len(in_specs) + i: i for i in range(5)}
    in_specs = in_specs + [pl.BlockSpec(memory_space=pl.ANY)] * len(bufs)
    flops = 12 * count * rows * width * ff
    outs = pl.pallas_call(
        ffn_kernel,
        grid=(count, steps),
        in_specs=in_specs,
        out_specs=[wide_spec, wide_spec, tile_spec, tile_spec, tile_spec, half_spec, half_spec, half_spec, half_spec],
        out_shape=[wide, wide, deep, deep, deep, part, part, part, part],
        scratch_shapes=[
            pltpu.VMEM((rows, width), jnp.bfloat16),
            pltpu.VMEM((rows, width), jnp.bfloat16),
            pltpu.VMEM((rows, width), jnp.float32),
            pltpu.VMEM((rows, width), jnp.float32),
        ],
        input_output_aliases=aliases,
        compiler_params=pltpu.CompilerParams(dimension_semantics=("arbitrary", "arbitrary"), vmem_limit_bytes=48 * 1024 * 1024),
        cost_estimate=pl.CostEstimate(flops=flops, bytes_accessed=8 * count * rows * (width + ff), transcendentals=count * rows * ff),
        name="ffn",
    )(tp_id, x_rows, dy_rows, gate, scale, wg, wl, wo, *bufs)
    return tuple(outs[:5]), outs[5:]


def solution(mesh):
    ep_size = mesh.shape['ep']

    def swap(arr, k):
        return lax.ppermute(arr, 'ep', [(i, i ^ k) for i in range(ep_size)])

    def swap_tp(arr):
        return lax.ppermute(arr, 'tp', [(0, 1), (1, 0)])

    def device_body(x_loc, dy_loc, idx_loc, norm_scale, w_router, gate_loc, lin_loc, out_loc):
        tok_count, width = x_loc.shape
        experts = w_router.shape[1]
        local_exp = gate_loc.shape[0]
        half = width // 2
        tokens = tok_count * ep_size
        cap = (5 * tok_count + 2 * experts - 1) // (2 * experts)
        ep_id = lax.axis_index('ep')
        tp_id = lax.axis_index('tp')
        tp_vec = tp_id.reshape(1).astype(jnp.int32)
        part_rows = tok_count // 2
        x_near = swap(lax.dynamic_slice_in_dim(x_loc, tp_id * part_rows, part_rows, 0), 2)
        dy_far = swap(dy_loc, 2)
        x_side = swap_tp(x_near)
        x_rows = [[x_loc], [swap(x_loc, 1)], [x_near, x_side], [swap(x_near, 1), swap(x_side, 1)]]
        dy_rows = [[dy_loc], [swap(dy_loc, 1)], [dy_far], [swap(dy_far, 1)]]
        scale_row = norm_scale.reshape(1, width)
        prob, cols, rows, tab, sums_own = router_call(ep_id.reshape(1).astype(jnp.int32), x_loc, idx_loc, scale_row, w_router, cap, local_exp, 512)
        tab = tab.reshape(5, experts, cap)
        slot_one = tab[0] * 128.0 + tab[1]
        slot_gate = jnp.where(slot_one > 0.0, (tab[2] + tab[3]) + tab[4], -1.0)
        pair = jnp.stack([slot_one, slot_gate], axis=1).reshape(ep_size, local_exp, 2, cap)
        sums_far = [swap(sums_own, k) for k in range(1, ep_size)]
        bufs = None
        tables = [lax.dynamic_index_in_dim(pair, ep_id ^ k, 0, keepdims=False) for k in range(ep_size)]
        tables = [swap(tables[k], k) if k else tables[k] for k in range(ep_size)]

        def take(srcs, idx):
            blk = min(1024, srcs[0].shape[0])
            return gather_rows(srcs, idx, blk, 2 * cap, 16).reshape(local_exp, cap, width)

        def fold(keep, send):
            return (keep.astype(jnp.float32) + send.astype(jnp.float32)).astype(jnp.bfloat16)

        sent = []
        for k in range(ep_size):
            mine = tables[k]
            if k:
                last = sent[k - 1][-1]
                mine, held = lax.optimization_barrier((mine, last[0]))
                sent[k - 1][-1] = (held,) + last[1:]
            tok = jnp.maximum(mine[:, 0].astype(jnp.int32) - 1, 0).reshape(-1)
            tok_x = tok if k < 2 else ((tok // part_rows) ^ tp_id) * part_rows + tok % part_rows
            gate_k = mine[:, 1].reshape(local_exp, cap, 1)
            xr = take(x_rows[k], tok_x)
            dr = take(dy_rows[k], tok)
            units = 2 if k == 0 else 1
            count = local_exp // units
            got = []
            for unit in range(units):
                bufs, parts = ffn_call(k, unit * count, count, ep_size, tp_vec, xr, dr, gate_k, scale_row, gate_loc, lin_loc, out_loc, bufs, 512)
                got.append((parts[0], swap_tp(parts[1]), parts[2], swap_tp(parts[3])))
            sent.append(got)
        u_slot, do_slot, h_slot, da_slot, db_slot = bufs
        d_gate = jnp.einsum('sxcd,sxcf->xdf', u_slot, da_slot, preferred_element_type=jnp.float32)
        d_lin = jnp.einsum('sxcd,sxcf->xdf', u_slot, db_slot, preferred_element_type=jnp.float32)
        d_out = jnp.einsum('sxcf,sxcd->xfd', h_slot, do_slot, preferred_element_type=jnp.float32)

        def after(held, *arrs):
            out = lax.optimization_barrier((*arrs, held))
            return out[:-1]

        tail = sent[-1][0][0]
        for k in range(ep_size - 1):
            for unit, (keep_o, got_o, keep_d, got_d) in enumerate(sent[k]):
                if k == ep_size - 2:
                    got_o, *sums_far = after(tail, got_o, *sums_far)
                    got_d, d_gate = lax.optimization_barrier((got_d, d_gate))
                else:
                    got_o, got_d = after(tail, got_o, got_d)
                sent[k][unit] = (keep_o, got_o, keep_d, got_d)
        keep_o, got_o, keep_d, got_d = sent[-1][0]
        got_o, d_lin = lax.optimization_barrier((got_o, d_lin))
        got_d, d_out = lax.optimization_barrier((got_d, d_out))
        sent[-1] = [(keep_o, got_o, keep_d, got_d)]
        o_back, du_back = [], []
        for k in range(ep_size):
            for keep_o, got_o, keep_d, got_d in sent[k]:
                o_sum = fold(keep_o, got_o)
                o_back.append(swap(o_sum, k) if k else o_sum)
                du_sum = fold(keep_d, got_d)
                du_back.append(swap(du_sum, k) if k else du_sum)

        row_first, row_second = rows[:, 0], rows[:, 1]

        def pick(src, rows):
            return src.at[rows].get(mode='promise_in_bounds')

        half_rows = jax.ShapeDtypeStruct((tok_count, half), jnp.bfloat16)
        o_all = jnp.concatenate(o_back, axis=0).reshape(experts * cap, half)
        y_half, dn_part = rows_call(
            combine_kernel, tp_vec,
            [('half', x_loc), ('half', dy_loc), ('row', pick(o_all, row_first)), ('row', pick(o_all, row_second)), ('row', cols)],
            [half_rows, jax.ShapeDtypeStruct((tok_count, 2), jnp.float32)], tok_count, 1024)
        dn_part = dn_part.T
        dn_other = swap_tp(dn_part)
        dn = (dn_part + dn_other).T

        def join(own, other):
            whole = jax.ShapeDtypeStruct((tok_count, width), jnp.bfloat16)
            return rows_call(join_kernel, tp_vec, [('row', own), ('row', other)], [whole], tok_count, 1024)[0]

        y_other = swap_tp(y_half)
        y_loc = join(y_half, y_other)
        stats = ((sums_own + sums_far[0]) + sums_far[1]) + sums_far[2]
        frac_first = stats[0, :experts] / tokens
        z_loss = Z_COEF * stats[2, 0] / tokens
        aux_loss = AUX_COEF * experts * jnp.sum(frac_first * stats[1, :experts]) / tokens
        aux_row = (AUX_COEF * experts * frac_first).reshape(1, experts)
        du_all = jnp.concatenate(du_back, axis=0).reshape(experts * cap, half)
        du_first = pick(du_all, row_first)
        du_second = pick(du_all, row_second)
        dxn, mix, d_scale_half, d_router_half = rows_call(
          norm_kernel, tp_vec,
          [('half', x_loc), ('row', du_first), ('row', du_second), ('row', prob), ('row', idx_loc), ('row', dn), ('same', aux_row), ('deep', w_router), ('lanes', scale_row), ('row', cols)],
          [jax.ShapeDtypeStruct((tok_count, half), jnp.float32), jax.ShapeDtypeStruct((tok_count, 1), jnp.float32), jax.ShapeDtypeStruct((1, half), jnp.float32), jax.ShapeDtypeStruct((half, experts), jnp.float32)], tok_count, 1024)
        mix = mix.reshape(tok_count)
        mix = ((mix + swap_tp(mix)) / width).reshape(tok_count, 1)
        dx_half = rows_call(dx_kernel, tp_vec, [('half', x_loc), ('half', dy_loc), ('row', dxn), ('row', cols), ('row', mix)], [half_rows], tok_count, 1024)[0]
        dx_loc = join(dx_half, swap_tp(dx_half))
        d_scale_half = d_scale_half.reshape(half)
        both = jnp.concatenate([d_router_half.reshape(-1), d_scale_half])
        both = lax.dynamic_update_slice_in_dim(jnp.zeros((2, both.shape[0]), jnp.float32), both[None], tp_id, 0)
        both = lax.psum(both, ('tp', 'ep'))
        d_router = both[:, :half * experts].reshape(width, experts)
        d_scale = both[:, half * experts:].reshape(width)
        losses = jnp.stack([z_loss, aux_loss])
        return (y_loc, losses, dx_loc, d_scale, d_router, d_gate, d_lin, d_out)

    tok_spec = P('ep', None)
    in_spec = P('ep', None, 'tp')
    out_spec = P('ep', 'tp', None)
    return jax.shard_map(device_body, mesh=mesh, in_specs=(tok_spec, tok_spec, tok_spec, P(), P(), in_spec, in_spec, out_spec), out_specs=(tok_spec, P(), tok_spec, P(), P(), in_spec, in_spec, out_spec), check_vma=False)
```

time: 4120 us -> 2120 us (0.51)
  waiting for transfers between devices: 1910 us -> 869 us
  Pallas kernels: 0 us -> 721 us
  local copies, waits for them, and re-layouts: 940 us -> 229 us
  matrix products: 703 us -> 186 us
  blocking collectives: 356 us -> 0 us
  other arithmetic: 139 us -> 61 us
    psum x2 -> x1, waiting for transfers between devices: 1360 us -> 40.1 us  [device_body(): both = lax.psum(both, ('tp', 'ep'))]
    ppermute x0 -> x34, waiting for transfers between devices: none -> 829 us  [the longest x15 607 us: swap_tp(): return lax.ppermute(arr, 'tp', [(0, 1), (1, 0)])]
    pallas_call x0 -> x19, Pallas kernels: none -> 721 us  [the longest x5 400 us: ffn_call(): pl.pallas_call(ffn_kernel, grid=(count, steps), in_specs=in_specs, out_sp...]
    gather x6 -> x4, local copies, waits for them, and re-layouts: 770 us -> 160 us  [pick(): return src.at[rows].get(mode='promise_in_bounds')]
    all_to_all x4 -> x0, waiting for transfers between devices: 547 us -> none  [the longest x1 337 us: device_block(): lax.all_to_all(exp_out.reshape(experts, slot_cap, model_width), 'ep', 0,...]
    dot_general x12 -> x3, matrix products: 703 us -> 186 us  [the longest x1 62.5 us: device_body(): jnp.einsum('sxcd,sxcf->xdf', u_slot, da_slot, preferred_element_type=jnp....]
    psum x2 -> x0, blocking collectives: 356 us -> none  [the longest x1 341 us: device_block(): first_count = lax.psum(jnp.sum(one_first, axis=0), 'ep')]
    scatter x4 -> x0, local copies, waits for them, and re-layouts: 123 us -> none  [the longest x2 61.5 us: slot_tables(): slot_tok = slot_tok.at[slot_first].set(tok_ids).at[slot_second].set(tok_ids)]
  transfers between devices with their start and end apart: 6 -> 35, of which waited for: 3 -> 13; matrix products, arithmetic and copies ran while one was open for 20% -> 22% of each run, Pallas kernels for 0% -> 32%
where the time goes in v1:
time: 2120 us; the launch traced here: 2110 us
  waiting for transfers between devices  869 us (41%)
  Pallas kernels  721 us (34%)
  local copies, waits for them, and re-layouts  229 us (11%)
  matrix products  186 us (9%)
  other arithmetic  61 us (3%)
  starting transfers between devices  27.3 us (1%)
    ppermute x15, waiting for transfers between devices, swap_tp(): return lax.ppermute(arr, 'tp', [(0, 1), (1, 0)])  607 us
    pallas_call x5, Pallas kernels, ffn_call(): pl.pallas_call(ffn_kernel, grid=(count, steps), in_specs=in_specs, out_sp...  400 us
    ppermute x19, waiting for transfers between devices, swap(): return lax.ppermute(arr, 'ep', [(i, i ^ k) for i in range(ep_size)])  222 us
    pallas_call x8, Pallas kernels, gather_rows(): pl.pallas_call(functools.partial(gather_kernel, parts, fills, blk, rows,...  189 us
    gather x4, local copies, waits for them, and re-layouts, pick(): return src.at[rows].get(mode='promise_in_bounds')  160 us
    pallas_call x5, Pallas kernels, rows_call(): pl.pallas_call(kernel, grid_spec=pltpu.PrefetchScalarGridSpec(num_scalar_...  81.4 us
    dot_general x1, matrix products, device_body(): jnp.einsum('sxcd,sxcf->xdf', u_slot, da_slot, preferred_element_type=jnp....  62.5 us
    dot_general x1, matrix products, device_body(): jnp.einsum('sxcf,sxcd->xfd', h_slot, do_slot, preferred_element_type=jnp....  61.8 us
  transfers between devices with their start and end apart: 35, of which 13 were waited for; matrix products, arithmetic and copies ran while one was open for 22% of the time, Pallas kernels for 32%

profile of v1, /device:TPU:0, one launch (start us, length us, event | category | flops | bytes accessed | tf_op | source)
XLA Modules:
  0.0 2108.9 jit_solution(1314542636623075059)
XLA Ops:
  8.1 2.5 collective-permute-start.9
  10.8 3.5 copy.117.idx_ref
  17.4 50.2 %router.1 = (f32[8192,32]{1,0:T(8,128)}, f32[8192,8]{1,0:T(8,128)}, s32[8192,2]{1,0:T(8,128)}, f32[160,640]{1,0:T(8,128)}, f32[8,128]{1,0:T(8,128)}) custom-call(s32[1]{0:T(128)} %bitcast.1.ep_ref, bf16[8192,768]{1,0:T(8,128)(2,1)} %x_ref.7, s32[8192,2]{1,0:T(8,128)} %copy.117.idx_ref, f32[1,768]{1,0:T(1,128)} %reshape.197.scale_ref, f32[768,32]{1,0:T(8,128)} %copy.118.wr_ref), custom_call_target="tpu_custom_call" | custom-call | flops 10000000000 | bytes 25165824 | tf_op jit(solution)/shard_map/router/pallas_call | solution.py:163
  69.7 5.9 constant_dynamic-slice_fusion
  76.2 23.5 %gather_rows.8 = bf16[5120,768]{1,0:T(8,128)(2,1)} custom-call(s32[5120]{0:T(1024)} %max.29.idx_ref, bf16[8192,768]{1,0:T(8,128)(2,1)} %x_ref.7), custom_call_target="tpu_custom_call" | custom-call | flops 40000000000 | bytes 15728640 | tf_op jit(solution)/shard_map/gather_rows/pallas_call | solution.py:227
  99.7 23.5 %gather_rows.9 = bf16[5120,768]{1,0:T(8,128)(2,1)} custom-call(s32[5120]{0:T(1024)} %max.29.idx_ref, bf16[8192,768]{1,0:T(8,128)(2,1)} %dy_ref.3), custom_call_target="tpu_custom_call" | custom-call | flops 40000000000 | bytes 15728640 | tf_op jit(solution)/shard_map/gather_rows/pallas_call | solution.py:227
  123.2 2.2 copy.119.gate_ref
  125.5 51.2 %ffn.5 = (bf16[4,8,640,768]{3,2,1,0:T(8,128)(2,1)}, bf16[4,8,640,768]{3,2,1,0:T(8,128)(2,1)}, bf16[4,8,640,1536]{3,2,1,0:T(8,128)(2,1)}, bf16[4,8,640,1536]{3,2,...) custom-call(s32[1]{0:T(128)} %bitcast.tp_ref, ...), custom_call_target="tpu_custom_call" | custom-call | flops 36238786560 | bytes 47185920 | tf_op jit(solution)/shard_map/ffn/pallas_call | solution.py:350
  180.6 51.8 %ffn.6 = (bf16[4,8,640,768]{3,2,1,0:T(8,128)(2,1)}, bf16[4,8,640,768]{3,2,1,0:T(8,128)(2,1)}, bf16[4,8,640,1536]{3,2,1,0:T(8,128)(2,1)}, bf16[4,8,640,1536]{3,2,...) custom-call(s32[1]{0:T(128)} %bitcast.tp_ref, ...), custom_call_target="tpu_custom_call", output_to_operand_aliasing={{0}: (8, {}), {1}: (9, {}), {2}: (10, {}), {3}: (11, {}), {... | custom-call | flops 36238786560 | bytes 47185920 | tf_op jit(solution)/shard_map/ffn/pallas_call | solution.py:350
  236.3 3.3 fusion.1
  245.1 23.5 %gather_rows.10 = bf16[5120,768]{1,0:T(8,128)(2,1)} custom-call(s32[5120]{0:T(1024)} %max.31.idx_ref, bf16[8192,768]{1,0:T(8,128)(2,1)} %collective-permute-done.5.refs_0_), custom_call_target="tpu_custom_call" | custom-call | flops 40000000000 | bytes 15728640 | tf_op jit(solution)/shard_map/gather_rows/pallas_call | solution.py:227
  268.6 148.3 %collective-permute-done.7.refs_0_ = bf16[4096,768]{1,0:T(8,128)(2,1)} collective-permute-done((bf16[4096,768]{1,0:T(8,128)(2,1)}, bf16[4096,768]{1,0:T(8,128)(2,1)}, u32[]{:S(2)}, u32[]{:S(2)}) %collective-permute-start.7) | collective-permute-done | bytes 6291488 | tf_op jit(solution)/shard_map/ppermute | solution.py:374
  416.9 2.0 collective-permute-start.8
  419.0 23.5 %gather_rows.11 = bf16[5120,768]{1,0:T(8,128)(2,1)} custom-call(s32[5120]{0:T(1024)} %max.31.idx_ref, bf16[8192,768]{1,0:T(8,128)(2,1)} %collective-permute-done.6.refs_0_), custom_call_target="tpu_custom_call" | custom-call | flops 40000000000 | bytes 15728640 | tf_op jit(solution)/shard_map/gather_rows/pallas_call | solution.py:227
  442.5 99.2 %ffn.7 = (bf16[4,8,640,768]{3,2,1,0:T(8,128)(2,1)}, bf16[4,8,640,768]{3,2,1,0:T(8,128)(2,1)}, bf16[4,8,640,1536]{3,2,1,0:T(8,128)(2,1)}, bf16[4,8,640,1536]{3,2,...) custom-call(s32[1]{0:T(128)} %bitcast.tp_ref, ...), custom_call_target="tpu_custom_call", output_to_operand_aliasing={{0}: (8, {}), {1}: (9, {}), {2}: (10, {}), {3}: (11, {}), {... | custom-call | flops 72477573120 | bytes 94371840 | tf_op jit(solution)/shard_map/ffn/pallas_call | solution.py:350
  545.1 23.5 %gather_rows.13 = bf16[5120,768]{1,0:T(8,128)(2,1)} custom-call(s32[5120]{0:T(1024)} %copy-done.30, bf16[8192,768]{1,0:T(8,128)(2,1)} %collective-permute-done.9.refs_0_), custom_call_target="tpu_custom_call" | custom-call | flops 40000000000 | bytes 15728640 | tf_op jit(solution)/shard_map/gather_rows/pallas_call | solution.py:227
  568.9 23.9 %gather_rows.12 = bf16[5120,768]{1,0:T(8,128)(2,1)} custom-call(s32[5120]{0:T(1024)} %fusion.16.idx_ref, bf16[4096,768]{1,0:T(8,128)(2,1)} %collective-permute-done.7.refs_0_, bf16[4096,768]{1,0:T(8,128)(2,1)} %collective-permute-done.8.refs_1_), custom_call_target="tpu_custom_call" | custom-call | flops 40000000000 | bytes 15728640 | tf_op jit(solution)/shard_map/gather_rows/pallas_call | solution.py:227
  592.8 99.0 %ffn.8 = (bf16[4,8,640,768]{3,2,1,0:T(8,128)(2,1)}, bf16[4,8,640,768]{3,2,1,0:T(8,128)(2,1)}, bf16[4,8,640,1536]{3,2,1,0:T(8,128)(2,1)}, bf16[4,8,640,1536]{3,2,...) custom-call(s32[1]{0:T(128)} %bitcast.tp_ref, ...), custom_call_target="tpu_custom_call", output_to_operand_aliasing={{0}: (8, {}), {1}: (9, {}), {2}: (10, {}), {3}: (11, {}), {... | custom-call | flops 72477573120 | bytes 94371840 | tf_op jit(solution)/shard_map/ffn/pallas_call | solution.py:350
  696.7 23.9 %gather_rows.14 = bf16[5120,768]{1,0:T(8,128)(2,1)} custom-call(s32[5120]{0:T(1024)} %fusion.19.idx_ref, bf16[4096,768]{1,0:T(8,128)(2,1)} %collective-permute-done.10.refs_0_, bf16[4096,768]{1,0:T(8,128)(2,1)} %collective-permute-done.11.refs_1_), custom_call_target="tpu_custom_call" | custom-call | flops 40000000000 | bytes 15728640 | tf_op jit(solution)/shard_map/gather_rows/pallas_call | solution.py:227
  722.3 23.5 %gather_rows.15 = bf16[5120,768]{1,0:T(8,128)(2,1)} custom-call(s32[5120]{0:T(1024)} %copy-done.29, bf16[8192,768]{1,0:T(8,128)(2,1)} %collective-permute-done.12.refs_0_), custom_call_target="tpu_custom_call" | custom-call | flops 40000000000 | bytes 15728640 | tf_op jit(solution)/shard_map/gather_rows/pallas_call | solution.py:227
  745.8 99.0 %ffn.9 = (bf16[4,8,640,768]{3,2,1,0:T(8,128)(2,1)}, bf16[4,8,640,768]{3,2,1,0:T(8,128)(2,1)}, bf16[4,8,640,1536]{3,2,1,0:T(8,128)(2,1)}, bf16[4,8,640,1536]{3,2,...) custom-call(s32[1]{0:T(128)} %bitcast.tp_ref, ...), custom_call_target="tpu_custom_call", output_to_operand_aliasing={{0}: (8, {}), {1}: (9, {}), {2}: (10, {}), {3}: (11, {}), {... | custom-call | flops 72477573120 | bytes 94371840 | tf_op jit(solution)/shard_map/ffn/pallas_call | solution.py:350
  844.9 61.7 %convolution_bitcast_fusion.1 = f32[8,768,1536]{2,1,0:T(8,128)} fusion(bf16[4,8,640,768]{3,2,1,0:T(8,128)(2,1)} %get-tuple-element.131, bf16[4,8,640,1536]{3,2,1,0:T(8,128)(2,1)} %get-tuple-element.132), kind=kOutput, calls=%fused_computation.5 | convolution fusion | flops 48318382080 | bytes 132120576 | tf_op jit(solution)/shard_map/sxcd,sxcf->xdf/dot_general | solution.py:434
  910.6 62.5 %convolution_bitcast_fusion = f32[8,768,1536]{2,1,0:T(8,128)} fusion(bf16[4,8,640,768]{3,2,1,0:T(8,128)(2,1)} %get-tuple-element.131, bf16[4,8,640,1536]{3,2,1,0:T(8,128)(2,1)} %get-tuple-element.148), kind=kOutput, calls=%fused_computation.4 | convolution fusion | flops 48318382080 | bytes 132120576 | tf_op jit(solution)/shard_map/sxcd,sxcf->xdf/dot_general | solution.py:433
  973.5 21.1 %collective-permute-done.18 = bf16[8,640,384]{2,1,0:T(8,128)(2,1)} collective-permute-done((bf16[8,640,384]{2,1,0:T(8,128)(2,1)}, bf16[8,640,384]{2,1,0:T(8,128)(2,1)}, u32[]{:S(2)}, u32[]{:S(2)}) %collective-permute-start.18) | collective-permute-done | bytes 3932192 | tf_op jit(solution)/shard_map/ppermute | solution.py:377
  995.0 83.9 %collective-permute-done.27 = bf16[8,640,384]{2,1,0:T(8,128)(2,1)} collective-permute-done((bf16[8,640,384]{2,1,0:T(8,128)(2,1)}, bf16[8,640,384]{2,1,0:T(8,128)(2,1)}, u32[]{:S(2)}, u32[]{:S(2)}) %collective-permute-start.27) | collective-permute-done | bytes 3932192 | tf_op jit(solution)/shard_map/ppermute | solution.py:377
  1079.3 6.2 add_convert_fusion.5
  1085.5 77.7 %collective-permute-done.23 = bf16[8,640,384]{2,1,0:T(8,128)(2,1)} collective-permute-done((bf16[8,640,384]{2,1,0:T(8,128)(2,1)}, bf16[8,640,384]{2,1,0:T(8,128)(2,1)}, u32[]{:S(2)}, u32[]{:S(2)}) %collective-permute-start.23) | collective-permute-done | bytes 3932192 | tf_op jit(solution)/shard_map/ppermute | solution.py:377
  1163.6 5.0 add_convert_fusion.4
  1168.6 5.3 add_convert_fusion.2
  1173.9 5.2 add_convert_fusion.1
  1179.1 5.0 add_convert_fusion.3
  1184.1 105.4 %collective-permute-done = bf16[4,640,384]{2,1,0:T(8,128)(2,1)S(1)} collective-permute-done((bf16[4,640,384]{2,1,0:T(8,128)(2,1)}, bf16[4,640,384]{2,1,0:T(8,128)(2,1)S(1)}, u32[]{:S(2)}, u32[]{:S(2)}) %collective-permute-start) | collective-permute-done | bytes 1966112 | tf_op jit(solution)/shard_map/ppermute | solution.py:377
  1289.5 42.1 %collective-permute-done.1 = bf16[4,640,384]{2,1,0:T(8,128)(2,1)S(1)} collective-permute-done((bf16[4,640,384]{2,1,0:T(8,128)(2,1)}, bf16[4,640,384]{2,1,0:T(8,128)(2,1)S(1)}, u32[]{:S(2)}, u32[]{:S(2)}) %collective-permute-start.1) | collective-permute-done | bytes 1966112 | tf_op jit(solution)/shard_map/ppermute | solution.py:377
  1333.1 40.6 %collective-permute-done.13 = bf16[4,640,384]{2,1,0:T(8,128)(2,1)S(1)} collective-permute-done((bf16[4,640,384]{2,1,0:T(8,128)(2,1)S(1)}, bf16[4,640,384]{2,1,0:T(8,128)(2,1)S(1)}, u32[]{:S(2)}, u32[]{:S(2)}) %collective-permute-start.13) | collective-permute-done | bytes 1966112 | tf_op jit(solution)/shard_map/ppermute | solution.py:377
  1373.8 41.1 %collective-permute-done.14 = bf16[4,640,384]{2,1,0:T(8,128)(2,1)S(1)} collective-permute-done((bf16[4,640,384]{2,1,0:T(8,128)(2,1)S(1)}, bf16[4,640,384]{2,1,0:T(8,128)(2,1)S(1)}, u32[]{:S(2)}, u32[]{:S(2)}) %collective-permute-start.14) | collective-permute-done | bytes 1966112 | tf_op jit(solution)/shard_map/ppermute | solution.py:377
  1416.5 61.8 %convolution_bitcast_fusion.2 = f32[8,1536,768]{2,1,0:T(8,128)} fusion(bf16[4,8,640,1536]{3,2,1,0:T(8,128)(2,1)} %get-tuple-element.152, bf16[4,8,640,768]{3,2,1,0:T(8,128)(2,1)} %get-tuple-element.153), kind=kOutput, calls=%fused_computation.6 | convolution fusion | flops 48318382080 | bytes 132120576 | tf_op jit(solution)/shard_map/sxcf,sxcd->xfd/dot_general | solution.py:435
  1478.3 6.3 add_convert_fusion
  1491.6 1.8 fusion.3
  1495.3 4.4 constant_dynamic-update-slice_fusion.2
  1499.7 4.5 constant_dynamic-update-slice_fusion.1
  1504.2 4.5 constant_dynamic-update-slice_fusion.5
  1508.7 4.4 constant_dynamic-update-slice_fusion.4
  1513.1 73.2 %collective-permute-done.24 = bf16[8,640,384]{2,1,0:T(8,128)(2,1)} collective-permute-done((bf16[8,640,384]{2,1,0:T(8,128)(2,1)}, bf16[8,640,384]{2,1,0:T(8,128)(2,1)}, u32[]{:S(2)}, u32[]{:S(2)}) %collective-permute-start.24) | collective-permute-done | bytes 3932192 | tf_op jit(solution)/shard_map/ppermute | solution.py:374
  1586.3 4.5 constant_dynamic-update-slice_fusion
  1590.8 40.1 %gather_fusion = bf16[8192,384]{1,0:T(8,128)(2,1)} fusion(bf16[20480,384]{1,0:T(8,128)(2,1)} %bitcast.21, s32[8192]{0:T(1024)S(1)} %copy-done.27), kind=kCustom, calls=%fused_computation | custom fusion | bytes 12615680 | tf_op jit(solution)/shard_map/gather | solution.py:465
  1630.9 40.1 %gather_fusion.1 = bf16[8192,384]{1,0:T(8,128)(2,1)} fusion(bf16[20480,384]{1,0:T(8,128)(2,1)} %bitcast.21, s32[8192]{0:T(1024)S(1)} %copy-done.26), kind=kCustom, calls=%fused_computation.1 | custom fusion | bytes 12615680 | tf_op jit(solution)/shard_map/gather | solution.py:465
  1670.9 16.6 shard_map.143
  1687.5 3.1 copy.127
  1691.1 4.4 constant_dynamic-update-slice_fusion.3
  1695.5 40.1 %gather_fusion.2 = bf16[8192,384]{1,0:T(8,128)(2,1)} fusion(bf16[20480,384]{1,0:T(8,128)(2,1)} %bitcast.26, s32[8192]{0:T(1024)S(1)} %copy-done.27), kind=kCustom, calls=%fused_computation.2 | custom fusion | bytes 12615680 | tf_op jit(solution)/shard_map/gather | solution.py:465
  1735.6 40.0 %gather_fusion.3 = bf16[8192,384]{1,0:T(8,128)(2,1)} fusion(bf16[20480,384]{1,0:T(8,128)(2,1)} %bitcast.26, s32[8192]{0:T(1024)S(1)} %copy-done.26), kind=kCustom, calls=%fused_computation.3 | custom fusion | bytes 12615680 | tf_op jit(solution)/shard_map/gather | solution.py:465
  1775.5 2.7 copy.128
  1778.2 5.9 add_bitcast_fusion.dn_ref
  1784.1 26.7 %shard_map.145 = (f32[8192,384]{1,0:T(8,128)}, f32[8192,1]{1,0:T(8,128)}, f32[1,384]{1,0:T(1,128)}, f32[384,32]{1,0:T(8,128)}) custom-call(s32[1]{0:T(128)} %bitcast.tp_ref, bf16[8192,768]{1,0:T(8,128)(2,1)} %x_ref.7, bf16[8192,384]{1,0:T(8,128)(2,1)} %gather_fusion.2, bf16[8192,384]{1,0:T(8,128)(2,1)} %gather_fusion.3, ...), custom_call_target="tpu_custom_call" | custom-call | flops 10000000000 | bytes 25937472 | tf_op jit(solution)/shard_map/pallas_call | solution.py:312
  1810.8 3.3 reduce.3
  1816.2 1.9 collective-permute-done.32
  1818.1 2.7 copy.131.mix_ref
  1820.8 15.2 shard_map.146.own_ref
  1836.0 1.9 collective-permute-start.33
  1842.0 40.1 %all-reduce.2.cloned.1.call-done = f32[2,12672]{1,0:T(2,128)} async-done(((f32[2,12672]{1,0:T(2,128)}), f32[2,12672]{1,0:T(2,128)}) %all-reduce.2.cloned.1.call-update) | async-done | bytes 101392 | tf_op jit(solution)/shard_map/psum | solution.py:502
  1885.3 70.4 %collective-permute-done.25.other_ref = bf16[8192,384]{1,0:T(8,128)(2,1)} collective-permute-done((bf16[8192,384]{1,0:T(8,128)(2,1)}, bf16[8192,384]{1,0:T(8,128)(2,1)}, u32[]{:S(2)}, u32[]{:S(2)}) %collective-permute-start.25) | collective-permute-done | bytes 6291488 | tf_op jit(solution)/shard_map/ppermute | solution.py:377
  1955.7 11.5 shard_map.144
  1967.2 122.9 %collective-permute-done.33.other_ref = bf16[8192,384]{1,0:T(8,128)(2,1)} collective-permute-done((bf16[8192,384]{1,0:T(8,128)(2,1)}, bf16[8192,384]{1,0:T(8,128)(2,1)}, u32[]{:S(2)}, u32[]{:S(2)}) %collective-permute-start.33) | collective-permute-done | bytes 6291488 | tf_op jit(solution)/shard_map/ppermute | solution.py:377
  2090.1 11.5 shard_map.147
  (162 shorter events, 56.6 us)
Async XLA Ops:
  7.2 1875.0 %all-reduce.2.cloned.1.call-start = ((), (), s32[]{:S(2)}) async-start(), calls=%async_computation | async-start | bytes 202752 | tf_op jit(solution)/shard_map/psum | solution.py:502
  7.2 409.7 %collective-permute-start.6 = (bf16[8192,768]{1,0:T(8,128)(2,1)}, bf16[8192,768]{1,0:T(8,128)(2,1)}, u32[]{:S(2)}, u32[]{:S(2)}) collective-permute-start(bf16[8192,768]{1,0:T(8,128)(2,1)} %dy_ref.3), channel_id=1, source_target_pairs={{0,1},{1,0},{2,3},{3,2},{4,5},{5,4},{6,7},{7,6}} | collective-permute-start | bytes 37748744 | tf_op jit(solution)/shard_map/ppermute | solution.py:374
  8.1 536.1 %collective-permute-start.9 = (bf16[8192,768]{1,0:T(8,128)(2,1)}, bf16[8192,768]{1,0:T(8,128)(2,1)}, u32[]{:S(2)}, u32[]{:S(2)}) collective-permute-start(bf16[8192,768]{1,0:T(8,128)(2,1)} %dy_ref.3), channel_id=1, source_target_pairs={{0,2},{1,3},{2,0},{3,1},{4,6},{5,7},{6,4},{7,5}} | collective-permute-start | bytes 37748744 | tf_op jit(solution)/shard_map/ppermute | solution.py:374
  10.6 234.0 %collective-permute-start.5 = (bf16[8192,768]{1,0:T(8,128)(2,1)}, bf16[8192,768]{1,0:T(8,128)(2,1)}, u32[]{:S(2)}, u32[]{:S(2)}) collective-permute-start(bf16[8192,768]{1,0:T(8,128)(2,1)} %x_ref.7), channel_id=1, source_target_pairs={{0,1},{1,0},{2,3},{3,2},{4,5},{5,4},{6,7},{7,6}} | collective-permute-start | bytes 37748744 | tf_op jit(solution)/shard_map/ppermute | solution.py:374
  69.4 170.9 %collective-permute-start.4 = (f32[8,2,640]{2,0,1:T(8,128)}, f32[8,2,640]{2,0,1:T(8,128)}, u32[]{:S(2)}, u32[]{:S(2)}) collective-permute-start(f32[8,2,640]{2,0,1:T(8,128)} %get-tuple-element.208), channel_id=1, source_target_pairs={{0,1},{1,0},{2,3},{3,2},{4,5},{5,4},{6,7},{7,6}} | collective-permute-start | bytes 122888 | tf_op jit(solution)/shard_map/ppermute | solution.py:374
  75.6 341.3 %collective-permute-start.7 = (bf16[4096,768]{1,0:T(8,128)(2,1)}, bf16[4096,768]{1,0:T(8,128)(2,1)}, u32[]{:S(2)}, u32[]{:S(2)}) collective-permute-start(bf16[4096,768]{1,0:T(8,128)(2,1)} %constant_dynamic-slice_fusion), channel_id=1, source_target_pairs={{0,2},{1,3},{2,0},{3,1},{4,6},{5,7},{6,4},{7,5}} | collective-permute-start | bytes 18874376 | tf_op jit(solution)/shard_map/ppermute | solution.py:374
  99.7 25.8 %copy-start.8 = (f32[1,768]{1,0:T(1,128)S(1)}, f32[1,768]{1,0:T(1,128)}, u32[]{:S(2)}) copy-start(f32[1,768]{1,0:T(1,128)} %reshape.197.scale_ref) | copy-start | bytes 9220
  179.3 1.3 copy-start.11
  180.6 55.7 %copy-start.12 = (s32[8192,2]{1,0:T(8,128)S(1)}, s32[8192,2]{1,0:T(8,128)}, u32[]{:S(2)}) copy-start(s32[8192,2]{1,0:T(8,128)} %get-tuple-element.134) | copy-start | bytes 196612
  233.6 1.3 copy-start.6
  235.0 1.3 copy-start.9
  240.2 451.6 %collective-permute-start.2 = (f32[8,2,640]{2,0,1:T(8,128)}, f32[8,2,640]{2,0,1:T(8,128)}, u32[]{:S(2)}, u32[]{:S(2)}) collective-permute-start(f32[8,2,640]{2,0,1:T(8,128)} %get-tuple-element.209), channel_id=1, source_target_pairs={{0,3},{1,2},{2,1},{3,0},{4,7},{5,6},{6,5},{7,4}} | collective-permute-start | bytes 122888 | tf_op jit(solution)/shard_map/ppermute | solution.py:374
  244.6 297.1 %collective-permute-start.3 = (f32[8,2,640]{2,0,1:T(8,128)}, f32[8,2,640]{2,0,1:T(8,128)}, u32[]{:S(2)}, u32[]{:S(2)}) collective-permute-start(f32[8,2,640]{2,0,1:T(8,128)} %get-tuple-element.210), channel_id=1, source_target_pairs={{0,2},{1,3},{2,0},{3,1},{4,6},{5,7},{6,4},{7,5}} | collective-permute-start | bytes 122888 | tf_op jit(solution)/shard_map/ppermute | solution.py:374
  416.9 489.6 %collective-permute-start.19 = (f32[8,128]{1,0:T(8,128)}, f32[8,128]{1,0:T(8,128)}, u32[]{:S(2)}, u32[]{:S(2)}) collective-permute-start(f32[8,128]{1,0:T(8,128)} %get-tuple-element.128), channel_id=1, source_target_pairs={{0,1},{1,0},{2,3},{3,2},{4,5},{5,4},{6,7},{7,6}} | collective-permute-start | bytes 12296 | tf_op jit(solution)/shard_map/ppermute | solution.py:374
  416.9 151.7 %collective-permute-start.8 = (bf16[4096,768]{1,0:T(8,128)(2,1)}, bf16[4096,768]{1,0:T(8,128)(2,1)}, u32[]{:S(2)}, u32[]{:S(2)}) collective-permute-start(bf16[4096,768]{1,0:T(8,128)(2,1)} %collective-permute-done.7.refs_0_), channel_id=1, source_target_pairs={{0,4},{4,0},{1,5},{5,1},{2,6},{6,2},{3,7},{7,3}} | collective-permute-start | bytes 18874376 | tf_op jit(solution)/shard_map/ppermute | solution.py:377
  541.7 154.5 %collective-permute-start.10 = (bf16[4096,768]{1,0:T(8,128)(2,1)}, bf16[4096,768]{1,0:T(8,128)(2,1)}, u32[]{:S(2)}, u32[]{:S(2)}) collective-permute-start(bf16[4096,768]{1,0:T(8,128)(2,1)} %collective-permute-done.7.refs_0_), channel_id=1, source_target_pairs={{0,1},{1,0},{2,3},{3,2},{4,5},{5,4},{6,7},{7,6}} | collective-permute-start | bytes 18874376 | tf_op jit(solution)/shard_map/ppermute | solution.py:374
  542.7 2.5 copy-start.30
  544.2 176.5 %collective-permute-start.12 = (bf16[8192,768]{1,0:T(8,128)(2,1)}, bf16[8192,768]{1,0:T(8,128)(2,1)}, u32[]{:S(2)}, u32[]{:S(2)}) collective-permute-start(bf16[8192,768]{1,0:T(8,128)(2,1)} %collective-permute-done.9.refs_0_), channel_id=1, source_target_pairs={{0,1},{1,0},{2,3},{3,2},{4,5},{5,4},{6,7},{7,6}} | collective-permute-start | bytes 37748744 | tf_op jit(solution)/shard_map/ppermute | solution.py:374
  568.6 127.7 %collective-permute-start.11 = (bf16[4096,768]{1,0:T(8,128)(2,1)}, bf16[4096,768]{1,0:T(8,128)(2,1)}, u32[]{:S(2)}, u32[]{:S(2)}) collective-permute-start(bf16[4096,768]{1,0:T(8,128)(2,1)} %collective-permute-done.8.refs_1_), channel_id=1, source_target_pairs={{0,1},{1,0},{2,3},{3,2},{4,5},{5,4},{6,7},{7,6}} | collective-permute-start | bytes 18874376 | tf_op jit(solution)/shard_map/ppermute | solution.py:374
  691.8 215.1 %collective-permute-start.20 = (f32[8,128]{1,0:T(8,128)}, f32[8,128]{1,0:T(8,128)}, u32[]{:S(2)}, u32[]{:S(2)}) collective-permute-start(f32[8,128]{1,0:T(8,128)} %get-tuple-element.128), channel_id=1, source_target_pairs={{0,2},{1,3},{2,0},{3,1},{4,6},{5,7},{6,4},{7,5}} | collective-permute-start | bytes 12296 | tf_op jit(solution)/shard_map/ppermute | solution.py:374
  694.0 26.6 %copy-start.29 = (s32[5120]{0:T(1024)}, s32[5120]{0:T(1024)S(1)}, u32[]{:S(2)}) copy-start(s32[5120]{0:T(1024)S(1)} %max.35.idx_ref) | copy-start | bytes 61444
  696.2 276.9 %collective-permute-start.21 = (f32[8,128]{1,0:T(8,128)}, f32[8,128]{1,0:T(8,128)}, u32[]{:S(2)}, u32[]{:S(2)}) collective-permute-start(f32[8,128]{1,0:T(8,128)} %get-tuple-element.128), channel_id=1, source_target_pairs={{0,3},{1,2},{2,1},{3,0},{4,7},{5,6},{6,5},{7,4}} | collective-permute-start | bytes 12296 | tf_op jit(solution)/shard_map/ppermute | solution.py:374
  696.3 212.2 %collective-permute-start.15 = (bf16[8,640,384]{2,1,0:T(8,128)(2,1)}, bf16[8,640,384]{2,1,0:T(8,128)(2,1)}, u32[]{:S(2)}, u32[]{:S(2)}) collective-permute-start(bf16[8,640,384]{2,1,0:T(8,128)(2,1)} %get-tuple-element.123), channel_id=1, source_target_pairs={{0,4},{4,0},{1,5},{5,1},{2,6},{6,2},{3,7},{7,3}} | collective-permute-start | bytes 11796488 | tf_op jit(solution)/shard_map/ppermute | solution.py:377
  720.7 188.2 %collective-permute-start.16 = (bf16[8,640,384]{2,1,0:T(8,128)(2,1)}, bf16[8,640,384]{2,1,0:T(8,128)(2,1)}, u32[]{:S(2)}, u32[]{:S(2)}) collective-permute-start(bf16[8,640,384]{2,1,0:T(8,128)(2,1)} %get-tuple-element.124), channel_id=1, source_target_pairs={{0,4},{4,0},{1,5},{5,1},{2,6},{6,2},{3,7},{7,3}} | collective-permute-start | bytes 11796488 | tf_op jit(solution)/shard_map/ppermute | solution.py:377
  906.5 88.1 %collective-permute-start.18 = (bf16[8,640,384]{2,1,0:T(8,128)(2,1)}, bf16[8,640,384]{2,1,0:T(8,128)(2,1)}, u32[]{:S(2)}, u32[]{:S(2)}) collective-permute-start(bf16[8,640,384]{2,1,0:T(8,128)(2,1)} %get-tuple-element.127), channel_id=1, source_target_pairs={{0,4},{4,0},{1,5},{5,1},{2,6},{6,2},{3,7},{7,3}} | collective-permute-start | bytes 11796488 | tf_op jit(solution)/shard_map/ppermute | solution.py:377
  906.9 172.0 %collective-permute-start.27 = (bf16[8,640,384]{2,1,0:T(8,128)(2,1)}, bf16[8,640,384]{2,1,0:T(8,128)(2,1)}, u32[]{:S(2)}, u32[]{:S(2)}) collective-permute-start(bf16[8,640,384]{2,1,0:T(8,128)(2,1)} %get-tuple-element.147), channel_id=1, source_target_pairs={{0,4},{4,0},{1,5},{5,1},{2,6},{6,2},{3,7},{7,3}} | collective-permute-start | bytes 11796488 | tf_op jit(solution)/shard_map/ppermute | solution.py:377
  908.5 254.6 %collective-permute-start.23 = (bf16[8,640,384]{2,1,0:T(8,128)(2,1)}, bf16[8,640,384]{2,1,0:T(8,128)(2,1)}, u32[]{:S(2)}, u32[]{:S(2)}) collective-permute-start(bf16[8,640,384]{2,1,0:T(8,128)(2,1)} %get-tuple-element.130), channel_id=1, source_target_pairs={{0,4},{4,0},{1,5},{5,1},{2,6},{6,2},{3,7},{7,3}} | collective-permute-start | bytes 11796488 | tf_op jit(solution)/shard_map/ppermute | solution.py:377
  908.9 507.4 %collective-permute-start.29 = (bf16[8,640,384]{2,1,0:T(8,128)(2,1)}, bf16[8,640,384]{2,1,0:T(8,128)(2,1)}, u32[]{:S(2)}, u32[]{:S(2)}) collective-permute-start(bf16[8,640,384]{2,1,0:T(8,128)(2,1)} %get-tuple-element.151), channel_id=1, source_target_pairs={{0,4},{4,0},{1,5},{5,1},{2,6},{6,2},{3,7},{7,3}} | collective-permute-start | bytes 11796488 | tf_op jit(solution)/shard_map/ppermute | solution.py:377
  910.6 168.3 %copy-start.10 = (bf16[4,640,384]{2,1,0:T(8,128)(2,1)S(1)}, bf16[4,640,384]{2,1,0:T(8,128)(2,1)}, u32[]{:S(2)}) copy-start(bf16[4,640,384]{2,1,0:T(8,128)(2,1)} %copy-done.9) | copy-start | bytes 5898244
  973.1 190.1 %copy-start.32 = (bf16[4,640,384]{2,1,0:T(8,128)(2,1)S(1)}, bf16[4,640,384]{2,1,0:T(8,128)(2,1)}, u32[]{:S(2)}) copy-start(bf16[4,640,384]{2,1,0:T(8,128)(2,1)} %get-tuple-element.120) | copy-start | bytes 5898244
  973.1 190.5 %copy-start.15 = (bf16[8,640,384]{2,1,0:T(8,128)(2,1)S(1)}, bf16[8,640,384]{2,1,0:T(8,128)(2,1)}, u32[]{:S(2)}) copy-start(bf16[8,640,384]{2,1,0:T(8,128)(2,1)} %get-tuple-element.126) | copy-start | bytes 11796484
  973.1 316.4 %collective-permute-start = (bf16[4,640,384]{2,1,0:T(8,128)(2,1)}, bf16[4,640,384]{2,1,0:T(8,128)(2,1)S(1)}, u32[]{:S(2)}, u32[]{:S(2)}) collective-permute-start(bf16[4,640,384]{2,1,0:T(8,128)(2,1)} %copy-done.11), channel_id=1, source_target_pairs={{0,4},{4,0},{1,5},{5,1},{2,6},{6,2},{3,7},{7,3}} | collective-permute-start | bytes 5898248 | tf_op jit(solution)/shard_map/ppermute | solution.py:377
  994.7 337.0 %collective-permute-start.1 = (bf16[4,640,384]{2,1,0:T(8,128)(2,1)}, bf16[4,640,384]{2,1,0:T(8,128)(2,1)S(1)}, u32[]{:S(2)}, u32[]{:S(2)}) collective-permute-start(bf16[4,640,384]{2,1,0:T(8,128)(2,1)} %get-tuple-element.89), channel_id=1, source_target_pairs={{0,4},{4,0},{1,5},{5,1},{2,6},{6,2},{3,7},{7,3}} | collective-permute-start | bytes 5898248 | tf_op jit(solution)/shard_map/ppermute | solution.py:377
  1078.9 294.8 %collective-permute-start.13 = (bf16[4,640,384]{2,1,0:T(8,128)(2,1)S(1)}, bf16[4,640,384]{2,1,0:T(8,128)(2,1)S(1)}, u32[]{:S(2)}, u32[]{:S(2)}) collective-permute-start(bf16[4,640,384]{2,1,0:T(8,128)(2,1)S(1)} %copy-done.10), channel_id=1, source_target_pairs={{0,4},{4,0},{1,5},{5,1},{2,6},{6,2},{3,7},{7,3}} | collective-permute-start | bytes 5898248 | tf_op jit(solution)/shard_map/ppermute | solution.py:377
  1085.5 83.1 %copy-start.13 = (bf16[8,640,384]{2,1,0:T(8,128)(2,1)S(1)}, bf16[8,640,384]{2,1,0:T(8,128)(2,1)}, u32[]{:S(2)}) copy-start(bf16[8,640,384]{2,1,0:T(8,128)(2,1)} %get-tuple-element.144) | copy-start | bytes 11796484
  1163.2 251.7 %collective-permute-start.14 = (bf16[4,640,384]{2,1,0:T(8,128)(2,1)S(1)}, bf16[4,640,384]{2,1,0:T(8,128)(2,1)S(1)}, u32[]{:S(2)}, u32[]{:S(2)}) collective-permute-start(bf16[4,640,384]{2,1,0:T(8,128)(2,1)S(1)} %copy-done.32), channel_id=1, source_target_pairs={{0,4},{4,0},{1,5},{5,1},{2,6},{6,2},{3,7},{7,3}} | collective-permute-start | bytes 5898248 | tf_op jit(solution)/shard_map/ppermute | solution.py:377
  1168.6 5.3 copy-start.14
  1173.9 5.2 copy-start.16
  1289.5 84.3 %copy-start.17 = (bf16[4,640,384]{2,1,0:T(8,128)(2,1)}, bf16[4,640,384]{2,1,0:T(8,128)(2,1)S(1)}, u32[]{:S(2)}) copy-start(bf16[4,640,384]{2,1,0:T(8,128)(2,1)S(1)} %collective-permute-done) | copy-start | bytes 5898244
  1289.5 195.1 %collective-permute-start.17 = (bf16[8,640,384]{2,1,0:T(8,128)(2,1)}, bf16[8,640,384]{2,1,0:T(8,128)(2,1)}, u32[]{:S(2)}, u32[]{:S(2)}) collective-permute-start(bf16[8,640,384]{2,1,0:T(8,128)(2,1)} %add_convert_fusion.5), channel_id=1, source_target_pairs={{0,1},{1,0},{2,3},{3,2},{4,5},{5,4},{6,7},{7,6}} | collective-permute-start | bytes 11796488 | tf_op jit(solution)/shard_map/ppermute | solution.py:374
  1331.6 42.1 %copy-start.19 = (bf16[4,640,384]{2,1,0:T(8,128)(2,1)}, bf16[4,640,384]{2,1,0:T(8,128)(2,1)S(1)}, u32[]{:S(2)}) copy-start(bf16[4,640,384]{2,1,0:T(8,128)(2,1)S(1)} %collective-permute-done.1) | copy-start | bytes 5898244
  1331.6 168.1 %collective-permute-start.22 = (bf16[8,640,384]{2,1,0:T(8,128)(2,1)}, bf16[8,640,384]{2,1,0:T(8,128)(2,1)}, u32[]{:S(2)}, u32[]{:S(2)}) collective-permute-start(bf16[8,640,384]{2,1,0:T(8,128)(2,1)} %add_convert_fusion.4), channel_id=1, source_target_pairs={{0,2},{1,3},{2,0},{3,1},{4,6},{5,7},{6,4},{7,5}} | collective-permute-start | bytes 11796488 | tf_op jit(solution)/shard_map/ppermute | solution.py:374
  1373.7 41.1 %copy-start.21 = (bf16[4,640,384]{2,1,0:T(8,128)(2,1)}, bf16[4,640,384]{2,1,0:T(8,128)(2,1)S(1)}, u32[]{:S(2)}) copy-start(bf16[4,640,384]{2,1,0:T(8,128)(2,1)S(1)} %collective-permute-done.13) | copy-start | bytes 5898244
  1373.7 130.5 %collective-permute-start.26 = (bf16[8,640,384]{2,1,0:T(8,128)(2,1)}, bf16[8,640,384]{2,1,0:T(8,128)(2,1)}, u32[]{:S(2)}, u32[]{:S(2)}) collective-permute-start(bf16[8,640,384]{2,1,0:T(8,128)(2,1)} %add_convert_fusion.2), channel_id=1, source_target_pairs={{0,1},{1,0},{2,3},{3,2},{4,5},{5,4},{6,7},{7,6}} | collective-permute-start | bytes 11796488 | tf_op jit(solution)/shard_map/ppermute | solution.py:374
  1414.9 1.5 copy-start.23
  1414.9 93.8 %collective-permute-start.28 = (bf16[8,640,384]{2,1,0:T(8,128)(2,1)}, bf16[8,640,384]{2,1,0:T(8,128)(2,1)}, u32[]{:S(2)}, u32[]{:S(2)}) collective-permute-start(bf16[8,640,384]{2,1,0:T(8,128)(2,1)} %add_convert_fusion.1), channel_id=1, source_target_pairs={{0,2},{1,3},{2,0},{3,1},{4,6},{5,7},{6,4},{7,5}} | collective-permute-start | bytes 11796488 | tf_op jit(solution)/shard_map/ppermute | solution.py:374
  1416.4 169.9 %collective-permute-start.24 = (bf16[8,640,384]{2,1,0:T(8,128)(2,1)}, bf16[8,640,384]{2,1,0:T(8,128)(2,1)}, u32[]{:S(2)}, u32[]{:S(2)}) collective-permute-start(bf16[8,640,384]{2,1,0:T(8,128)(2,1)} %add_convert_fusion.3), channel_id=1, source_target_pairs={{0,3},{1,2},{2,1},{3,0},{4,7},{5,6},{6,5},{7,4}} | collective-permute-start | bytes 11796488 | tf_op jit(solution)/shard_map/ppermute | solution.py:374
  1478.3 9.8 copy-start.3
  1478.3 9.8 copy-start.18
  1478.3 11.6 copy-start.1
  1478.3 11.6 copy-start.20
  1484.6 7.1 copy-start.7
  1484.6 7.1 copy-start.22
  1484.6 206.5 %collective-permute-start.30 = (bf16[8,640,384]{2,1,0:T(8,128)(2,1)}, bf16[8,640,384]{2,1,0:T(8,128)(2,1)}, u32[]{:S(2)}, u32[]{:S(2)}) collective-permute-start(bf16[8,640,384]{2,1,0:T(8,128)(2,1)} %add_convert_fusion), channel_id=1, source_target_pairs={{0,3},{1,2},{2,1},{3,0},{4,7},{5,6},{6,5},{7,4}} | collective-permute-start | bytes 11796488 | tf_op jit(solution)/shard_map/ppermute | solution.py:374
  1489.8 3.6 copy-start.5
  1489.9 3.6 copy-start.24
  1508.7 82.1 %copy-start.27 = (s32[8192]{0:T(1024)S(1)}, s32[8192]{0:T(1024)}, u32[]{:S(2)}) copy-start(s32[8192]{0:T(1024)} %get-tuple-element.215) | copy-start | bytes 98308
  1590.8 40.1 %copy-start.26 = (s32[8192]{0:T(1024)S(1)}, s32[8192]{0:T(1024)}, u32[]{:S(2)}) copy-start(s32[8192]{0:T(1024)} %get-tuple-element.214) | copy-start | bytes 98308
  1690.6 84.9 %collective-permute-start.31 = (f32[2,8192]{1,0:T(2,128)S(1)}, f32[2,8192]{1,0:T(2,128)S(1)}, u32[]{:S(2)}, u32[]{:S(2)}) collective-permute-start(f32[2,8192]{1,0:T(2,128)S(1)} %copy.127), channel_id=1, source_target_pairs={{0,4},{4,0},{1,5},{5,1},{2,6},{6,2},{3,7},{7,3}} | collective-permute-start | bytes 196616 | tf_op jit(solution)/shard_map/ppermute | solution.py:377
  1814.1 4.0 collective-permute-start.32
  1815.7 140.0 %collective-permute-start.25 = (bf16[8192,384]{1,0:T(8,128)(2,1)}, bf16[8192,384]{1,0:T(8,128)(2,1)}, u32[]{:S(2)}, u32[]{:S(2)}) collective-permute-start(bf16[8192,384]{1,0:T(8,128)(2,1)} %get-tuple-element.136.own_ref), channel_id=1, source_target_pairs={{0,4},{4,0},{1,5},{5,1},{2,6},{6,2},{3,7},{7,3}} | collective-permute-start | bytes 18874376 | tf_op jit(solution)/shard_map/ppermute | solution.py:377
  1820.8 18.9 copy-start.31
  1820.8 18.9 copy-start.28
  1836.0 254.2 %collective-permute-start.33 = (bf16[8192,384]{1,0:T(8,128)(2,1)}, bf16[8192,384]{1,0:T(8,128)(2,1)}, u32[]{:S(2)}, u32[]{:S(2)}) collective-permute-start(bf16[8192,384]{1,0:T(8,128)(2,1)} %shard_map.146.own_ref), channel_id=1, source_target_pairs={{0,4},{4,0},{1,5},{5,1},{2,6},{6,2},{3,7},{7,3}} | collective-permute-start | bytes 18874376 | tf_op jit(solution)/shard_map/ppermute | solution.py:377
  (4 other events, 4.5 us)
Sparse Core Ops, SparseCore 0:
  1841.6 40.5 all-reduce.1

commit v2 on v1

--- a/solution.py
+++ b/solution.py
@@ -120,12 +120,12 @@
             owner = route // local_exp
             spot = (owner ^ ep_ref[0]) * (local_exp * cap) + (route - owner * local_exp) * cap + pos
             row_ref[:, c:c + 1] = jnp.where(kept, spot, 0)
+            col_ref[:, 6 + c:7 + c] = jnp.where(kept, spot % 2, 0).astype(jnp.float32)
             col_ref[:, 2 + c:3 + c] = jnp.where(kept, 1.0, 0.0)
         col_ref[:, 0:1] = n_first
         col_ref[:, 1:2] = n_second
         col_ref[:, 4:5] = inv
         col_ref[:, 5:6] = log_norm
-        col_ref[:, 6:8] = jnp.zeros((rows, 2), jnp.float32)
         token = lax.broadcasted_iota(jnp.int32, (rows, 1), 0) + ((step - blocks) * rows + 1)
         tok_hi = (token // 128).astype(jnp.float32)
         tok_lo = (token % 128).astype(jnp.float32)
@@ -205,7 +205,7 @@
 
         def body(q, carry):
             base = q * group
-            vals = [store[pl.ds(pl.multiple_of(idx_ref[start + base + r] * 8, 8), 8), :] for r in range(group)]
+            vals = [store[pl.ds(pl.multiple_of(idx_ref[start + base + r], 8), 8), :] for r in range(group)]
             for r in range(group):
                 stage[pl.ds(pl.multiple_of((base + r) * 8, 8), 8), :] = vals[r]
             return carry
@@ -234,20 +234,20 @@
         compiler_params=pltpu.CompilerParams(dimension_semantics=("arbitrary",), vmem_limit_bytes=60 * 1024 * 1024),
         cost_estimate=pl.CostEstimate(flops=40_000_000_000, bytes_accessed=4 * width * idx.shape[0], transcendentals=0),
         name="gather_rows",
-    )(idx, *srcs)
-
-
-def combine_kernel(tp_ref, x_ref, dy_ref, o1_ref, o2_ref, col_ref, y_ref, dn_ref):
+    )(idx * 8, *srcs)
+
+
+def combine_kernel(start, pick_first, pick_second, x_ref, dy_ref, col_ref, y_ref, dn_ref):
     col = col_ref[...]
-    o1 = jnp.where(col[:, 2:3] > 0.0, o1_ref[...].astype(jnp.float32), 0.0)
-    o2 = jnp.where(col[:, 3:4] > 0.0, o2_ref[...].astype(jnp.float32), 0.0)
+    o1 = jnp.where(col[:, 2:3] > 0.0, pick_first(col[:, 6:7]), 0.0)
+    o2 = jnp.where(col[:, 3:4] > 0.0, pick_second(col[:, 7:8]), 0.0)
     y_ref[...] = (x_ref[...].astype(jnp.float32) + col[:, 0:1] * o1 + col[:, 1:2] * o2).astype(y_ref.dtype)
     dy = dy_ref[...].astype(jnp.float32)
     dn_ref[:, 0:1] = jnp.sum(dy * o1, axis=-1, keepdims=True)
     dn_ref[:, 1:2] = jnp.sum(dy * o2, axis=-1, keepdims=True)
 
 
-def norm_kernel(tp_ref, x_ref, d1_ref, d2_ref, prob_ref, idx_ref, dn_ref, aux_ref, wr_ref, scale_ref, col_ref, dxn_ref, mix_ref, ds_ref, dr_ref):
+def norm_kernel(start, pick_first, pick_second, x_ref, prob_ref, idx_ref, dn_ref, aux_ref, wr_ref, scale_ref, col_ref, dxn_ref, mix_ref, ds_ref, dr_ref):
     col = col_ref[...]
     n_first, n_second = col[:, 0:1], col[:, 1:2]
     dn_first, dn_second = dn_ref[:, 0:1], dn_ref[:, 1:2]
@@ -259,7 +259,7 @@
     dl = dl + (2.0 * Z_COEF) * col[:, 5:6] * prob
     dl = dl + jnp.where(idx_ref[:, 0:1] == lane, n_first * (dn_first - gate_mix), 0.0)
     dl = dl + jnp.where(idx_ref[:, 1:2] == lane, n_second * (dn_second - gate_mix), 0.0)
-    du = jnp.where(col[:, 2:3] > 0.0, d1_ref[...].astype(jnp.float32), 0.0) + jnp.where(col[:, 3:4] > 0.0, d2_ref[...].astype(jnp.float32), 0.0)
+    du = jnp.where(col[:, 2:3] > 0.0, pick_first(col[:, 6:7]), 0.0) + jnp.where(col[:, 3:4] > 0.0, pick_second(col[:, 7:8]), 0.0)
     du = du + lax.dot_general(dl, wr_ref[...], (((1,), (1,)), ((), ())), preferred_element_type=jnp.float32)
     xn = x_ref[...].astype(jnp.float32) * col[:, 4:5]
     dxn = du * scale_ref[...]
@@ -269,12 +269,12 @@
     ds = jnp.sum(du * xn, axis=0, keepdims=True)
     dr = lax.dot_general(u_wide, dl, (((0,), (0,)), ((), ())), preferred_element_type=jnp.float32)
 
-    @pl.when(pl.program_id(0) == 0)
+    @pl.when(pl.program_id(0) == start)
     def _():
         ds_ref[...] = ds
         dr_ref[...] = dr
 
-    @pl.when(pl.program_id(0) > 0)
+    @pl.when(pl.program_id(0) > start)
     def _():
         ds_ref[...] += ds
         dr_ref[...] += dr
@@ -294,28 +294,86 @@
     out_ref[:, half:] = jnp.where(first, other, own)
 
 
-def rows_call(kernel, tp_vec, ins, outs, rows, block):
-    specs, args = [], []
+def picking(kernel, parts, fills, blk, group):
+    def body(tp_ref, first_ref, second_ref, *refs):
+        srcs, rest = refs[:parts], refs[parts:-3]
+        store, stage_first, stage_second = refs[-3:]
+        step = pl.program_id(0)
+        start = parts * fills
+        chunks = srcs[0].shape[1] // 128
+        rows = stage_first.shape[0] // 8
+        for p in range(parts):
+
+            @pl.when((step >= p * fills) & (step < (p + 1) * fills))
+            def _(p=p):
+                val = srcs[p][...].astype(jnp.float32)
+                base = pl.multiple_of(step * (blk * 4), blk * 4)
+                for j in range(chunks):
+                    store[pl.ds(base + j, blk, stride=4), :] = val[:, j * 128:(j + 1) * 128]
+
+        @pl.when(step >= start)
+        def _():
+            offset = (step - start) * rows
+
+            def move(q, carry):
+                base = q * group
+                for idx_ref, stage in ((first_ref, stage_first), (second_ref, stage_second)):
+                    vals = [store[pl.ds(pl.multiple_of(idx_ref[offset + base + r], 8), 8), :] for r in range(group)]
+                    for r in range(group):
+                        stage[pl.ds(pl.multiple_of((base + r) * 8, 8), 8), :] = vals[r]
+                return carry
+
+            lax.fori_loop(0, rows // group, move, 0)
+
+            def picker(stage):
+                def pick(odd):
+                    return jnp.concatenate([jnp.where(odd > 0.0, stage[pl.ds(4 + j, rows, stride=8), :], stage[pl.ds(j, rows, stride=8), :]) for j in range(chunks)], axis=1)
+
+                return pick
+
+            kernel(start, picker(stage_first), picker(stage_second), *rest)
+
+    return body
+
+
+def rows_call(kernel, tp_vec, ins, outs, rows, block, picks=None):
+    specs, args, scalars, scratch, start = [], [], [tp_vec], [], 0
+    if picks is not None:
+        srcs, first, second = picks
+        count, width = srcs[0].shape
+        blk = 640
+        fills = count // blk
+        start = len(srcs) * fills
+        kernel = picking(kernel, len(srcs), fills, blk, 16)
+        scalars += [first, second]
+        for p, src in enumerate(srcs):
+            specs.append(pl.BlockSpec((blk, width), functools.partial(lambda p, i, *_: (jnp.clip(i - p * fills, 0, fills - 1), 0), p)))
+            args.append(src)
+        scratch = [pltpu.VMEM((len(srcs) * count * 4, 128), jnp.float32), pltpu.VMEM((block * 8, 128), jnp.float32), pltpu.VMEM((block * 8, 128), jnp.float32)]
+
+    def at(i):
+        return jnp.maximum(i - start, 0) if start else i
+
     for kind, arr in ins:
         if kind == 'half':
-            specs.append(pl.BlockSpec((block, arr.shape[1] // 2), lambda i, tp: (i, tp[0])))
+            specs.append(pl.BlockSpec((block, arr.shape[1] // 2), lambda i, tp, *_: (at(i), tp[0])))
         elif kind == 'row':
-            specs.append(pl.BlockSpec((block, arr.shape[1]), lambda i, tp: (i, 0)))
+            specs.append(pl.BlockSpec((block, arr.shape[1]), lambda i, *_: (at(i), 0)))
         elif kind == 'same':
-            specs.append(pl.BlockSpec(arr.shape, lambda i, tp: (0, 0)))
+            specs.append(pl.BlockSpec(arr.shape, lambda i, *_: (0, 0)))
         elif kind == 'lanes':
-            specs.append(pl.BlockSpec((1, arr.shape[1] // 2), lambda i, tp: (0, tp[0])))
+            specs.append(pl.BlockSpec((1, arr.shape[1] // 2), lambda i, tp, *_: (0, tp[0])))
         else:
-            specs.append(pl.BlockSpec((arr.shape[0] // 2, arr.shape[1]), lambda i, tp: (tp[0], 0)))
+            specs.append(pl.BlockSpec((arr.shape[0] // 2, arr.shape[1]), lambda i, tp, *_: (tp[0], 0)))
         args.append(arr)
-    out_specs = [pl.BlockSpec((block if o.shape[0] == rows else o.shape[0], o.shape[1]), (lambda i, tp: (i, 0)) if o.shape[0] == rows else (lambda i, tp: (0, 0))) for o in outs]
+    out_specs = [pl.BlockSpec((block if o.shape[0] == rows else o.shape[0], o.shape[1]), (lambda i, *_: (at(i), 0)) if o.shape[0] == rows else (lambda i, *_: (0, 0))) for o in outs]
     return pl.pallas_call(
         kernel,
-        grid_spec=pltpu.PrefetchScalarGridSpec(num_scalar_prefetch=1, grid=(rows // block,), in_specs=specs, out_specs=out_specs),
+        grid_spec=pltpu.PrefetchScalarGridSpec(num_scalar_prefetch=len(scalars), grid=(start + rows // block,), in_specs=specs, out_specs=out_specs, scratch_shapes=scratch),
         out_shape=outs,
-        compiler_params=pltpu.CompilerParams(dimension_semantics=("arbitrary",)),
-        cost_estimate=pl.CostEstimate(flops=10_000_000_000, bytes_accessed=sum(a.size * 2 for _, a in ins), transcendentals=0),
-    )(tp_vec, *args)
+        compiler_params=pltpu.CompilerParams(dimension_semantics=("arbitrary",), vmem_limit_bytes=60 * 1024 * 1024),
+        cost_estimate=pl.CostEstimate(flops=10_000_000_000, bytes_accessed=sum(a.size * 2 for a in args), transcendentals=0),
+    )(*scalars, *args)
 
 
 def ffn_call(k, base, count, chunks, tp_id, x_rows, dy_rows, gate, scale, wg, wl, wo, bufs, tile):
@@ -387,10 +445,14 @@
         tp_id = lax.axis_index('tp')
         tp_vec = tp_id.reshape(1).astype(jnp.int32)
         part_rows = tok_count // 2
-        x_near = swap(lax.dynamic_slice_in_dim(x_loc, tp_id * part_rows, part_rows, 0), 2)
+        pieces = 2
+        piece = part_rows // pieces
+        x_near = [swap(lax.dynamic_slice_in_dim(x_loc, tp_id * part_rows + p * piece, piece, 0), 2) for p in range(pieces)]
         dy_far = swap(dy_loc, 2)
-        x_side = swap_tp(x_near)
-        x_rows = [[x_loc], [swap(x_loc, 1)], [x_near, x_side], [swap(x_near, 1), swap(x_side, 1)]]
+        x_side = [swap_tp(x_near[0])]
+        x_side.append(swap_tp(x_near[1]))
+        x_far = x_near + x_side
+        x_rows = [[x_loc], [swap(x_loc, 1)], x_far, [swap(p, 1) for p in x_far]]
         dy_rows = [[dy_loc], [swap(dy_loc, 1)], [dy_far], [swap(dy_far, 1)]]
         scale_row = norm_scale.reshape(1, width)
         prob, cols, rows, tab, sums_own = router_call(ep_id.reshape(1).astype(jnp.int32), x_loc, idx_loc, scale_row, w_router, cap, local_exp, 512)
@@ -422,7 +484,7 @@
             gate_k = mine[:, 1].reshape(local_exp, cap, 1)
             xr = take(x_rows[k], tok_x)
             dr = take(dy_rows[k], tok)
-            units = 2 if k == 0 else 1
+            units = 2
             count = local_exp // units
             got = []
             for unit in range(units):
@@ -438,19 +500,26 @@
             out = lax.optimization_barrier((*arrs, held))
             return out[:-1]
 
-        tail = sent[-1][0][0]
-        for k in range(ep_size - 1):
+        tail = sent[-1][-1][0]
+        for k in range(ep_size - 2):
             for unit, (keep_o, got_o, keep_d, got_d) in enumerate(sent[k]):
-                if k == ep_size - 2:
-                    got_o, *sums_far = after(tail, got_o, *sums_far)
-                    got_d, d_gate = lax.optimization_barrier((got_d, d_gate))
-                else:
-                    got_o, got_d = after(tail, got_o, got_d)
+                got_o, = after(tail, got_o)
+                got_d, d_out = lax.optimization_barrier((got_d, d_out))
                 sent[k][unit] = (keep_o, got_o, keep_d, got_d)
-        keep_o, got_o, keep_d, got_d = sent[-1][0]
-        got_o, d_lin = lax.optimization_barrier((got_o, d_lin))
-        got_d, d_out = lax.optimization_barrier((got_d, d_out))
-        sent[-1] = [(keep_o, got_o, keep_d, got_d)]
+        near = sent[-1][0][0]
+        for unit, (keep_o, got_o, keep_d, got_d) in enumerate(sent[-2]):
+            got_o, = after(near, got_o)
+            if unit:
+                got_d, d_gate = lax.optimization_barrier((got_d, d_gate))
+            else:
+                got_d, = after(near, got_d)
+            sent[-2][unit] = (keep_o, got_o, keep_d, got_d)
+        sums_far = after(tail, *sums_far)
+        for unit in range(2):
+            keep_o, got_o, keep_d, got_d = sent[-1][unit]
+            got_o, d_gate = lax.optimization_barrier((got_o, d_gate))
+            got_d, d_lin = lax.optimization_barrier((got_d, d_lin))
+            sent[-1][unit] = (keep_o, got_o, keep_d, got_d)
         o_back, du_back = [], []
         for k in range(ep_size):
             for keep_o, got_o, keep_d, got_d in sent[k]:
@@ -459,17 +528,14 @@
                 du_sum = fold(keep_d, got_d)
                 du_back.append(swap(du_sum, k) if k else du_sum)
 
-        row_first, row_second = rows[:, 0], rows[:, 1]
-
-        def pick(src, rows):
-            return src.at[rows].get(mode='promise_in_bounds')
+        tile_rows = (rows >> 1) * 8
+        row_first, row_second = tile_rows[:, 0], tile_rows[:, 1]
 
         half_rows = jax.ShapeDtypeStruct((tok_count, half), jnp.bfloat16)
-        o_all = jnp.concatenate(o_back, axis=0).reshape(experts * cap, half)
+        o_parts = [arr.reshape(-1, half) for arr in o_back]
         y_half, dn_part = rows_call(
-            combine_kernel, tp_vec,
-            [('half', x_loc), ('half', dy_loc), ('row', pick(o_all, row_first)), ('row', pick(o_all, row_second)), ('row', cols)],
-            [half_rows, jax.ShapeDtypeStruct((tok_count, 2), jnp.float32)], tok_count, 1024)
+            combine_kernel, tp_vec, [('half', x_loc), ('half', dy_loc), ('row', cols)],
+            [half_rows, jax.ShapeDtypeStruct((tok_count, 2), jnp.float32)], tok_count, 512, (o_parts, row_first, row_second))
         dn_part = dn_part.T
         dn_other = swap_tp(dn_part)
         dn = (dn_part + dn_other).T
@@ -485,13 +551,12 @@
         z_loss = Z_COEF * stats[2, 0] / tokens
         aux_loss = AUX_COEF * experts * jnp.sum(frac_first * stats[1, :experts]) / tokens
         aux_row = (AUX_COEF * experts * frac_first).reshape(1, experts)
-        du_all = jnp.concatenate(du_back, axis=0).reshape(experts * cap, half)
-        du_first = pick(du_all, row_first)
-        du_second = pick(du_all, row_second)
+        du_parts = [arr.reshape(-1, half) for arr in du_back]
         dxn, mix, d_scale_half, d_router_half = rows_call(
-          norm_kernel, tp_vec,
-          [('half', x_loc), ('row', du_first), ('row', du_second), ('row', prob), ('row', idx_loc), ('row', dn), ('same', aux_row), ('deep', w_router), ('lanes', scale_row), ('row', cols)],
-          [jax.ShapeDtypeStruct((tok_count, half), jnp.float32), jax.ShapeDtypeStruct((tok_count, 1), jnp.float32), jax.ShapeDtypeStruct((1, half), jnp.float32), jax.ShapeDtypeStruct((half, experts), jnp.float32)], tok_count, 1024)
+            norm_kernel, tp_vec,
+            [('half', x_loc), ('row', prob), ('row', idx_loc), ('row', dn), ('same', aux_row), ('deep', w_router), ('lanes', scale_row), ('row', cols)],
+            [jax.ShapeDtypeStruct((tok_count, half), jnp.float32), jax.ShapeDtypeStruct((tok_count, 1), jnp.float32), jax.ShapeDtypeStruct((1, half), jnp.float32), jax.ShapeDtypeStruct((half, experts), jnp.float32)],
+            tok_count, 512, (du_parts, row_first, row_second))
         mix = mix.reshape(tok_count)
         mix = ((mix + swap_tp(mix)) / width).reshape(tok_count, 1)
         dx_half = rows_call(dx_kernel, tp_vec, [('half', x_loc), ('half', dy_loc), ('row', dxn), ('row', cols), ('row', mix)], [half_rows], tok_count, 1024)[0]

time: 2120 us -> 2150 us (1.014)
  local copies, waits for them, and re-layouts: 229 us -> 69.6 us
  Pallas kernels: 721 us -> 824 us
  waiting for transfers between devices: 869 us -> 948 us
    gather x4 -> x0, local copies, waits for them, and re-layouts: 160 us -> none  [pick(): return src.at[rows].get(mode='promise_in_bounds')]
    pallas_call x5, Pallas kernels: 81.4 us -> 182 us  [rows_call(): pl.pallas_call(kernel, grid_spec=pltpu.PrefetchScalarGridSpec(num_scalar_...]
    ppermute x15 -> x22, waiting for transfers between devices: 607 us -> 657 us  [swap_tp(): return lax.ppermute(arr, 'tp', [(0, 1), (1, 0)])]
    ppermute x19 -> x28, waiting for transfers between devices: 222 us -> 249 us  [swap(): return lax.ppermute(arr, 'ep', [(i, i ^ k) for i in range(ep_size)])]
    pallas_call x5 -> x8, Pallas kernels: 400 us -> 412 us  [ffn_call(): pl.pallas_call(ffn_kernel, grid=(count, steps), in_specs=in_specs, out_sp...]
    convert_element_type x6 -> x16, other arithmetic: 33 us -> 43.1 us  [fold(): (keep.astype(jnp.float32) + send.astype(jnp.float32)).astype(jnp.bfloat16)]
  transfers between devices with their start and end apart: 35 -> 51, of which waited for: 13 -> 25; matrix products, arithmetic and copies ran while one was open for 22% -> 13% of each run, Pallas kernels for 32% -> 34%
where the time goes in v2:
time: 2150 us; the launch traced here: 2140 us
  waiting for transfers between devices  948 us (44%)
  Pallas kernels  824 us (38%)
  matrix products  186 us (9%)
  local copies, waits for them, and re-layouts  69.6 us (3%)
  other arithmetic  64 us (3%)
  starting transfers between devices  34.8 us (2%)
    ppermute x22, waiting for transfers between devices, swap_tp(): return lax.ppermute(arr, 'tp', [(0, 1), (1, 0)])  657 us
    pallas_call x8, Pallas kernels, ffn_call(): pl.pallas_call(ffn_kernel, grid=(count, steps), in_specs=in_specs, out_sp...  412 us
    ppermute x28, waiting for transfers between devices, swap(): return lax.ppermute(arr, 'ep', [(i, i ^ k) for i in range(ep_size)])  249 us
    pallas_call x5, Pallas kernels, rows_call(): pl.pallas_call(kernel, grid_spec=pltpu.PrefetchScalarGridSpec(num_scalar_...  182 us
    pallas_call x8, Pallas kernels, gather_rows(): pl.pallas_call(functools.partial(gather_kernel, parts, fills, blk, rows,...  177 us
    dot_general x1, matrix products, device_body(): jnp.einsum('sxcd,sxcf->xdf', u_slot, da_slot, preferred_element_type=jnp....  62.2 us
    dot_general x1, matrix products, device_body(): jnp.einsum('sxcf,sxcd->xfd', h_slot, do_slot, preferred_element_type=jnp....  62.1 us
    dot_general x1, matrix products, device_body(): jnp.einsum('sxcd,sxcf->xdf', u_slot, db_slot, preferred_element_type=jnp....  61.7 us
  transfers between devices with their start and end apart: 51, of which 25 were waited for; matrix products, arithmetic and copies ran while one was open for 13% of the time, Pallas kernels for 34%

profile of v2, /device:TPU:0, one launch (start us, length us, event | category | flops | bytes accessed | tf_op | source)
XLA Modules:
  0.0 2142.5 jit_solution(4742042106613814260)
XLA Ops:
  8.1 2.5 collective-permute-start.10
  10.8 3.3 copy.144.idx_ref.refs_10_
  15.6 53.4 %router.1 = (f32[8192,32]{1,0:T(8,128)}, f32[8192,8]{1,0:T(8,128)}, s32[8192,2]{1,0:T(8,128)}, f32[160,640]{1,0:T(8,128)}, f32[8,128]{1,0:T(8,128)}) custom-call(s32[1]{0:T(128)} %bitcast.1.ep_ref, bf16[8192,768]{1,0:T(8,128)(2,1)} %x_ref.3, s32[8192,2]{1,0:T(8,128)} %copy.144.idx_ref.refs_10_, f32[1,768]{1,0:T(1,128)} %reshape.257.scale_ref.refs_14_, ...), custom_call_target="tpu_custom_call" | custom-call | flops 10000000000 | bytes 25165824 | tf_op jit(solution)/shard_map/router/pallas_call | solution.py:163
  71.8 21.8 %gather_rows.8 = bf16[5120,768]{1,0:T(8,128)(2,1)} custom-call(s32[5120]{0:T(1024)} %mul.81.idx_ref, bf16[8192,768]{1,0:T(8,128)(2,1)} %x_ref.3), custom_call_target="tpu_custom_call" | custom-call | flops 40000000000 | bytes 15728640 | tf_op jit(solution)/shard_map/gather_rows/pallas_call | solution.py:227
  95.9 5.9 constant_dynamic-slice_fusion
  101.9 21.8 %gather_rows.9 = bf16[5120,768]{1,0:T(8,128)(2,1)} custom-call(s32[5120]{0:T(1024)} %mul.81.idx_ref, bf16[8192,768]{1,0:T(8,128)(2,1)} %dy_ref.1), custom_call_target="tpu_custom_call" | custom-call | flops 40000000000 | bytes 15728640 | tf_op jit(solution)/shard_map/gather_rows/pallas_call | solution.py:227
  123.7 2.5 shift-right-arithmetic_multiply_fusion
  126.2 51.4 %ffn.8 = (bf16[4,8,640,768]{3,2,1,0:T(8,128)(2,1)}, bf16[4,8,640,768]{3,2,1,0:T(8,128)(2,1)}, bf16[4,8,640,1536]{3,2,1,0:T(8,128)(2,1)}, bf16[4,8,640,1536]{3,2,...) custom-call(s32[1]{0:T(128)} %bitcast.tp_ref, ...), custom_call_target="tpu_custom_call" | custom-call | flops 36238786560 | bytes 47185920 | tf_op jit(solution)/shard_map/ffn/pallas_call | solution.py:408
  180.2 51.4 %ffn.9 = (bf16[4,8,640,768]{3,2,1,0:T(8,128)(2,1)}, bf16[4,8,640,768]{3,2,1,0:T(8,128)(2,1)}, bf16[4,8,640,1536]{3,2,1,0:T(8,128)(2,1)}, bf16[4,8,640,1536]{3,2,...) custom-call(s32[1]{0:T(128)} %bitcast.tp_ref, ...), custom_call_target="tpu_custom_call", output_to_operand_aliasing={{0}: (8, {}), {1}: (9, {}), {2}: (10, {}), {3}: (11, {}), {... | custom-call | flops 36238786560 | bytes 47185920 | tf_op jit(solution)/shard_map/ffn/pallas_call | solution.py:408
  231.7 3.9 slice_reduce_fusion
  242.1 21.8 %gather_rows.10 = bf16[5120,768]{1,0:T(8,128)(2,1)} custom-call(s32[5120]{0:T(1024)} %mul.83.idx_ref, bf16[8192,768]{1,0:T(8,128)(2,1)} %collective-permute-done.4.refs_0_), custom_call_target="tpu_custom_call" | custom-call | flops 40000000000 | bytes 15728640 | tf_op jit(solution)/shard_map/gather_rows/pallas_call | solution.py:227
  263.9 87.1 %collective-permute-done.6.refs_0_ = bf16[2048,768]{1,0:T(8,128)(2,1)} collective-permute-done((bf16[2048,768]{1,0:T(8,128)(2,1)}, bf16[2048,768]{1,0:T(8,128)(2,1)}, u32[]{:S(2)}, u32[]{:S(2)}) %collective-permute-start.6) | collective-permute-done | bytes 3145760 | tf_op jit(solution)/shard_map/ppermute | solution.py:432
  354.3 21.8 %gather_rows.11 = bf16[5120,768]{1,0:T(8,128)(2,1)} custom-call(s32[5120]{0:T(1024)} %mul.83.idx_ref, bf16[8192,768]{1,0:T(8,128)(2,1)} %collective-permute-done.5.refs_0_), custom_call_target="tpu_custom_call" | custom-call | flops 40000000000 | bytes 15728640 | tf_op jit(solution)/shard_map/gather_rows/pallas_call | solution.py:227
  376.1 51.7 %ffn.10 = (bf16[4,8,640,768]{3,2,1,0:T(8,128)(2,1)}, bf16[4,8,640,768]{3,2,1,0:T(8,128)(2,1)}, bf16[4,8,640,1536]{3,2,1,0:T(8,128)(2,1)}, bf16[4,8,640,1536]{3,2...) custom-call(s32[1]{0:T(128)} %bitcast.tp_ref, ...), custom_call_target="tpu_custom_call", output_to_operand_aliasing={{0}: (8, {}), {1}: (9, {}), {2}: (10, {}), {3}: (11, {}), {... | custom-call | flops 36238786560 | bytes 47185920 | tf_op jit(solution)/shard_map/ffn/pallas_call | solution.py:408
  431.7 51.4 %ffn.11 = (bf16[4,8,640,768]{3,2,1,0:T(8,128)(2,1)}, bf16[4,8,640,768]{3,2,1,0:T(8,128)(2,1)}, bf16[4,8,640,1536]{3,2,1,0:T(8,128)(2,1)}, bf16[4,8,640,1536]{3,2...) custom-call(s32[1]{0:T(128)} %bitcast.tp_ref, ...), custom_call_target="tpu_custom_call", output_to_operand_aliasing={{0}: (8, {}), {1}: (9, {}), {2}: (10, {}), {3}: (11, {}), {... | custom-call | flops 36238786560 | bytes 47185920 | tf_op jit(solution)/shard_map/ffn/pallas_call | solution.py:408
  490.8 21.8 %gather_rows.13 = bf16[5120,768]{1,0:T(8,128)(2,1)} custom-call(s32[5120]{0:T(1024)} %mul.88.idx_ref, bf16[8192,768]{1,0:T(8,128)(2,1)} %collective-permute-done.10.refs_0_), custom_call_target="tpu_custom_call" | custom-call | flops 40000000000 | bytes 15728640 | tf_op jit(solution)/shard_map/gather_rows/pallas_call | solution.py:227
  512.6 45.2 %collective-permute-done.9.refs_3_ = bf16[2048,768]{1,0:T(8,128)(2,1)} collective-permute-done((bf16[2048,768]{1,0:T(8,128)(2,1)}, bf16[2048,768]{1,0:T(8,128)(2,1)}, u32[]{:S(2)}, u32[]{:S(2)}) %collective-permute-start.9) | collective-permute-done | bytes 3145760 | tf_op jit(solution)/shard_map/ppermute | solution.py:435
  557.8 23.0 %gather_rows.12 = bf16[5120,768]{1,0:T(8,128)(2,1)} custom-call(s32[5120]{0:T(1024)} %fusion.11.idx_ref, bf16[2048,768]{1,0:T(8,128)(2,1)} %collective-permute-done.6.refs_0_, bf16[2048,768]{1,0:T(8,128)(2,1)} %collective-permute-done.7.refs_1_, bf16[2048,768]{1,0:T(8,128)(2,1)} %collective-permute-done.8.refs_2_, ...), custom_call_target="tpu_custom_call" | custom-call | flops 40000000000 | bytes 15728640 | tf_op jit(solution)/shard_map/gather_rows/pallas_call | solution.py:227
  583.8 51.3 %ffn.12 = (bf16[4,8,640,768]{3,2,1,0:T(8,128)(2,1)}, bf16[4,8,640,768]{3,2,1,0:T(8,128)(2,1)}, bf16[4,8,640,1536]{3,2,1,0:T(8,128)(2,1)}, bf16[4,8,640,1536]{3,2...) custom-call(s32[1]{0:T(128)} %bitcast.tp_ref, ...), custom_call_target="tpu_custom_call", output_to_operand_aliasing={{0}: (8, {}), {1}: (9, {}), {2}: (10, {}), {3}: (11, {}), {... | custom-call | flops 36238786560 | bytes 47185920 | tf_op jit(solution)/shard_map/ffn/pallas_call | solution.py:408
  639.5 51.6 %ffn.13 = (bf16[4,8,640,768]{3,2,1,0:T(8,128)(2,1)}, bf16[4,8,640,768]{3,2,1,0:T(8,128)(2,1)}, bf16[4,8,640,1536]{3,2,1,0:T(8,128)(2,1)}, bf16[4,8,640,1536]{3,2...) custom-call(s32[1]{0:T(128)} %bitcast.tp_ref, ...), custom_call_target="tpu_custom_call", output_to_operand_aliasing={{0}: (8, {}), {1}: (9, {}), {2}: (10, {}), {3}: (11, {}), {... | custom-call | flops 36238786560 | bytes 47185920 | tf_op jit(solution)/shard_map/ffn/pallas_call | solution.py:408
  703.1 22.9 %gather_rows.14 = bf16[5120,768]{1,0:T(8,128)(2,1)} custom-call(s32[5120]{0:T(1024)} %fusion.15.idx_ref, bf16[2048,768]{1,0:T(8,128)(2,1)} %collective-permute-done.11.refs_0_, bf16[2048,768]{1,0:T(8,128)(2,1)} %collective-permute-done.12.refs_1_, bf16[2048,768]{1,0:T(8,128)(2,1)} %collective-permute-done.13.refs_2_, ...), custom_call_target="tpu_custom_call" | custom-call | flops 40000000000 | bytes 15728640 | tf_op jit(solution)/shard_map/gather_rows/pallas_call | solution.py:227
  727.5 21.8 %gather_rows.15 = bf16[5120,768]{1,0:T(8,128)(2,1)} custom-call(s32[5120]{0:T(1024)} %mul.92.idx_ref, bf16[8192,768]{1,0:T(8,128)(2,1)} %collective-permute-done.15.refs_0_), custom_call_target="tpu_custom_call" | custom-call | flops 40000000000 | bytes 15728640 | tf_op jit(solution)/shard_map/gather_rows/pallas_call | solution.py:227
  749.3 51.5 %ffn.14 = (bf16[4,8,640,768]{3,2,1,0:T(8,128)(2,1)}, bf16[4,8,640,768]{3,2,1,0:T(8,128)(2,1)}, bf16[4,8,640,1536]{3,2,1,0:T(8,128)(2,1)}, bf16[4,8,640,1536]{3,2...) custom-call(s32[1]{0:T(128)} %bitcast.tp_ref, ...), custom_call_target="tpu_custom_call", output_to_operand_aliasing={{0}: (8, {}), {1}: (9, {}), {2}: (10, {}), {3}: (11, {}), {... | custom-call | flops 36238786560 | bytes 47185920 | tf_op jit(solution)/shard_map/ffn/pallas_call | solution.py:408
  804.8 51.4 %ffn.15 = (bf16[4,8,640,768]{3,2,1,0:T(8,128)(2,1)}, bf16[4,8,640,768]{3,2,1,0:T(8,128)(2,1)}, bf16[4,8,640,1536]{3,2,1,0:T(8,128)(2,1)}, bf16[4,8,640,1536]{3,2...) custom-call(s32[1]{0:T(128)} %bitcast.tp_ref, ...), custom_call_target="tpu_custom_call", output_to_operand_aliasing={{0}: (8, {}), {1}: (9, {}), {2}: (10, {}), {3}: (11, {}), {... | custom-call | flops 36238786560 | bytes 47185920 | tf_op jit(solution)/shard_map/ffn/pallas_call | solution.py:408
  860.0 62.2 %convolution_bitcast_fusion.1 = f32[8,768,1536]{2,1,0:T(8,128)} fusion(bf16[4,8,640,768]{3,2,1,0:T(8,128)(2,1)} %get-tuple-element.190, bf16[4,8,640,1536]{3,2,1,0:T(8,128)(2,1)} %get-tuple-element.191), kind=kOutput, calls=%fused_computation.1 | convolution fusion | flops 48318382080 | bytes 132120576 | tf_op jit(solution)/shard_map/sxcd,sxcf->xdf/dot_general | solution.py:495
  926.8 61.7 %convolution_bitcast_fusion = f32[8,768,1536]{2,1,0:T(8,128)} fusion(bf16[4,8,640,768]{3,2,1,0:T(8,128)(2,1)} %get-tuple-element.190, bf16[4,8,640,1536]{3,2,1,0:T(8,128)(2,1)} %get-tuple-element.227), kind=kOutput, calls=%fused_computation | convolution fusion | flops 48318382080 | bytes 132120576 | tf_op jit(solution)/shard_map/sxcd,sxcf->xdf/dot_general | solution.py:496
  990.0 20.3 collective-permute-done.35
  1010.9 41.6 %collective-permute-done.17 = bf16[4,640,384]{2,1,0:T(8,128)(2,1)} collective-permute-done((bf16[4,640,384]{2,1,0:T(8,128)(2,1)}, bf16[4,640,384]{2,1,0:T(8,128)(2,1)}, u32[]{:S(2)}, u32[]{:S(2)}) %collective-permute-start.17) | collective-permute-done | bytes 1966112 | tf_op jit(solution)/shard_map/ppermute | solution.py:435
  1053.0 41.6 %collective-permute-done.19 = bf16[4,640,384]{2,1,0:T(8,128)(2,1)} collective-permute-done((bf16[4,640,384]{2,1,0:T(8,128)(2,1)}, bf16[4,640,384]{2,1,0:T(8,128)(2,1)}, u32[]{:S(2)}, u32[]{:S(2)}) %collective-permute-start.19) | collective-permute-done | bytes 1966112 | tf_op jit(solution)/shard_map/ppermute | solution.py:435
  1095.1 41.6 %collective-permute-done.21 = bf16[4,640,384]{2,1,0:T(8,128)(2,1)} collective-permute-done((bf16[4,640,384]{2,1,0:T(8,128)(2,1)}, bf16[4,640,384]{2,1,0:T(8,128)(2,1)}, u32[]{:S(2)}, u32[]{:S(2)}) %collective-permute-start.21) | collective-permute-done | bytes 1966112 | tf_op jit(solution)/shard_map/ppermute | solution.py:435
  1137.3 62.1 %convolution_bitcast_fusion.2 = f32[8,1536,768]{2,1,0:T(8,128)} fusion(bf16[4,8,640,1536]{3,2,1,0:T(8,128)(2,1)} %get-tuple-element.205, bf16[4,8,640,768]{3,2,1,0:T(8,128)(2,1)} %get-tuple-element.206), kind=kOutput, calls=%fused_computation.2 | convolution fusion | flops 48318382080 | bytes 132120576 | tf_op jit(solution)/shard_map/sxcf,sxcd->xfd/dot_general | solution.py:497
  1199.3 4.0 add_convert_fusion.15
  1203.4 3.6 add_convert_fusion.14
  1212.9 8.1 collective-permute-done.26
  1221.5 41.6 %collective-permute-done.36 = bf16[4,640,384]{2,1,0:T(8,128)(2,1)} collective-permute-done((bf16[4,640,384]{2,1,0:T(8,128)(2,1)}, bf16[4,640,384]{2,1,0:T(8,128)(2,1)}, u32[]{:S(2)}, u32[]{:S(2)}) %collective-permute-start.36) | collective-permute-done | bytes 1966112 | tf_op jit(solution)/shard_map/ppermute | solution.py:435
  1263.2 42.1 %collective-permute-done.38 = bf16[4,640,384]{2,1,0:T(8,128)(2,1)} collective-permute-done((bf16[4,640,384]{2,1,0:T(8,128)(2,1)}, bf16[4,640,384]{2,1,0:T(8,128)(2,1)}, u32[]{:S(2)}, u32[]{:S(2)}) %collective-permute-start.38) | collective-permute-done | bytes 1966112 | tf_op jit(solution)/shard_map/ppermute | solution.py:435
  1305.3 42.1 %collective-permute-done.25 = bf16[4,640,384]{2,1,0:T(8,128)(2,1)} collective-permute-done((bf16[4,640,384]{2,1,0:T(8,128)(2,1)}, bf16[4,640,384]{2,1,0:T(8,128)(2,1)}, u32[]{:S(2)}, u32[]{:S(2)}) %collective-permute-start.25) | collective-permute-done | bytes 1966112 | tf_op jit(solution)/shard_map/ppermute | solution.py:435
  1352.1 3.4 add_convert_fusion.7
  1355.5 3.5 add_convert_fusion.6
  1359.0 30.4 %collective-permute-done.28 = bf16[4,640,384]{2,1,0:T(8,128)(2,1)S(1)} collective-permute-done((bf16[4,640,384]{2,1,0:T(8,128)(2,1)S(1)}, bf16[4,640,384]{2,1,0:T(8,128)(2,1)S(1)}, u32[]{:S(2)}, u32[]{:S(2)}) %collective-permute-start.28) | collective-permute-done | bytes 1966112 | tf_op jit(solution)/shard_map/ppermute | solution.py:435
  1392.6 39.0 %collective-permute-done.40 = bf16[4,640,384]{2,1,0:T(8,128)(2,1)S(1)} collective-permute-done((bf16[4,640,384]{2,1,0:T(8,128)(2,1)S(1)}, bf16[4,640,384]{2,1,0:T(8,128)(2,1)S(1)}, u32[]{:S(2)}, u32[]{:S(2)}) %collective-permute-start.40) | collective-permute-done | bytes 1966112 | tf_op jit(solution)/shard_map/ppermute | solution.py:435
  1433.6 40.1 %collective-permute-done.43 = bf16[4,640,384]{2,1,0:T(8,128)(2,1)S(1)} collective-permute-done((bf16[4,640,384]{2,1,0:T(8,128)(2,1)S(1)}, bf16[4,640,384]{2,1,0:T(8,128)(2,1)S(1)}, u32[]{:S(2)}, u32[]{:S(2)}) %collective-permute-start.43) | collective-permute-done | bytes 1966112 | tf_op jit(solution)/shard_map/ppermute | solution.py:435
  1473.7 3.4 add_convert_fusion.5
  1477.1 3.5 add_convert_fusion.4
  1482.4 3.5 add_convert_fusion.2
  1486.0 28.7 %collective-permute-done.45 = bf16[4,640,384]{2,1,0:T(8,128)(2,1)S(1)} collective-permute-done((bf16[4,640,384]{2,1,0:T(8,128)(2,1)S(1)}, bf16[4,640,384]{2,1,0:T(8,128)(2,1)S(1)}, u32[]{:S(2)}, u32[]{:S(2)}) %collective-permute-start.45) | collective-permute-done | bytes 1966112 | tf_op jit(solution)/shard_map/ppermute | solution.py:435
  1519.9 39.6 %collective-permute-done.27 = bf16[4,640,384]{2,1,0:T(8,128)(2,1)S(1)} collective-permute-done((bf16[4,640,384]{2,1,0:T(8,128)(2,1)S(1)}, bf16[4,640,384]{2,1,0:T(8,128)(2,1)S(1)}, u32[]{:S(2)}, u32[]{:S(2)}) %collective-permute-start.27) | collective-permute-done | bytes 1966112 | tf_op jit(solution)/shard_map/ppermute | solution.py:432
  1561.1 40.6 %collective-permute-done.29 = bf16[4,640,384]{2,1,0:T(8,128)(2,1)S(1)} collective-permute-done((bf16[4,640,384]{2,1,0:T(8,128)(2,1)S(1)}, bf16[4,640,384]{2,1,0:T(8,128)(2,1)S(1)}, u32[]{:S(2)}, u32[]{:S(2)}) %collective-permute-start.29) | collective-permute-done | bytes 1966112 | tf_op jit(solution)/shard_map/ppermute | solution.py:432
  1603.0 65.2 %shard_map.143 = (bf16[8192,384]{1,0:T(8,128)(2,1)}, f32[8192,2]{1,0:T(8,128)}) custom-call(s32[1]{0:T(128)} %bitcast.tp_ref, s32[8192]{0:T(1024)} %get-tuple-element.283.first_ref, s32[8192]{0:T(1024)} %get-tuple-element.282.second_ref, bf16[2560,384]{1,0:T(8,128)(2,1)} %bitcast.105, bf16[2560,384]{1,0:T(8,128)(2,1)} %bitcast.106, ...), custom_call_target="tpu_custom_call" | custom-call | flops 10000000000 | bytes 41025536 | tf_op jit(solution)/shard_map/pallas_call | solution.py:370
  1668.2 3.0 copy.157
  1671.5 3.4 add_convert_fusion
  1677.2 2.9 copy.158
  1680.2 5.9 add_bitcast_fusion.refs_11_
  1688.0 40.2 %collective-permute-done.44 = bf16[4,640,384]{2,1,0:T(8,128)(2,1)S(1)} collective-permute-done((bf16[4,640,384]{2,1,0:T(8,128)(2,1)}, bf16[4,640,384]{2,1,0:T(8,128)(2,1)S(1)}, u32[]{:S(2)}, u32[]{:S(2)}) %collective-permute-start.44) | collective-permute-done | bytes 1966112 | tf_op jit(solution)/shard_map/ppermute | solution.py:432
  1728.2 38.8 %collective-permute-done.46 = bf16[4,640,384]{2,1,0:T(8,128)(2,1)} collective-permute-done((bf16[4,640,384]{2,1,0:T(8,128)(2,1)}, bf16[4,640,384]{2,1,0:T(8,128)(2,1)}, u32[]{:S(2)}, u32[]{:S(2)}) %collective-permute-start.46) | collective-permute-done | bytes 1966112 | tf_op jit(solution)/shard_map/ppermute | solution.py:432
  1767.1 78.2 %shard_map.145 = (f32[8192,384]{1,0:T(8,128)}, f32[8192,1]{1,0:T(8,128)}, f32[1,384]{1,0:T(1,128)}, f32[384,32]{1,0:T(8,128)}) custom-call(s32[1]{0:T(128)} %bitcast.tp_ref, s32[8192]{0:T(1024)} %get-tuple-element.283.first_ref, s32[8192]{0:T(1024)} %get-tuple-element.282.second_ref, bf16[2560,384]{1,0:T(8,128)(2,1)} %bitcast.103, ...), custom_call_target="tpu_custom_call" | custom-call | flops 10000000000 | bytes 29083200 | tf_op jit(solution)/shard_map/pallas_call | solution.py:370
  1845.3 3.3 reduce.3
  1852.6 2.7 copy.161.mix_ref
  1855.3 15.1 shard_map.146.own_ref
  1875.0 42.1 %all-reduce.2.cloned.1.call-done = f32[2,12672]{1,0:T(2,128)} async-done(((f32[2,12672]{1,0:T(2,128)}), f32[2,12672]{1,0:T(2,128)}) %all-reduce.2.cloned.1.call-update) | async-done | bytes 101392 | tf_op jit(solution)/shard_map/psum | solution.py:567
  1920.3 68.5 %collective-permute-done.30.other_ref = bf16[8192,384]{1,0:T(8,128)(2,1)} collective-permute-done((bf16[8192,384]{1,0:T(8,128)(2,1)}, bf16[8192,384]{1,0:T(8,128)(2,1)}, u32[]{:S(2)}, u32[]{:S(2)}) %collective-permute-start.30) | collective-permute-done | bytes 6291488 | tf_op jit(solution)/shard_map/ppermute | solution.py:435
  1988.8 11.5 shard_map.144
  2000.3 123.4 %collective-permute-done.49.other_ref = bf16[8192,384]{1,0:T(8,128)(2,1)} collective-permute-done((bf16[8192,384]{1,0:T(8,128)(2,1)}, bf16[8192,384]{1,0:T(8,128)(2,1)}, u32[]{:S(2)}, u32[]{:S(2)}) %collective-permute-start.49) | collective-permute-done | bytes 6291488 | tf_op jit(solution)/shard_map/ppermute | solution.py:435
  2123.6 11.5 shard_map.147
  (245 shorter events, 109.1 us)
Async XLA Ops:
  7.2 1909.9 %all-reduce.2.cloned.1.call-start = ((), (), s32[]{:S(2)}) async-start(), calls=%async_computation | async-start | bytes 202752 | tf_op jit(solution)/shard_map/psum | solution.py:567
  7.2 345.6 %collective-permute-start.5 = (bf16[8192,768]{1,0:T(8,128)(2,1)}, bf16[8192,768]{1,0:T(8,128)(2,1)}, u32[]{:S(2)}, u32[]{:S(2)}) collective-permute-start(bf16[8192,768]{1,0:T(8,128)(2,1)} %dy_ref.1), channel_id=1, source_target_pairs={{0,1},{1,0},{2,3},{3,2},{4,5},{5,4},{6,7},{7,6}} | collective-permute-start | bytes 37748744 | tf_op jit(solution)/shard_map/ppermute | solution.py:432
  8.1 482.4 %collective-permute-start.10 = (bf16[8192,768]{1,0:T(8,128)(2,1)}, bf16[8192,768]{1,0:T(8,128)(2,1)}, u32[]{:S(2)}, u32[]{:S(2)}) collective-permute-start(bf16[8192,768]{1,0:T(8,128)(2,1)} %dy_ref.1), channel_id=1, source_target_pairs={{0,2},{1,3},{2,0},{3,1},{4,6},{5,7},{6,4},{7,5}} | collective-permute-start | bytes 37748744 | tf_op jit(solution)/shard_map/ppermute | solution.py:432
  10.6 231.2 %collective-permute-start.4 = (bf16[8192,768]{1,0:T(8,128)(2,1)}, bf16[8192,768]{1,0:T(8,128)(2,1)}, u32[]{:S(2)}, u32[]{:S(2)}) collective-permute-start(bf16[8192,768]{1,0:T(8,128)(2,1)} %x_ref.3), channel_id=1, source_target_pairs={{0,1},{1,0},{2,3},{3,2},{4,5},{5,4},{6,7},{7,6}} | collective-permute-start | bytes 37748744 | tf_op jit(solution)/shard_map/ppermute | solution.py:432
  70.8 568.2 %collective-permute-start.1 = (f32[8,2,640]{2,0,1:T(8,128)}, f32[8,2,640]{2,0,1:T(8,128)}, u32[]{:S(2)}, u32[]{:S(2)}) collective-permute-start(f32[8,2,640]{2,0,1:T(8,128)} %get-tuple-element.289), channel_id=1, source_target_pairs={{0,3},{1,2},{2,1},{3,0},{4,7},{5,6},{6,5},{7,4}} | collective-permute-start | bytes 122888 | tf_op jit(solution)/shard_map/ppermute | solution.py:432
  70.8 164.8 %collective-permute-start.3 = (f32[8,2,640]{2,0,1:T(8,128)}, f32[8,2,640]{2,0,1:T(8,128)}, u32[]{:S(2)}, u32[]{:S(2)}) collective-permute-start(f32[8,2,640]{2,0,1:T(8,128)} %get-tuple-element.288), channel_id=1, source_target_pairs={{0,1},{1,0},{2,3},{3,2},{4,5},{5,4},{6,7},{7,6}} | collective-permute-start | bytes 122888 | tf_op jit(solution)/shard_map/ppermute | solution.py:432
  235.6 251.3 %collective-permute-start.2 = (f32[8,2,640]{2,0,1:T(8,128)}, f32[8,2,640]{2,0,1:T(8,128)}, u32[]{:S(2)}, u32[]{:S(2)}) collective-permute-start(f32[8,2,640]{2,0,1:T(8,128)} %get-tuple-element.290), channel_id=1, source_target_pairs={{0,2},{1,3},{2,0},{3,1},{4,6},{5,7},{6,4},{7,5}} | collective-permute-start | bytes 122888 | tf_op jit(solution)/shard_map/ppermute | solution.py:432
  241.8 109.2 %collective-permute-start.6 = (bf16[2048,768]{1,0:T(8,128)(2,1)}, bf16[2048,768]{1,0:T(8,128)(2,1)}, u32[]{:S(2)}, u32[]{:S(2)}) collective-permute-start(bf16[2048,768]{1,0:T(8,128)(2,1)} %get-tuple-element.287), channel_id=1, source_target_pairs={{0,2},{1,3},{2,0},{3,1},{4,6},{5,7},{6,4},{7,5}} | collective-permute-start | bytes 9437192 | tf_op jit(solution)/shard_map/ppermute | solution.py:432
  351.1 135.9 %collective-permute-start.7 = (bf16[2048,768]{1,0:T(8,128)(2,1)}, bf16[2048,768]{1,0:T(8,128)(2,1)}, u32[]{:S(2)}, u32[]{:S(2)}) collective-permute-start(bf16[2048,768]{1,0:T(8,128)(2,1)} %get-tuple-element.286), channel_id=1, source_target_pairs={{0,2},{1,3},{2,0},{3,1},{4,6},{5,7},{6,4},{7,5}} | collective-permute-start | bytes 9437192 | tf_op jit(solution)/shard_map/ppermute | solution.py:432
  352.8 137.4 %collective-permute-start.8 = (bf16[2048,768]{1,0:T(8,128)(2,1)}, bf16[2048,768]{1,0:T(8,128)(2,1)}, u32[]{:S(2)}, u32[]{:S(2)}) collective-permute-start(bf16[2048,768]{1,0:T(8,128)(2,1)} %collective-permute-done.6.refs_0_), channel_id=1, source_target_pairs={{0,4},{4,0},{1,5},{5,1},{2,6},{6,2},{3,7},{7,3}} | collective-permute-start | bytes 9437192 | tf_op jit(solution)/shard_map/ppermute | solution.py:435
  486.9 213.8 %collective-permute-start.11 = (bf16[2048,768]{1,0:T(8,128)(2,1)}, bf16[2048,768]{1,0:T(8,128)(2,1)}, u32[]{:S(2)}, u32[]{:S(2)}) collective-permute-start(bf16[2048,768]{1,0:T(8,128)(2,1)} %collective-permute-done.6.refs_0_), channel_id=1, source_target_pairs={{0,1},{1,0},{2,3},{3,2},{4,5},{5,4},{6,7},{7,6}} | collective-permute-start | bytes 9437192 | tf_op jit(solution)/shard_map/ppermute | solution.py:432
  486.9 70.8 %collective-permute-start.9 = (bf16[2048,768]{1,0:T(8,128)(2,1)}, bf16[2048,768]{1,0:T(8,128)(2,1)}, u32[]{:S(2)}, u32[]{:S(2)}) collective-permute-start(bf16[2048,768]{1,0:T(8,128)(2,1)} %collective-permute-done.7.refs_1_), channel_id=1, source_target_pairs={{0,4},{4,0},{1,5},{5,1},{2,6},{6,2},{3,7},{7,3}} | collective-permute-start | bytes 9437192 | tf_op jit(solution)/shard_map/ppermute | solution.py:435
  490.2 210.5 %collective-permute-start.12 = (bf16[2048,768]{1,0:T(8,128)(2,1)}, bf16[2048,768]{1,0:T(8,128)(2,1)}, u32[]{:S(2)}, u32[]{:S(2)}) collective-permute-start(bf16[2048,768]{1,0:T(8,128)(2,1)} %collective-permute-done.7.refs_1_), channel_id=1, source_target_pairs={{0,1},{1,0},{2,3},{3,2},{4,5},{5,4},{6,7},{7,6}} | collective-permute-start | bytes 9437192 | tf_op jit(solution)/shard_map/ppermute | solution.py:432
  490.4 210.9 %collective-permute-start.13 = (bf16[2048,768]{1,0:T(8,128)(2,1)}, bf16[2048,768]{1,0:T(8,128)(2,1)}, u32[]{:S(2)}, u32[]{:S(2)}) collective-permute-start(bf16[2048,768]{1,0:T(8,128)(2,1)} %collective-permute-done.8.refs_2_), channel_id=1, source_target_pairs={{0,1},{1,0},{2,3},{3,2},{4,5},{5,4},{6,7},{7,6}} | collective-permute-start | bytes 9437192 | tf_op jit(solution)/shard_map/ppermute | solution.py:432
  557.8 168.2 %collective-permute-start.15 = (bf16[8192,768]{1,0:T(8,128)(2,1)}, bf16[8192,768]{1,0:T(8,128)(2,1)}, u32[]{:S(2)}, u32[]{:S(2)}) collective-permute-start(bf16[8192,768]{1,0:T(8,128)(2,1)} %collective-permute-done.10.refs_0_), channel_id=1, source_target_pairs={{0,1},{1,0},{2,3},{3,2},{4,5},{5,4},{6,7},{7,6}} | collective-permute-start | bytes 37748744 | tf_op jit(solution)/shard_map/ppermute | solution.py:432
  639.0 63.7 %collective-permute-start.14 = (bf16[2048,768]{1,0:T(8,128)(2,1)}, bf16[2048,768]{1,0:T(8,128)(2,1)}, u32[]{:S(2)}, u32[]{:S(2)}) collective-permute-start(bf16[2048,768]{1,0:T(8,128)(2,1)} %collective-permute-done.9.refs_3_), channel_id=1, source_target_pairs={{0,1},{1,0},{2,3},{3,2},{4,5},{5,4},{6,7},{7,6}} | collective-permute-start | bytes 9437192 | tf_op jit(solution)/shard_map/ppermute | solution.py:432
  700.7 221.5 %collective-permute-start.31 = (f32[8,128]{1,0:T(8,128)}, f32[8,128]{1,0:T(8,128)}, u32[]{:S(2)}, u32[]{:S(2)}) collective-permute-start(f32[8,128]{1,0:T(8,128)} %get-tuple-element.199), channel_id=1, source_target_pairs={{0,1},{1,0},{2,3},{3,2},{4,5},{5,4},{6,7},{7,6}} | collective-permute-start | bytes 12296 | tf_op jit(solution)/shard_map/ppermute | solution.py:432
  700.8 222.0 %collective-permute-start.32 = (f32[8,128]{1,0:T(8,128)}, f32[8,128]{1,0:T(8,128)}, u32[]{:S(2)}, u32[]{:S(2)}) collective-permute-start(f32[8,128]{1,0:T(8,128)} %get-tuple-element.199), channel_id=1, source_target_pairs={{0,2},{1,3},{2,0},{3,1},{4,6},{5,7},{6,4},{7,5}} | collective-permute-start | bytes 12296 | tf_op jit(solution)/shard_map/ppermute | solution.py:432
  701.3 222.9 %collective-permute-start.33 = (f32[8,128]{1,0:T(8,128)}, f32[8,128]{1,0:T(8,128)}, u32[]{:S(2)}, u32[]{:S(2)}) collective-permute-start(f32[8,128]{1,0:T(8,128)} %get-tuple-element.199), channel_id=1, source_target_pairs={{0,3},{1,2},{2,1},{3,0},{4,7},{5,6},{6,5},{7,4}} | collective-permute-start | bytes 12296 | tf_op jit(solution)/shard_map/ppermute | solution.py:432
  702.6 222.1 %collective-permute-start = (bf16[4,640,384]{2,1,0:T(8,128)(2,1)}, bf16[4,640,384]{2,1,0:T(8,128)(2,1)}, u32[]{:S(2)}, u32[]{:S(2)}) collective-permute-start(bf16[4,640,384]{2,1,0:T(8,128)(2,1)} %copy-done.30), channel_id=1, source_target_pairs={{0,4},{4,0},{1,5},{5,1},{2,6},{6,2},{3,7},{7,3}} | collective-permute-start | bytes 5898248 | tf_op jit(solution)/shard_map/ppermute | solution.py:435
  726.0 200.3 %collective-permute-start.16 = (bf16[4,640,384]{2,1,0:T(8,128)(2,1)}, bf16[4,640,384]{2,1,0:T(8,128)(2,1)}, u32[]{:S(2)}, u32[]{:S(2)}) collective-permute-start(bf16[4,640,384]{2,1,0:T(8,128)(2,1)} %copy-done.31), channel_id=1, source_target_pairs={{0,4},{4,0},{1,5},{5,1},{2,6},{6,2},{3,7},{7,3}} | collective-permute-start | bytes 5898248 | tf_op jit(solution)/shard_map/ppermute | solution.py:435
  922.2 66.3 %collective-permute-start.34 = (bf16[4,640,384]{2,1,0:T(8,128)(2,1)}, bf16[4,640,384]{2,1,0:T(8,128)(2,1)}, u32[]{:S(2)}, u32[]{:S(2)}) collective-permute-start(bf16[4,640,384]{2,1,0:T(8,128)(2,1)} %get-tuple-element.204), channel_id=1, source_target_pairs={{0,4},{4,0},{1,5},{5,1},{2,6},{6,2},{3,7},{7,3}} | collective-permute-start | bytes 5898248 | tf_op jit(solution)/shard_map/ppermute | solution.py:435
  922.7 87.6 %collective-permute-start.35 = (bf16[4,640,384]{2,1,0:T(8,128)(2,1)}, bf16[4,640,384]{2,1,0:T(8,128)(2,1)}, u32[]{:S(2)}, u32[]{:S(2)}) collective-permute-start(bf16[4,640,384]{2,1,0:T(8,128)(2,1)} %get-tuple-element.209), channel_id=1, source_target_pairs={{0,4},{4,0},{1,5},{5,1},{2,6},{6,2},{3,7},{7,3}} | collective-permute-start | bytes 5898248 | tf_op jit(solution)/shard_map/ppermute | solution.py:435
  924.3 128.2 %collective-permute-start.17 = (bf16[4,640,384]{2,1,0:T(8,128)(2,1)}, bf16[4,640,384]{2,1,0:T(8,128)(2,1)}, u32[]{:S(2)}, u32[]{:S(2)}) collective-permute-start(bf16[4,640,384]{2,1,0:T(8,128)(2,1)} %copy-done.32), channel_id=1, source_target_pairs={{0,4},{4,0},{1,5},{5,1},{2,6},{6,2},{3,7},{7,3}} | collective-permute-start | bytes 5898248 | tf_op jit(solution)/shard_map/ppermute | solution.py:435
  924.8 169.9 %collective-permute-start.19 = (bf16[4,640,384]{2,1,0:T(8,128)(2,1)}, bf16[4,640,384]{2,1,0:T(8,128)(2,1)}, u32[]{:S(2)}, u32[]{:S(2)}) collective-permute-start(bf16[4,640,384]{2,1,0:T(8,128)(2,1)} %copy-done.33), channel_id=1, source_target_pairs={{0,4},{4,0},{1,5},{5,1},{2,6},{6,2},{3,7},{7,3}} | collective-permute-start | bytes 5898248 | tf_op jit(solution)/shard_map/ppermute | solution.py:435
  926.3 210.5 %collective-permute-start.21 = (bf16[4,640,384]{2,1,0:T(8,128)(2,1)}, bf16[4,640,384]{2,1,0:T(8,128)(2,1)}, u32[]{:S(2)}, u32[]{:S(2)}) collective-permute-start(bf16[4,640,384]{2,1,0:T(8,128)(2,1)} %copy-done.34), channel_id=1, source_target_pairs={{0,4},{4,0},{1,5},{5,1},{2,6},{6,2},{3,7},{7,3}} | collective-permute-start | bytes 5898248 | tf_op jit(solution)/shard_map/ppermute | solution.py:435
  988.5 218.5 %collective-permute-start.23 = (bf16[4,640,384]{2,1,0:T(8,128)(2,1)}, bf16[4,640,384]{2,1,0:T(8,128)(2,1)}, u32[]{:S(2)}, u32[]{:S(2)}) collective-permute-start(bf16[4,640,384]{2,1,0:T(8,128)(2,1)} %copy-done.35), channel_id=1, source_target_pairs={{0,4},{4,0},{1,5},{5,1},{2,6},{6,2},{3,7},{7,3}} | collective-permute-start | bytes 5898248 | tf_op jit(solution)/shard_map/ppermute | solution.py:435
  1010.4 210.7 %collective-permute-start.26 = (bf16[4,640,384]{2,1,0:T(8,128)(2,1)}, bf16[4,640,384]{2,1,0:T(8,128)(2,1)}, u32[]{:S(2)}, u32[]{:S(2)}) collective-permute-start(bf16[4,640,384]{2,1,0:T(8,128)(2,1)} %get-tuple-element.189), channel_id=1, source_target_pairs={{0,4},{4,0},{1,5},{5,1},{2,6},{6,2},{3,7},{7,3}} | collective-permute-start | bytes 5898248 | tf_op jit(solution)/shard_map/ppermute | solution.py:435
  1052.5 210.7 %collective-permute-start.36 = (bf16[4,640,384]{2,1,0:T(8,128)(2,1)}, bf16[4,640,384]{2,1,0:T(8,128)(2,1)}, u32[]{:S(2)}, u32[]{:S(2)}) collective-permute-start(bf16[4,640,384]{2,1,0:T(8,128)(2,1)} %get-tuple-element.213), channel_id=1, source_target_pairs={{0,4},{4,0},{1,5},{5,1},{2,6},{6,2},{3,7},{7,3}} | collective-permute-start | bytes 5898248 | tf_op jit(solution)/shard_map/ppermute | solution.py:435
  1094.6 210.7 %collective-permute-start.38 = (bf16[4,640,384]{2,1,0:T(8,128)(2,1)}, bf16[4,640,384]{2,1,0:T(8,128)(2,1)}, u32[]{:S(2)}, u32[]{:S(2)}) collective-permute-start(bf16[4,640,384]{2,1,0:T(8,128)(2,1)} %get-tuple-element.217), channel_id=1, source_target_pairs={{0,4},{4,0},{1,5},{5,1},{2,6},{6,2},{3,7},{7,3}} | collective-permute-start | bytes 5898248 | tf_op jit(solution)/shard_map/ppermute | solution.py:435
  1136.8 210.7 %collective-permute-start.25 = (bf16[4,640,384]{2,1,0:T(8,128)(2,1)}, bf16[4,640,384]{2,1,0:T(8,128)(2,1)}, u32[]{:S(2)}, u32[]{:S(2)}) collective-permute-start(bf16[4,640,384]{2,1,0:T(8,128)(2,1)} %copy-done.38), channel_id=1, source_target_pairs={{0,4},{4,0},{1,5},{5,1},{2,6},{6,2},{3,7},{7,3}} | collective-permute-start | bytes 5898248 | tf_op jit(solution)/shard_map/ppermute | solution.py:435
  1207.0 182.5 %collective-permute-start.28 = (bf16[4,640,384]{2,1,0:T(8,128)(2,1)S(1)}, bf16[4,640,384]{2,1,0:T(8,128)(2,1)S(1)}, u32[]{:S(2)}, u32[]{:S(2)}) collective-permute-start(bf16[4,640,384]{2,1,0:T(8,128)(2,1)S(1)} %copy-done.37), channel_id=1, source_target_pairs={{0,4},{4,0},{1,5},{5,1},{2,6},{6,2},{3,7},{7,3}} | collective-permute-start | bytes 5898248 | tf_op jit(solution)/shard_map/ppermute | solution.py:435
  1210.6 136.8 %copy-start.54 = (bf16[4,640,384]{2,1,0:T(8,128)(2,1)S(1)}, bf16[4,640,384]{2,1,0:T(8,128)(2,1)}, u32[]{:S(2)}) copy-start(bf16[4,640,384]{2,1,0:T(8,128)(2,1)} %get-tuple-element.226) | copy-start | bytes 5898244
  1210.6 137.3 %copy-start.20 = (bf16[4,640,384]{2,1,0:T(8,128)(2,1)S(1)}, bf16[4,640,384]{2,1,0:T(8,128)(2,1)}, u32[]{:S(2)}) copy-start(bf16[4,640,384]{2,1,0:T(8,128)(2,1)} %copy-done.19) | copy-start | bytes 5898244
  1212.9 137.1 %copy-start.22 = (bf16[4,640,384]{2,1,0:T(8,128)(2,1)S(1)}, bf16[4,640,384]{2,1,0:T(8,128)(2,1)}, u32[]{:S(2)}) copy-start(bf16[4,640,384]{2,1,0:T(8,128)(2,1)} %copy-done.21) | copy-start | bytes 5898244
  1221.0 210.6 %collective-permute-start.40 = (bf16[4,640,384]{2,1,0:T(8,128)(2,1)S(1)}, bf16[4,640,384]{2,1,0:T(8,128)(2,1)S(1)}, u32[]{:S(2)}, u32[]{:S(2)}) collective-permute-start(bf16[4,640,384]{2,1,0:T(8,128)(2,1)S(1)} %copy-done.52), channel_id=1, source_target_pairs={{0,4},{4,0},{1,5},{5,1},{2,6},{6,2},{3,7},{7,3}} | collective-permute-start | bytes 5898248 | tf_op jit(solution)/shard_map/ppermute | solution.py:435
  1263.2 169.0 %collective-permute-start.18 = (bf16[4,640,384]{2,1,0:T(8,128)(2,1)S(1)}, bf16[4,640,384]{2,1,0:T(8,128)(2,1)S(1)}, u32[]{:S(2)}, u32[]{:S(2)}) collective-permute-start(bf16[4,640,384]{2,1,0:T(8,128)(2,1)S(1)} %add_convert_fusion.13), channel_id=1, source_target_pairs={{0,1},{1,0},{2,3},{3,2},{4,5},{5,4},{6,7},{7,6}} | collective-permute-start | bytes 5898248 | tf_op jit(solution)/shard_map/ppermute | solution.py:432
  1305.3 128.3 %collective-permute-start.20 = (bf16[4,640,384]{2,1,0:T(8,128)(2,1)S(1)}, bf16[4,640,384]{2,1,0:T(8,128)(2,1)S(1)}, u32[]{:S(2)}, u32[]{:S(2)}) collective-permute-start(bf16[4,640,384]{2,1,0:T(8,128)(2,1)S(1)} %add_convert_fusion.12), channel_id=1, source_target_pairs={{0,1},{1,0},{2,3},{3,2},{4,5},{5,4},{6,7},{7,6}} | collective-permute-start | bytes 5898248 | tf_op jit(solution)/shard_map/ppermute | solution.py:432
  1347.4 126.3 %collective-permute-start.43 = (bf16[4,640,384]{2,1,0:T(8,128)(2,1)S(1)}, bf16[4,640,384]{2,1,0:T(8,128)(2,1)S(1)}, u32[]{:S(2)}, u32[]{:S(2)}) collective-permute-start(bf16[4,640,384]{2,1,0:T(8,128)(2,1)S(1)} %copy-done.54), channel_id=1, source_target_pairs={{0,4},{4,0},{1,5},{5,1},{2,6},{6,2},{3,7},{7,3}} | collective-permute-start | bytes 5898248 | tf_op jit(solution)/shard_map/ppermute | solution.py:435
  1355.5 34.4 %copy-start.26 = (bf16[4,640,384]{2,1,0:T(8,128)(2,1)S(1)}, bf16[4,640,384]{2,1,0:T(8,128)(2,1)}, u32[]{:S(2)}) copy-start(bf16[4,640,384]{2,1,0:T(8,128)(2,1)} %copy-done.25) | copy-start | bytes 5898244
  1389.4 125.2 %collective-permute-start.45 = (bf16[4,640,384]{2,1,0:T(8,128)(2,1)S(1)}, bf16[4,640,384]{2,1,0:T(8,128)(2,1)S(1)}, u32[]{:S(2)}, u32[]{:S(2)}) collective-permute-start(bf16[4,640,384]{2,1,0:T(8,128)(2,1)S(1)} %copy-done.53), channel_id=1, source_target_pairs={{0,4},{4,0},{1,5},{5,1},{2,6},{6,2},{3,7},{7,3}} | collective-permute-start | bytes 5898248 | tf_op jit(solution)/shard_map/ppermute | solution.py:435
  1392.0 81.7 %copy-start.3 = (bf16[4,640,384]{2,1,0:T(8,128)(2,1)S(1)}, bf16[4,640,384]{2,1,0:T(8,128)(2,1)}, u32[]{:S(2)}) copy-start(bf16[4,640,384]{2,1,0:T(8,128)(2,1)} %copy-done.2) | copy-start | bytes 5898244
  1392.6 84.5 %copy-start.5 = (bf16[4,640,384]{2,1,0:T(8,128)(2,1)S(1)}, bf16[4,640,384]{2,1,0:T(8,128)(2,1)}, u32[]{:S(2)}) copy-start(bf16[4,640,384]{2,1,0:T(8,128)(2,1)} %copy-done.4) | copy-start | bytes 5898244
  1431.6 86.8 %collective-permute-start.22 = (bf16[4,640,384]{2,1,0:T(8,128)(2,1)S(1)}, bf16[4,640,384]{2,1,0:T(8,128)(2,1)S(1)}, u32[]{:S(2)}, u32[]{:S(2)}) collective-permute-start(bf16[4,640,384]{2,1,0:T(8,128)(2,1)S(1)} %add_convert_fusion.11), channel_id=1, source_target_pairs={{0,2},{1,3},{2,0},{3,1},{4,6},{5,7},{6,4},{7,5}} | collective-permute-start | bytes 5898248 | tf_op jit(solution)/shard_map/ppermute | solution.py:432
  1432.1 48.5 %copy-start.39 = (bf16[4,640,384]{2,1,0:T(8,128)(2,1)}, bf16[4,640,384]{2,1,0:T(8,128)(2,1)S(1)}, u32[]{:S(2)}) copy-start(bf16[4,640,384]{2,1,0:T(8,128)(2,1)S(1)} %collective-permute-done.18) | copy-start | bytes 5898244
  1432.1 87.3 %collective-permute-start.24 = (bf16[4,640,384]{2,1,0:T(8,128)(2,1)S(1)}, bf16[4,640,384]{2,1,0:T(8,128)(2,1)S(1)}, u32[]{:S(2)}, u32[]{:S(2)}) collective-permute-start(bf16[4,640,384]{2,1,0:T(8,128)(2,1)S(1)} %add_convert_fusion.10), channel_id=1, source_target_pairs={{0,2},{1,3},{2,0},{3,1},{4,6},{5,7},{6,4},{7,5}} | collective-permute-start | bytes 5898248 | tf_op jit(solution)/shard_map/ppermute | solution.py:432
  1433.6 47.0 %copy-start.40 = (bf16[4,640,384]{2,1,0:T(8,128)(2,1)}, bf16[4,640,384]{2,1,0:T(8,128)(2,1)S(1)}, u32[]{:S(2)}) copy-start(bf16[4,640,384]{2,1,0:T(8,128)(2,1)S(1)} %collective-permute-done.20) | copy-start | bytes 5898244
  1433.6 126.0 %collective-permute-start.27 = (bf16[4,640,384]{2,1,0:T(8,128)(2,1)S(1)}, bf16[4,640,384]{2,1,0:T(8,128)(2,1)S(1)}, u32[]{:S(2)}, u32[]{:S(2)}) collective-permute-start(bf16[4,640,384]{2,1,0:T(8,128)(2,1)S(1)} %add_convert_fusion.9), channel_id=1, source_target_pairs={{0,3},{1,2},{2,1},{3,0},{4,7},{5,6},{6,5},{7,4}} | collective-permute-start | bytes 5898248 | tf_op jit(solution)/shard_map/ppermute | solution.py:432
  1473.7 128.0 %collective-permute-start.29 = (bf16[4,640,384]{2,1,0:T(8,128)(2,1)S(1)}, bf16[4,640,384]{2,1,0:T(8,128)(2,1)S(1)}, u32[]{:S(2)}, u32[]{:S(2)}) collective-permute-start(bf16[4,640,384]{2,1,0:T(8,128)(2,1)S(1)} %add_convert_fusion.8), channel_id=1, source_target_pairs={{0,3},{1,2},{2,1},{3,0},{4,7},{5,6},{6,5},{7,4}} | collective-permute-start | bytes 5898248 | tf_op jit(solution)/shard_map/ppermute | solution.py:432
  1482.4 34.1 %copy-start.24 = (bf16[4,640,384]{2,1,0:T(8,128)(2,1)S(1)}, bf16[4,640,384]{2,1,0:T(8,128)(2,1)}, u32[]{:S(2)}) copy-start(bf16[4,640,384]{2,1,0:T(8,128)(2,1)} %copy-done.23) | copy-start | bytes 5898244
  1514.6 165.5 %collective-permute-start.37 = (bf16[4,640,384]{2,1,0:T(8,128)(2,1)}, bf16[4,640,384]{2,1,0:T(8,128)(2,1)}, u32[]{:S(2)}, u32[]{:S(2)}) collective-permute-start(bf16[4,640,384]{2,1,0:T(8,128)(2,1)} %add_convert_fusion.5), channel_id=1, source_target_pairs={{0,1},{1,0},{2,3},{3,2},{4,5},{5,4},{6,7},{7,6}} | collective-permute-start | bytes 5898248 | tf_op jit(solution)/shard_map/ppermute | solution.py:432
  1518.3 84.6 %copy-start.42 = (bf16[4,640,384]{2,1,0:T(8,128)(2,1)}, bf16[4,640,384]{2,1,0:T(8,128)(2,1)S(1)}, u32[]{:S(2)}) copy-start(bf16[4,640,384]{2,1,0:T(8,128)(2,1)S(1)} %collective-permute-done.22) | copy-start | bytes 5898244
  1518.4 167.7 %collective-permute-start.39 = (bf16[4,640,384]{2,1,0:T(8,128)(2,1)}, bf16[4,640,384]{2,1,0:T(8,128)(2,1)}, u32[]{:S(2)}, u32[]{:S(2)}) collective-permute-start(bf16[4,640,384]{2,1,0:T(8,128)(2,1)} %add_convert_fusion.4), channel_id=1, source_target_pairs={{0,1},{1,0},{2,3},{3,2},{4,5},{5,4},{6,7},{7,6}} | collective-permute-start | bytes 5898248 | tf_op jit(solution)/shard_map/ppermute | solution.py:432
  1519.4 83.6 %copy-start.43 = (bf16[4,640,384]{2,1,0:T(8,128)(2,1)}, bf16[4,640,384]{2,1,0:T(8,128)(2,1)S(1)}, u32[]{:S(2)}) copy-start(bf16[4,640,384]{2,1,0:T(8,128)(2,1)S(1)} %collective-permute-done.24) | copy-start | bytes 5898244
  1519.4 166.7 %collective-permute-start.41 = (bf16[4,640,384]{2,1,0:T(8,128)(2,1)}, bf16[4,640,384]{2,1,0:T(8,128)(2,1)}, u32[]{:S(2)}, u32[]{:S(2)}) collective-permute-start(bf16[4,640,384]{2,1,0:T(8,128)(2,1)} %add_convert_fusion.3), channel_id=1, source_target_pairs={{0,2},{1,3},{2,0},{3,1},{4,6},{5,7},{6,4},{7,5}} | collective-permute-start | bytes 5898248 | tf_op jit(solution)/shard_map/ppermute | solution.py:432
  1559.6 42.1 %copy-start.44 = (bf16[4,640,384]{2,1,0:T(8,128)(2,1)}, bf16[4,640,384]{2,1,0:T(8,128)(2,1)S(1)}, u32[]{:S(2)}) copy-start(bf16[4,640,384]{2,1,0:T(8,128)(2,1)S(1)} %collective-permute-done.27) | copy-start | bytes 5898244
  1559.6 128.5 %collective-permute-start.42 = (bf16[4,640,384]{2,1,0:T(8,128)(2,1)}, bf16[4,640,384]{2,1,0:T(8,128)(2,1)}, u32[]{:S(2)}, u32[]{:S(2)}) collective-permute-start(bf16[4,640,384]{2,1,0:T(8,128)(2,1)} %add_convert_fusion.2), channel_id=1, source_target_pairs={{0,2},{1,3},{2,0},{3,1},{4,6},{5,7},{6,4},{7,5}} | collective-permute-start | bytes 5898248 | tf_op jit(solution)/shard_map/ppermute | solution.py:432
  1671.2 4.3 collective-permute-start.47
  1675.5 52.7 %collective-permute-start.44 = (bf16[4,640,384]{2,1,0:T(8,128)(2,1)}, bf16[4,640,384]{2,1,0:T(8,128)(2,1)S(1)}, u32[]{:S(2)}, u32[]{:S(2)}) collective-permute-start(bf16[4,640,384]{2,1,0:T(8,128)(2,1)} %add_convert_fusion.1), channel_id=1, source_target_pairs={{0,3},{1,2},{2,1},{3,0},{4,7},{5,6},{6,5},{7,4}} | collective-permute-start | bytes 5898248 | tf_op jit(solution)/shard_map/ppermute | solution.py:432
  1680.1 87.0 %collective-permute-start.46 = (bf16[4,640,384]{2,1,0:T(8,128)(2,1)}, bf16[4,640,384]{2,1,0:T(8,128)(2,1)}, u32[]{:S(2)}, u32[]{:S(2)}) collective-permute-start(bf16[4,640,384]{2,1,0:T(8,128)(2,1)} %add_convert_fusion), channel_id=1, source_target_pairs={{0,3},{1,2},{2,1},{3,0},{4,7},{5,6},{6,5},{7,4}} | collective-permute-start | bytes 5898248 | tf_op jit(solution)/shard_map/ppermute | solution.py:432
  1728.2 38.9 %copy-start.46 = (bf16[4,640,384]{2,1,0:T(8,128)(2,1)}, bf16[4,640,384]{2,1,0:T(8,128)(2,1)S(1)}, u32[]{:S(2)}) copy-start(bf16[4,640,384]{2,1,0:T(8,128)(2,1)S(1)} %collective-permute-done.44) | copy-start | bytes 5898244
  1848.7 3.9 collective-permute-start.48
  1849.0 139.8 %collective-permute-start.30 = (bf16[8192,384]{1,0:T(8,128)(2,1)}, bf16[8192,384]{1,0:T(8,128)(2,1)}, u32[]{:S(2)}, u32[]{:S(2)}) collective-permute-start(bf16[8192,384]{1,0:T(8,128)(2,1)} %get-tuple-element.198.own_ref), channel_id=1, source_target_pairs={{0,4},{4,0},{1,5},{5,1},{2,6},{6,2},{3,7},{7,3}} | collective-permute-start | bytes 18874376 | tf_op jit(solution)/shard_map/ppermute | solution.py:435
  1870.4 253.2 %collective-permute-start.49 = (bf16[8192,384]{1,0:T(8,128)(2,1)}, bf16[8192,384]{1,0:T(8,128)(2,1)}, u32[]{:S(2)}, u32[]{:S(2)}) collective-permute-start(bf16[8192,384]{1,0:T(8,128)(2,1)} %shard_map.146.own_ref), channel_id=1, source_target_pairs={{0,4},{4,0},{1,5},{5,1},{2,6},{6,2},{3,7},{7,3}} | collective-permute-start | bytes 18874376 | tf_op jit(solution)/shard_map/ppermute | solution.py:435
  (42 other events, 200.7 us)
Sparse Core Ops, SparseCore 0:
  1874.5 42.5 all-reduce.1

commit v3 on v2

--- a/solution.py
+++ b/solution.py
@@ -504,7 +504,6 @@
         for k in range(ep_size - 2):
             for unit, (keep_o, got_o, keep_d, got_d) in enumerate(sent[k]):
                 got_o, = after(tail, got_o)
-                got_d, d_out = lax.optimization_barrier((got_d, d_out))
                 sent[k][unit] = (keep_o, got_o, keep_d, got_d)
         near = sent[-1][0][0]
         for unit, (keep_o, got_o, keep_d, got_d) in enumerate(sent[-2]):
@@ -520,13 +519,12 @@
             got_o, d_gate = lax.optimization_barrier((got_o, d_gate))
             got_d, d_lin = lax.optimization_barrier((got_d, d_lin))
             sent[-1][unit] = (keep_o, got_o, keep_d, got_d)
-        o_back, du_back = [], []
-        for k in range(ep_size):
-            for keep_o, got_o, keep_d, got_d in sent[k]:
-                o_sum = fold(keep_o, got_o)
-                o_back.append(swap(o_sum, k) if k else o_sum)
-                du_sum = fold(keep_d, got_d)
-                du_back.append(swap(du_sum, k) if k else du_sum)
+
+        def back(k, keep, got):
+            total = fold(keep, got)
+            return swap(total, k) if k else total
+
+        o_back = [back(k, *sent[k][unit][:2]) for k in range(ep_size) for unit in range(2)]
 
         tile_rows = (rows >> 1) * 8
         row_first, row_second = tile_rows[:, 0], tile_rows[:, 1]
@@ -551,6 +549,11 @@
         z_loss = Z_COEF * stats[2, 0] / tokens
         aux_loss = AUX_COEF * experts * jnp.sum(frac_first * stats[1, :experts]) / tokens
         aux_row = (AUX_COEF * experts * frac_first).reshape(1, experts)
+        for k in range(ep_size - 2):
+            for unit, (keep_o, got_o, keep_d, got_d) in enumerate(sent[k]):
+                got_d, = after(y_half, got_d)
+                sent[k][unit] = (keep_o, got_o, keep_d, got_d)
+        du_back = [back(k, *sent[k][unit][2:]) for k in range(ep_size) for unit in range(2)]
         du_parts = [arr.reshape(-1, half) for arr in du_back]
         dxn, mix, d_scale_half, d_router_half = rows_call(
             norm_kernel, tp_vec,
@@ -560,7 +563,8 @@
         mix = mix.reshape(tok_count)
         mix = ((mix + swap_tp(mix)) / width).reshape(tok_count, 1)
         dx_half = rows_call(dx_kernel, tp_vec, [('half', x_loc), ('half', dy_loc), ('row', dxn), ('row', cols), ('row', mix)], [half_rows], tok_count, 1024)[0]
-        dx_loc = join(dx_half, swap_tp(dx_half))
+        dx_other = swap_tp(dx_half)
+        dx_loc = join(dx_half, dx_other)
         d_scale_half = d_scale_half.reshape(half)
         both = jnp.concatenate([d_router_half.reshape(-1), d_scale_half])
         both = lax.dynamic_update_slice_in_dim(jnp.zeros((2, both.shape[0]), jnp.float32), both[None], tp_id, 0)

time: 2150 us -> 1850 us (0.86)
  waiting for transfers between devices: 948 us -> 627 us
    ppermute x22, waiting for transfers between devices: 657 us -> 448 us  [swap_tp(): return lax.ppermute(arr, 'tp', [(0, 1), (1, 0)])]
    ppermute x28, waiting for transfers between devices: 249 us -> 139 us  [swap(): return lax.ppermute(arr, 'ep', [(i, i ^ k) for i in range(ep_size)])]
  transfers between devices with their start and end apart: 51 -> 51, of which waited for: 25 -> 17; matrix products, arithmetic and copies ran while one was open for 13% -> 16% of each run, Pallas kernels for 34% -> 40%
where the time goes in v3:
time: 1850 us; the launch traced here: 1830 us
  Pallas kernels  825 us (45%)
  waiting for transfers between devices  627 us (34%)
  matrix products  186 us (10%)
  other arithmetic  76.2 us (4%)
  local copies, waits for them, and re-layouts  64.2 us (3%)
  starting transfers between devices  39.2 us (2%)
    ppermute x22, waiting for transfers between devices, swap_tp(): return lax.ppermute(arr, 'tp', [(0, 1), (1, 0)])  448 us
    pallas_call x8, Pallas kernels, ffn_call(): pl.pallas_call(ffn_kernel, grid=(count, steps), in_specs=in_specs, out_sp...  413 us
    pallas_call x5, Pallas kernels, rows_call(): pl.pallas_call(kernel, grid_spec=pltpu.PrefetchScalarGridSpec(num_scalar_...  182 us
    pallas_call x8, Pallas kernels, gather_rows(): pl.pallas_call(functools.partial(gather_kernel, parts, fills, blk, rows,...  177 us
    ppermute x28, waiting for transfers between devices, swap(): return lax.ppermute(arr, 'ep', [(i, i ^ k) for i in range(ep_size)])  139 us
    dot_general x1, matrix products, device_body(): jnp.einsum('sxcd,sxcf->xdf', u_slot, da_slot, preferred_element_type=jnp....  62 us
    dot_general x1, matrix products, device_body(): jnp.einsum('sxcd,sxcf->xdf', u_slot, db_slot, preferred_element_type=jnp....  61.8 us
    dot_general x1, matrix products, device_body(): jnp.einsum('sxcf,sxcd->xfd', h_slot, do_slot, preferred_element_type=jnp....  61.7 us
  transfers between devices with their start and end apart: 51, of which 17 were waited for; matrix products, arithmetic and copies ran while one was open for 16% of the time, Pallas kernels for 40%

profile of v3, /device:TPU:0, one launch (start us, length us, event | category | flops | bytes accessed | tf_op | source)
XLA Modules:
  0.0 1833.2 jit_solution(11926033626414032489)
XLA Ops:
  10.8 3.4 copy.144.idx_ref.refs_10_
  15.7 53.4 %router.1 = (f32[8192,32]{1,0:T(8,128)}, f32[8192,8]{1,0:T(8,128)}, s32[8192,2]{1,0:T(8,128)}, f32[160,640]{1,0:T(8,128)}, f32[8,128]{1,0:T(8,128)}) custom-call(s32[1]{0:T(128)} %bitcast.1.ep_ref, bf16[8192,768]{1,0:T(8,128)(2,1)} %x_ref.3, s32[8192,2]{1,0:T(8,128)} %copy.144.idx_ref.refs_10_, f32[1,768]{1,0:T(1,128)} %reshape.257.scale_ref.refs_14_, ...), custom_call_target="tpu_custom_call" | custom-call | flops 10000000000 | bytes 25165824 | tf_op jit(solution)/shard_map/router/pallas_call | solution.py:163
  71.9 21.8 %gather_rows.8 = bf16[5120,768]{1,0:T(8,128)(2,1)} custom-call(s32[5120]{0:T(1024)} %mul.81.idx_ref, bf16[8192,768]{1,0:T(8,128)(2,1)} %x_ref.3), custom_call_target="tpu_custom_call" | custom-call | flops 40000000000 | bytes 15728640 | tf_op jit(solution)/shard_map/gather_rows/pallas_call | solution.py:227
  96.0 5.9 constant_dynamic-slice_fusion
  101.9 21.8 %gather_rows.9 = bf16[5120,768]{1,0:T(8,128)(2,1)} custom-call(s32[5120]{0:T(1024)} %mul.81.idx_ref, bf16[8192,768]{1,0:T(8,128)(2,1)} %dy_ref.1), custom_call_target="tpu_custom_call" | custom-call | flops 40000000000 | bytes 15728640 | tf_op jit(solution)/shard_map/gather_rows/pallas_call | solution.py:227
  123.7 2.5 shift-right-arithmetic_multiply_fusion
  126.3 51.4 %ffn.8 = (bf16[4,8,640,768]{3,2,1,0:T(8,128)(2,1)}, bf16[4,8,640,768]{3,2,1,0:T(8,128)(2,1)}, bf16[4,8,640,1536]{3,2,1,0:T(8,128)(2,1)}, bf16[4,8,640,1536]{3,2,...) custom-call(s32[1]{0:T(128)} %bitcast.tp_ref, ...), custom_call_target="tpu_custom_call" | custom-call | flops 36238786560 | bytes 47185920 | tf_op jit(solution)/shard_map/ffn/pallas_call | solution.py:408
  180.3 51.6 %ffn.9 = (bf16[4,8,640,768]{3,2,1,0:T(8,128)(2,1)}, bf16[4,8,640,768]{3,2,1,0:T(8,128)(2,1)}, bf16[4,8,640,1536]{3,2,1,0:T(8,128)(2,1)}, bf16[4,8,640,1536]{3,2,...) custom-call(s32[1]{0:T(128)} %bitcast.tp_ref, ...), custom_call_target="tpu_custom_call", output_to_operand_aliasing={{0}: (8, {}), {1}: (9, {}), {2}: (10, {}), {3}: (11, {}), {... | custom-call | flops 36238786560 | bytes 47185920 | tf_op jit(solution)/shard_map/ffn/pallas_call | solution.py:408
  231.9 3.9 slice_reduce_fusion
  242.3 21.8 %gather_rows.10 = bf16[5120,768]{1,0:T(8,128)(2,1)} custom-call(s32[5120]{0:T(1024)} %mul.83.idx_ref, bf16[8192,768]{1,0:T(8,128)(2,1)} %collective-permute-done.4.refs_0_), custom_call_target="tpu_custom_call" | custom-call | flops 40000000000 | bytes 15728640 | tf_op jit(solution)/shard_map/gather_rows/pallas_call | solution.py:227
  264.2 86.9 %collective-permute-done.6.refs_0_ = bf16[2048,768]{1,0:T(8,128)(2,1)} collective-permute-done((bf16[2048,768]{1,0:T(8,128)(2,1)}, bf16[2048,768]{1,0:T(8,128)(2,1)}, u32[]{:S(2)}, u32[]{:S(2)}) %collective-permute-start.6) | collective-permute-done | bytes 3145760 | tf_op jit(solution)/shard_map/ppermute | solution.py:432
  354.3 21.8 %gather_rows.11 = bf16[5120,768]{1,0:T(8,128)(2,1)} custom-call(s32[5120]{0:T(1024)} %mul.83.idx_ref, bf16[8192,768]{1,0:T(8,128)(2,1)} %collective-permute-done.5.refs_0_), custom_call_target="tpu_custom_call" | custom-call | flops 40000000000 | bytes 15728640 | tf_op jit(solution)/shard_map/gather_rows/pallas_call | solution.py:227
  376.1 51.8 %ffn.10 = (bf16[4,8,640,768]{3,2,1,0:T(8,128)(2,1)}, bf16[4,8,640,768]{3,2,1,0:T(8,128)(2,1)}, bf16[4,8,640,1536]{3,2,1,0:T(8,128)(2,1)}, bf16[4,8,640,1536]{3,2...) custom-call(s32[1]{0:T(128)} %bitcast.tp_ref, ...), custom_call_target="tpu_custom_call", output_to_operand_aliasing={{0}: (8, {}), {1}: (9, {}), {2}: (10, {}), {3}: (11, {}), {... | custom-call | flops 36238786560 | bytes 47185920 | tf_op jit(solution)/shard_map/ffn/pallas_call | solution.py:408
  431.8 51.4 %ffn.11 = (bf16[4,8,640,768]{3,2,1,0:T(8,128)(2,1)}, bf16[4,8,640,768]{3,2,1,0:T(8,128)(2,1)}, bf16[4,8,640,1536]{3,2,1,0:T(8,128)(2,1)}, bf16[4,8,640,1536]{3,2...) custom-call(s32[1]{0:T(128)} %bitcast.tp_ref, ...), custom_call_target="tpu_custom_call", output_to_operand_aliasing={{0}: (8, {}), {1}: (9, {}), {2}: (10, {}), {3}: (11, {}), {... | custom-call | flops 36238786560 | bytes 47185920 | tf_op jit(solution)/shard_map/ffn/pallas_call | solution.py:408
  490.9 21.8 %gather_rows.13 = bf16[5120,768]{1,0:T(8,128)(2,1)} custom-call(s32[5120]{0:T(1024)} %mul.88.idx_ref, bf16[8192,768]{1,0:T(8,128)(2,1)} %collective-permute-done.10.refs_0_), custom_call_target="tpu_custom_call" | custom-call | flops 40000000000 | bytes 15728640 | tf_op jit(solution)/shard_map/gather_rows/pallas_call | solution.py:227
  512.7 45.2 %collective-permute-done.9.refs_3_ = bf16[2048,768]{1,0:T(8,128)(2,1)} collective-permute-done((bf16[2048,768]{1,0:T(8,128)(2,1)}, bf16[2048,768]{1,0:T(8,128)(2,1)}, u32[]{:S(2)}, u32[]{:S(2)}) %collective-permute-start.9) | collective-permute-done | bytes 3145760 | tf_op jit(solution)/shard_map/ppermute | solution.py:435
  557.9 23.0 %gather_rows.12 = bf16[5120,768]{1,0:T(8,128)(2,1)} custom-call(s32[5120]{0:T(1024)} %fusion.11.idx_ref, bf16[2048,768]{1,0:T(8,128)(2,1)} %collective-permute-done.6.refs_0_, bf16[2048,768]{1,0:T(8,128)(2,1)} %collective-permute-done.7.refs_1_, bf16[2048,768]{1,0:T(8,128)(2,1)} %collective-permute-done.8.refs_2_, ...), custom_call_target="tpu_custom_call" | custom-call | flops 40000000000 | bytes 15728640 | tf_op jit(solution)/shard_map/gather_rows/pallas_call | solution.py:227
  583.9 51.3 %ffn.12 = (bf16[4,8,640,768]{3,2,1,0:T(8,128)(2,1)}, bf16[4,8,640,768]{3,2,1,0:T(8,128)(2,1)}, bf16[4,8,640,1536]{3,2,1,0:T(8,128)(2,1)}, bf16[4,8,640,1536]{3,2...) custom-call(s32[1]{0:T(128)} %bitcast.tp_ref, ...), custom_call_target="tpu_custom_call", output_to_operand_aliasing={{0}: (8, {}), {1}: (9, {}), {2}: (10, {}), {3}: (11, {}), {... | custom-call | flops 36238786560 | bytes 47185920 | tf_op jit(solution)/shard_map/ffn/pallas_call | solution.py:408
  639.6 51.8 %ffn.13 = (bf16[4,8,640,768]{3,2,1,0:T(8,128)(2,1)}, bf16[4,8,640,768]{3,2,1,0:T(8,128)(2,1)}, bf16[4,8,640,1536]{3,2,1,0:T(8,128)(2,1)}, bf16[4,8,640,1536]{3,2...) custom-call(s32[1]{0:T(128)} %bitcast.tp_ref, ...), custom_call_target="tpu_custom_call", output_to_operand_aliasing={{0}: (8, {}), {1}: (9, {}), {2}: (10, {}), {3}: (11, {}), {... | custom-call | flops 36238786560 | bytes 47185920 | tf_op jit(solution)/shard_map/ffn/pallas_call | solution.py:408
  702.0 22.9 %gather_rows.14 = bf16[5120,768]{1,0:T(8,128)(2,1)} custom-call(s32[5120]{0:T(1024)} %fusion.15.idx_ref, bf16[2048,768]{1,0:T(8,128)(2,1)} %collective-permute-done.11.refs_0_, bf16[2048,768]{1,0:T(8,128)(2,1)} %collective-permute-done.12.refs_1_, bf16[2048,768]{1,0:T(8,128)(2,1)} %collective-permute-done.13.refs_2_, ...), custom_call_target="tpu_custom_call" | custom-call | flops 40000000000 | bytes 15728640 | tf_op jit(solution)/shard_map/gather_rows/pallas_call | solution.py:227
  726.4 21.8 %gather_rows.15 = bf16[5120,768]{1,0:T(8,128)(2,1)} custom-call(s32[5120]{0:T(1024)} %mul.92.idx_ref, bf16[8192,768]{1,0:T(8,128)(2,1)} %collective-permute-done.15.refs_0_), custom_call_target="tpu_custom_call" | custom-call | flops 40000000000 | bytes 15728640 | tf_op jit(solution)/shard_map/gather_rows/pallas_call | solution.py:227
  748.2 51.9 %ffn.14 = (bf16[4,8,640,768]{3,2,1,0:T(8,128)(2,1)}, bf16[4,8,640,768]{3,2,1,0:T(8,128)(2,1)}, bf16[4,8,640,1536]{3,2,1,0:T(8,128)(2,1)}, bf16[4,8,640,1536]{3,2...) custom-call(s32[1]{0:T(128)} %bitcast.tp_ref, ...), custom_call_target="tpu_custom_call", output_to_operand_aliasing={{0}: (8, {}), {1}: (9, {}), {2}: (10, {}), {3}: (11, {}), {... | custom-call | flops 36238786560 | bytes 47185920 | tf_op jit(solution)/shard_map/ffn/pallas_call | solution.py:408
  807.4 51.7 %ffn.15 = (bf16[4,8,640,768]{3,2,1,0:T(8,128)(2,1)}, bf16[4,8,640,768]{3,2,1,0:T(8,128)(2,1)}, bf16[4,8,640,1536]{3,2,1,0:T(8,128)(2,1)}, bf16[4,8,640,1536]{3,2...) custom-call(s32[1]{0:T(128)} %bitcast.tp_ref, ...), custom_call_target="tpu_custom_call", output_to_operand_aliasing={{0}: (8, {}), {1}: (9, {}), {2}: (10, {}), {3}: (11, {}), {... | custom-call | flops 36238786560 | bytes 47185920 | tf_op jit(solution)/shard_map/ffn/pallas_call | solution.py:408
  860.4 4.0 add_convert_fusion.13
  864.5 3.3 add_convert_fusion.12
  869.3 21.4 %collective-permute-done.21 = bf16[4,640,384]{2,1,0:T(8,128)(2,1)} collective-permute-done((bf16[4,640,384]{2,1,0:T(8,128)(2,1)S(1)}, bf16[4,640,384]{2,1,0:T(8,128)(2,1)}, u32[]{:S(2)}, u32[]{:S(2)}) %collective-permute-start.21) | collective-permute-done | bytes 1966112 | tf_op jit(solution)/shard_map/ppermute | solution.py:435
  891.2 41.6 %collective-permute-done.23 = bf16[4,640,384]{2,1,0:T(8,128)(2,1)} collective-permute-done((bf16[4,640,384]{2,1,0:T(8,128)(2,1)}, bf16[4,640,384]{2,1,0:T(8,128)(2,1)}, u32[]{:S(2)}, u32[]{:S(2)}) %collective-permute-start.23) | collective-permute-done | bytes 1966112 | tf_op jit(solution)/shard_map/ppermute | solution.py:435
  932.9 42.1 %collective-permute-done.26 = bf16[4,640,384]{2,1,0:T(8,128)(2,1)} collective-permute-done((bf16[4,640,384]{2,1,0:T(8,128)(2,1)}, bf16[4,640,384]{2,1,0:T(8,128)(2,1)}, u32[]{:S(2)}, u32[]{:S(2)}) %collective-permute-start.26) | collective-permute-done | bytes 1966112 | tf_op jit(solution)/shard_map/ppermute | solution.py:435
  975.0 42.1 %collective-permute-done.25 = bf16[4,640,384]{2,1,0:T(8,128)(2,1)} collective-permute-done((bf16[4,640,384]{2,1,0:T(8,128)(2,1)}, bf16[4,640,384]{2,1,0:T(8,128)(2,1)}, u32[]{:S(2)}, u32[]{:S(2)}) %collective-permute-start.25) | collective-permute-done | bytes 1966112 | tf_op jit(solution)/shard_map/ppermute | solution.py:435
  1017.6 62.0 %convolution_bitcast_fusion.1 = f32[8,768,1536]{2,1,0:T(8,128)} fusion(bf16[4,8,640,768]{3,2,1,0:T(8,128)(2,1)} %get-tuple-element.186, bf16[4,8,640,1536]{3,2,1,0:T(8,128)(2,1)} %get-tuple-element.187), kind=kOutput, calls=%fused_computation.1 | convolution fusion | flops 48318382080 | bytes 132120576 | tf_op jit(solution)/shard_map/sxcd,sxcf->xdf/dot_general | solution.py:495
  1079.6 4.0 add_convert_fusion.11
  1083.7 3.5 add_convert_fusion.10
  1087.1 3.4 add_convert_fusion.9
  1090.9 10.5 collective-permute-done.40
  1104.0 39.6 %collective-permute-done.28 = bf16[4,640,384]{2,1,0:T(8,128)(2,1)} collective-permute-done((bf16[4,640,384]{2,1,0:T(8,128)(2,1)}, bf16[4,640,384]{2,1,0:T(8,128)(2,1)}, u32[]{:S(2)}, u32[]{:S(2)}) %collective-permute-start.28) | collective-permute-done | bytes 1966112 | tf_op jit(solution)/shard_map/ppermute | solution.py:435
  1143.5 61.8 %convolution_bitcast_fusion = f32[8,768,1536]{2,1,0:T(8,128)} fusion(bf16[4,8,640,768]{3,2,1,0:T(8,128)(2,1)} %get-tuple-element.186, bf16[4,8,640,1536]{3,2,1,0:T(8,128)(2,1)} %get-tuple-element.218), kind=kOutput, calls=%fused_computation | convolution fusion | flops 48318382080 | bytes 132120576 | tf_op jit(solution)/shard_map/sxcd,sxcf->xdf/dot_general | solution.py:496
  1205.3 4.0 add_convert_fusion.15
  1213.3 3.3 add_convert_fusion.14
  1216.7 3.5 add_convert_fusion.3
  1220.2 3.5 add_convert_fusion.2
  1231.4 3.3 add_convert_fusion.1
  1234.8 3.4 add_convert_fusion
  1238.1 19.0 %collective-permute-done.29 = bf16[4,640,384]{2,1,0:T(8,128)(2,1)} collective-permute-done((bf16[4,640,384]{2,1,0:T(8,128)(2,1)S(1)}, bf16[4,640,384]{2,1,0:T(8,128)(2,1)}, u32[]{:S(2)}, u32[]{:S(2)}) %collective-permute-start.29) | collective-permute-done | bytes 1966112 | tf_op jit(solution)/shard_map/ppermute | solution.py:432
  1258.8 65.4 %shard_map.143 = (bf16[8192,384]{1,0:T(8,128)(2,1)}, f32[8192,2]{1,0:T(8,128)}) custom-call(s32[1]{0:T(128)} %bitcast.tp_ref, s32[8192]{0:T(1024)} %get-tuple-element.275.first_ref, s32[8192]{0:T(1024)} %get-tuple-element.274.second_ref, bf16[2560,384]{1,0:T(8,128)(2,1)} %bitcast.103, bf16[2560,384]{1,0:T(8,128)(2,1)} %bitcast.104, ...), custom_call_target="tpu_custom_call" | custom-call | flops 10000000000 | bytes 41025536 | tf_op jit(solution)/shard_map/pallas_call | solution.py:370
  1326.4 27.5 %collective-permute-done.36 = bf16[4,640,384]{2,1,0:T(8,128)(2,1)} collective-permute-done((bf16[4,640,384]{2,1,0:T(8,128)(2,1)}, bf16[4,640,384]{2,1,0:T(8,128)(2,1)}, u32[]{:S(2)}, u32[]{:S(2)}) %collective-permute-start.36) | collective-permute-done | bytes 1966112 | tf_op jit(solution)/shard_map/ppermute | solution.py:435
  1353.9 41.2 %collective-permute-done.38 = bf16[4,640,384]{2,1,0:T(8,128)(2,1)} collective-permute-done((bf16[4,640,384]{2,1,0:T(8,128)(2,1)}, bf16[4,640,384]{2,1,0:T(8,128)(2,1)}, u32[]{:S(2)}, u32[]{:S(2)}) %collective-permute-start.38) | collective-permute-done | bytes 1966112 | tf_op jit(solution)/shard_map/ppermute | solution.py:435
  1395.1 2.8 copy.156
  1398.5 3.4 add_convert_fusion.7
  1401.9 3.5 add_convert_fusion.6
  1405.4 3.5 add_convert_fusion.5
  1408.9 3.4 add_convert_fusion.4
  1412.3 2.7 copy.157
  1415.5 5.9 add_bitcast_fusion.refs_11_
  1421.4 32.8 %collective-permute-done.46 = bf16[4,640,384]{2,1,0:T(8,128)(2,1)} collective-permute-done((bf16[4,640,384]{2,1,0:T(8,128)(2,1)}, bf16[4,640,384]{2,1,0:T(8,128)(2,1)}, u32[]{:S(2)}, u32[]{:S(2)}) %collective-permute-start.46) | collective-permute-done | bytes 1966112 | tf_op jit(solution)/shard_map/ppermute | solution.py:432
  1455.4 78.3 %shard_map.145 = (f32[8192,384]{1,0:T(8,128)}, f32[8192,1]{1,0:T(8,128)}, f32[1,384]{1,0:T(1,128)}, f32[384,32]{1,0:T(8,128)}) custom-call(s32[1]{0:T(128)} %bitcast.tp_ref, s32[8192]{0:T(1024)} %get-tuple-element.275.first_ref, s32[8192]{0:T(1024)} %get-tuple-element.274.second_ref, bf16[2560,384]{1,0:T(8,128)(2,1)} %bitcast.105, ...), custom_call_target="tpu_custom_call" | custom-call | flops 10000000000 | bytes 29083200 | tf_op jit(solution)/shard_map/pallas_call | solution.py:370
  1533.7 3.3 reduce.3
  1541.0 2.7 copy.160.mix_ref
  1543.6 15.1 shard_map.146.own_ref
  1560.6 61.7 %convolution_bitcast_fusion.2 = f32[8,1536,768]{2,1,0:T(8,128)} fusion(bf16[4,8,640,1536]{3,2,1,0:T(8,128)(2,1)} %get-tuple-element.232, bf16[4,8,640,768]{3,2,1,0:T(8,128)(2,1)} %get-tuple-element.233), kind=kOutput, calls=%fused_computation.2 | convolution fusion | flops 48318382080 | bytes 132120576 | tf_op jit(solution)/shard_map/sxcf,sxcd->xfd/dot_general | solution.py:497
  1624.7 39.9 %all-reduce.2.cloned.1.call-done = f32[2,12672]{1,0:T(2,128)} async-done(((f32[2,12672]{1,0:T(2,128)}), f32[2,12672]{1,0:T(2,128)}) %all-reduce.2.cloned.1.call-update) | async-done | bytes 101392 | tf_op jit(solution)/shard_map/psum | solution.py:571
  1667.8 13.0 collective-permute-done.30.other_ref
  1680.8 11.5 shard_map.144
  1692.2 122.2 %collective-permute-done.49.other_ref = bf16[8192,384]{1,0:T(8,128)(2,1)} collective-permute-done((bf16[8192,384]{1,0:T(8,128)(2,1)}, bf16[8192,384]{1,0:T(8,128)(2,1)}, u32[]{:S(2)}, u32[]{:S(2)}) %collective-permute-start.49) | collective-permute-done | bytes 6291488 | tf_op jit(solution)/shard_map/ppermute | solution.py:435
  1814.5 11.5 shard_map.147
  (217 shorter events, 95.4 us)
Async XLA Ops:
  7.2 7.0 copy-start.39
  7.2 7.6 copy-start.38
  7.2 1657.4 %all-reduce.2.cloned.1.call-start = ((), (), s32[]{:S(2)}) async-start(), calls=%async_computation | async-start | bytes 202752 | tf_op jit(solution)/shard_map/psum | solution.py:571
  7.2 345.6 %collective-permute-start.5 = (bf16[8192,768]{1,0:T(8,128)(2,1)}, bf16[8192,768]{1,0:T(8,128)(2,1)}, u32[]{:S(2)}, u32[]{:S(2)}) collective-permute-start(bf16[8192,768]{1,0:T(8,128)(2,1)} %dy_ref.1), channel_id=1, source_target_pairs={{0,1},{1,0},{2,3},{3,2},{4,5},{5,4},{6,7},{7,6}} | collective-permute-start | bytes 37748744 | tf_op jit(solution)/shard_map/ppermute | solution.py:432
  8.1 482.5 %collective-permute-start.10 = (bf16[8192,768]{1,0:T(8,128)(2,1)}, bf16[8192,768]{1,0:T(8,128)(2,1)}, u32[]{:S(2)}, u32[]{:S(2)}) collective-permute-start(bf16[8192,768]{1,0:T(8,128)(2,1)} %dy_ref.1), channel_id=1, source_target_pairs={{0,2},{1,3},{2,0},{3,1},{4,6},{5,7},{6,4},{7,5}} | collective-permute-start | bytes 37748744 | tf_op jit(solution)/shard_map/ppermute | solution.py:432
  10.6 231.5 %collective-permute-start.4 = (bf16[8192,768]{1,0:T(8,128)(2,1)}, bf16[8192,768]{1,0:T(8,128)(2,1)}, u32[]{:S(2)}, u32[]{:S(2)}) collective-permute-start(bf16[8192,768]{1,0:T(8,128)(2,1)} %x_ref.3), channel_id=1, source_target_pairs={{0,1},{1,0},{2,3},{3,2},{4,5},{5,4},{6,7},{7,6}} | collective-permute-start | bytes 37748744 | tf_op jit(solution)/shard_map/ppermute | solution.py:432
  70.8 568.3 %collective-permute-start.1 = (f32[8,2,640]{2,0,1:T(8,128)}, f32[8,2,640]{2,0,1:T(8,128)}, u32[]{:S(2)}, u32[]{:S(2)}) collective-permute-start(f32[8,2,640]{2,0,1:T(8,128)} %get-tuple-element.281), channel_id=1, source_target_pairs={{0,3},{1,2},{2,1},{3,0},{4,7},{5,6},{6,5},{7,4}} | collective-permute-start | bytes 122888 | tf_op jit(solution)/shard_map/ppermute | solution.py:432
  70.8 165.0 %collective-permute-start.3 = (f32[8,2,640]{2,0,1:T(8,128)}, f32[8,2,640]{2,0,1:T(8,128)}, u32[]{:S(2)}, u32[]{:S(2)}) collective-permute-start(f32[8,2,640]{2,0,1:T(8,128)} %get-tuple-element.280), channel_id=1, source_target_pairs={{0,1},{1,0},{2,3},{3,2},{4,5},{5,4},{6,7},{7,6}} | collective-permute-start | bytes 122888 | tf_op jit(solution)/shard_map/ppermute | solution.py:432
  235.9 251.2 %collective-permute-start.2 = (f32[8,2,640]{2,0,1:T(8,128)}, f32[8,2,640]{2,0,1:T(8,128)}, u32[]{:S(2)}, u32[]{:S(2)}) collective-permute-start(f32[8,2,640]{2,0,1:T(8,128)} %get-tuple-element.282), channel_id=1, source_target_pairs={{0,2},{1,3},{2,0},{3,1},{4,6},{5,7},{6,4},{7,5}} | collective-permute-start | bytes 122888 | tf_op jit(solution)/shard_map/ppermute | solution.py:432
  242.1 109.0 %collective-permute-start.6 = (bf16[2048,768]{1,0:T(8,128)(2,1)}, bf16[2048,768]{1,0:T(8,128)(2,1)}, u32[]{:S(2)}, u32[]{:S(2)}) collective-permute-start(bf16[2048,768]{1,0:T(8,128)(2,1)} %get-tuple-element.279), channel_id=1, source_target_pairs={{0,2},{1,3},{2,0},{3,1},{4,6},{5,7},{6,4},{7,5}} | collective-permute-start | bytes 9437192 | tf_op jit(solution)/shard_map/ppermute | solution.py:432
  351.1 136.0 %collective-permute-start.7 = (bf16[2048,768]{1,0:T(8,128)(2,1)}, bf16[2048,768]{1,0:T(8,128)(2,1)}, u32[]{:S(2)}, u32[]{:S(2)}) collective-permute-start(bf16[2048,768]{1,0:T(8,128)(2,1)} %get-tuple-element.278), channel_id=1, source_target_pairs={{0,2},{1,3},{2,0},{3,1},{4,6},{5,7},{6,4},{7,5}} | collective-permute-start | bytes 9437192 | tf_op jit(solution)/shard_map/ppermute | solution.py:432
  352.8 137.6 %collective-permute-start.8 = (bf16[2048,768]{1,0:T(8,128)(2,1)}, bf16[2048,768]{1,0:T(8,128)(2,1)}, u32[]{:S(2)}, u32[]{:S(2)}) collective-permute-start(bf16[2048,768]{1,0:T(8,128)(2,1)} %collective-permute-done.6.refs_0_), channel_id=1, source_target_pairs={{0,4},{4,0},{1,5},{5,1},{2,6},{6,2},{3,7},{7,3}} | collective-permute-start | bytes 9437192 | tf_op jit(solution)/shard_map/ppermute | solution.py:435
  487.1 212.6 %collective-permute-start.11 = (bf16[2048,768]{1,0:T(8,128)(2,1)}, bf16[2048,768]{1,0:T(8,128)(2,1)}, u32[]{:S(2)}, u32[]{:S(2)}) collective-permute-start(bf16[2048,768]{1,0:T(8,128)(2,1)} %collective-permute-done.6.refs_0_), channel_id=1, source_target_pairs={{0,1},{1,0},{2,3},{3,2},{4,5},{5,4},{6,7},{7,6}} | collective-permute-start | bytes 9437192 | tf_op jit(solution)/shard_map/ppermute | solution.py:432
  487.1 70.8 %collective-permute-start.9 = (bf16[2048,768]{1,0:T(8,128)(2,1)}, bf16[2048,768]{1,0:T(8,128)(2,1)}, u32[]{:S(2)}, u32[]{:S(2)}) collective-permute-start(bf16[2048,768]{1,0:T(8,128)(2,1)} %collective-permute-done.7.refs_1_), channel_id=1, source_target_pairs={{0,4},{4,0},{1,5},{5,1},{2,6},{6,2},{3,7},{7,3}} | collective-permute-start | bytes 9437192 | tf_op jit(solution)/shard_map/ppermute | solution.py:435
  490.4 209.3 %collective-permute-start.12 = (bf16[2048,768]{1,0:T(8,128)(2,1)}, bf16[2048,768]{1,0:T(8,128)(2,1)}, u32[]{:S(2)}, u32[]{:S(2)}) collective-permute-start(bf16[2048,768]{1,0:T(8,128)(2,1)} %collective-permute-done.7.refs_1_), channel_id=1, source_target_pairs={{0,1},{1,0},{2,3},{3,2},{4,5},{5,4},{6,7},{7,6}} | collective-permute-start | bytes 9437192 | tf_op jit(solution)/shard_map/ppermute | solution.py:432
  490.6 209.7 %collective-permute-start.13 = (bf16[2048,768]{1,0:T(8,128)(2,1)}, bf16[2048,768]{1,0:T(8,128)(2,1)}, u32[]{:S(2)}, u32[]{:S(2)}) collective-permute-start(bf16[2048,768]{1,0:T(8,128)(2,1)} %collective-permute-done.8.refs_2_), channel_id=1, source_target_pairs={{0,1},{1,0},{2,3},{3,2},{4,5},{5,4},{6,7},{7,6}} | collective-permute-start | bytes 9437192 | tf_op jit(solution)/shard_map/ppermute | solution.py:432
  557.9 167.0 %collective-permute-start.15 = (bf16[8192,768]{1,0:T(8,128)(2,1)}, bf16[8192,768]{1,0:T(8,128)(2,1)}, u32[]{:S(2)}, u32[]{:S(2)}) collective-permute-start(bf16[8192,768]{1,0:T(8,128)(2,1)} %collective-permute-done.10.refs_0_), channel_id=1, source_target_pairs={{0,1},{1,0},{2,3},{3,2},{4,5},{5,4},{6,7},{7,6}} | collective-permute-start | bytes 37748744 | tf_op jit(solution)/shard_map/ppermute | solution.py:432
  639.1 62.4 %collective-permute-start.14 = (bf16[2048,768]{1,0:T(8,128)(2,1)}, bf16[2048,768]{1,0:T(8,128)(2,1)}, u32[]{:S(2)}, u32[]{:S(2)}) collective-permute-start(bf16[2048,768]{1,0:T(8,128)(2,1)} %collective-permute-done.9.refs_3_), channel_id=1, source_target_pairs={{0,1},{1,0},{2,3},{3,2},{4,5},{5,4},{6,7},{7,6}} | collective-permute-start | bytes 9437192 | tf_op jit(solution)/shard_map/ppermute | solution.py:432
  699.7 103.1 %collective-permute-start.31 = (f32[8,128]{1,0:T(8,128)}, f32[8,128]{1,0:T(8,128)}, u32[]{:S(2)}, u32[]{:S(2)}) collective-permute-start(f32[8,128]{1,0:T(8,128)} %get-tuple-element.195), channel_id=1, source_target_pairs={{0,1},{1,0},{2,3},{3,2},{4,5},{5,4},{6,7},{7,6}} | collective-permute-start | bytes 12296 | tf_op jit(solution)/shard_map/ppermute | solution.py:432
  699.7 103.6 %collective-permute-start.32 = (f32[8,128]{1,0:T(8,128)}, f32[8,128]{1,0:T(8,128)}, u32[]{:S(2)}, u32[]{:S(2)}) collective-permute-start(f32[8,128]{1,0:T(8,128)} %get-tuple-element.195), channel_id=1, source_target_pairs={{0,2},{1,3},{2,0},{3,1},{4,6},{5,7},{6,4},{7,5}} | collective-permute-start | bytes 12296 | tf_op jit(solution)/shard_map/ppermute | solution.py:432
  700.2 104.6 %collective-permute-start.33 = (f32[8,128]{1,0:T(8,128)}, f32[8,128]{1,0:T(8,128)}, u32[]{:S(2)}, u32[]{:S(2)}) collective-permute-start(f32[8,128]{1,0:T(8,128)} %get-tuple-element.195), channel_id=1, source_target_pairs={{0,3},{1,2},{2,1},{3,0},{4,7},{5,6},{6,5},{7,4}} | collective-permute-start | bytes 12296 | tf_op jit(solution)/shard_map/ppermute | solution.py:432
  701.5 103.8 %collective-permute-start.17 = (bf16[4,640,384]{2,1,0:T(8,128)(2,1)}, bf16[4,640,384]{2,1,0:T(8,128)(2,1)}, u32[]{:S(2)}, u32[]{:S(2)}) collective-permute-start(bf16[4,640,384]{2,1,0:T(8,128)(2,1)} %copy-done.31), channel_id=1, source_target_pairs={{0,4},{4,0},{1,5},{5,1},{2,6},{6,2},{3,7},{7,3}} | collective-permute-start | bytes 5898248 | tf_op jit(solution)/shard_map/ppermute | solution.py:435
  724.9 82.0 %collective-permute-start.19 = (bf16[4,640,384]{2,1,0:T(8,128)(2,1)}, bf16[4,640,384]{2,1,0:T(8,128)(2,1)}, u32[]{:S(2)}, u32[]{:S(2)}) collective-permute-start(bf16[4,640,384]{2,1,0:T(8,128)(2,1)} %copy-done.32), channel_id=1, source_target_pairs={{0,4},{4,0},{1,5},{5,1},{2,6},{6,2},{3,7},{7,3}} | collective-permute-start | bytes 5898248 | tf_op jit(solution)/shard_map/ppermute | solution.py:435
  748.2 54.6 %copy-start.30 = (bf16[4,640,384]{2,1,0:T(8,128)(2,1)S(1)}, bf16[4,640,384]{2,1,0:T(8,128)(2,1)}, u32[]{:S(2)}) copy-start(bf16[4,640,384]{2,1,0:T(8,128)(2,1)} %copy-done.29) | copy-start | bytes 5898244
  748.2 55.1 %copy-start.34 = (bf16[4,640,384]{2,1,0:T(8,128)(2,1)S(1)}, bf16[4,640,384]{2,1,0:T(8,128)(2,1)}, u32[]{:S(2)}) copy-start(bf16[4,640,384]{2,1,0:T(8,128)(2,1)} %copy-done.33) | copy-start | bytes 5898244
  802.8 65.0 %collective-permute-start = (bf16[4,640,384]{2,1,0:T(8,128)(2,1)S(1)}, bf16[4,640,384]{2,1,0:T(8,128)(2,1)}, u32[]{:S(2)}, u32[]{:S(2)}) collective-permute-start(bf16[4,640,384]{2,1,0:T(8,128)(2,1)S(1)} %copy-done.30), channel_id=1, source_target_pairs={{0,4},{4,0},{1,5},{5,1},{2,6},{6,2},{3,7},{7,3}} | collective-permute-start | bytes 5898248 | tf_op jit(solution)/shard_map/ppermute | solution.py:435
  803.3 87.4 %collective-permute-start.21 = (bf16[4,640,384]{2,1,0:T(8,128)(2,1)S(1)}, bf16[4,640,384]{2,1,0:T(8,128)(2,1)}, u32[]{:S(2)}, u32[]{:S(2)}) collective-permute-start(bf16[4,640,384]{2,1,0:T(8,128)(2,1)S(1)} %copy-done.34), channel_id=1, source_target_pairs={{0,4},{4,0},{1,5},{5,1},{2,6},{6,2},{3,7},{7,3}} | collective-permute-start | bytes 5898248 | tf_op jit(solution)/shard_map/ppermute | solution.py:435
  804.8 128.0 %collective-permute-start.23 = (bf16[4,640,384]{2,1,0:T(8,128)(2,1)}, bf16[4,640,384]{2,1,0:T(8,128)(2,1)}, u32[]{:S(2)}, u32[]{:S(2)}) collective-permute-start(bf16[4,640,384]{2,1,0:T(8,128)(2,1)} %get-tuple-element.182), channel_id=1, source_target_pairs={{0,4},{4,0},{1,5},{5,1},{2,6},{6,2},{3,7},{7,3}} | collective-permute-start | bytes 5898248 | tf_op jit(solution)/shard_map/ppermute | solution.py:435
  805.3 169.7 %collective-permute-start.26 = (bf16[4,640,384]{2,1,0:T(8,128)(2,1)}, bf16[4,640,384]{2,1,0:T(8,128)(2,1)}, u32[]{:S(2)}, u32[]{:S(2)}) collective-permute-start(bf16[4,640,384]{2,1,0:T(8,128)(2,1)} %get-tuple-element.185), channel_id=1, source_target_pairs={{0,4},{4,0},{1,5},{5,1},{2,6},{6,2},{3,7},{7,3}} | collective-permute-start | bytes 5898248 | tf_op jit(solution)/shard_map/ppermute | solution.py:435
  806.9 210.3 %collective-permute-start.25 = (bf16[4,640,384]{2,1,0:T(8,128)(2,1)}, bf16[4,640,384]{2,1,0:T(8,128)(2,1)}, u32[]{:S(2)}, u32[]{:S(2)}) collective-permute-start(bf16[4,640,384]{2,1,0:T(8,128)(2,1)} %get-tuple-element.184), channel_id=1, source_target_pairs={{0,4},{4,0},{1,5},{5,1},{2,6},{6,2},{3,7},{7,3}} | collective-permute-start | bytes 5898248 | tf_op jit(solution)/shard_map/ppermute | solution.py:435
  807.4 53.1 %copy-start.12 = (bf16[4,640,384]{2,1,0:T(8,128)(2,1)S(1)}, bf16[4,640,384]{2,1,0:T(8,128)(2,1)}, u32[]{:S(2)}) copy-start(bf16[4,640,384]{2,1,0:T(8,128)(2,1)} %copy-done.11) | copy-start | bytes 5898244
  860.4 7.4 copy-start.22
  860.4 4.1 copy-start.16
  867.8 222.7 %collective-permute-start.16 = (bf16[4,640,384]{2,1,0:T(8,128)(2,1)}, bf16[4,640,384]{2,1,0:T(8,128)(2,1)}, u32[]{:S(2)}, u32[]{:S(2)}) collective-permute-start(bf16[4,640,384]{2,1,0:T(8,128)(2,1)} %get-tuple-element.169), channel_id=1, source_target_pairs={{0,4},{4,0},{1,5},{5,1},{2,6},{6,2},{3,7},{7,3}} | collective-permute-start | bytes 5898248 | tf_op jit(solution)/shard_map/ppermute | solution.py:435
  890.7 210.7 %collective-permute-start.40 = (bf16[4,640,384]{2,1,0:T(8,128)(2,1)}, bf16[4,640,384]{2,1,0:T(8,128)(2,1)}, u32[]{:S(2)}, u32[]{:S(2)}) collective-permute-start(bf16[4,640,384]{2,1,0:T(8,128)(2,1)} %get-tuple-element.212), channel_id=1, source_target_pairs={{0,4},{4,0},{1,5},{5,1},{2,6},{6,2},{3,7},{7,3}} | collective-permute-start | bytes 5898248 | tf_op jit(solution)/shard_map/ppermute | solution.py:435
  932.9 169.1 %collective-permute-start.18 = (bf16[4,640,384]{2,1,0:T(8,128)(2,1)}, bf16[4,640,384]{2,1,0:T(8,128)(2,1)}, u32[]{:S(2)}, u32[]{:S(2)}) collective-permute-start(bf16[4,640,384]{2,1,0:T(8,128)(2,1)} %add_convert_fusion.13), channel_id=1, source_target_pairs={{0,1},{1,0},{2,3},{3,2},{4,5},{5,4},{6,7},{7,6}} | collective-permute-start | bytes 5898248 | tf_op jit(solution)/shard_map/ppermute | solution.py:432
  975.0 127.2 %collective-permute-start.20 = (bf16[4,640,384]{2,1,0:T(8,128)(2,1)}, bf16[4,640,384]{2,1,0:T(8,128)(2,1)}, u32[]{:S(2)}, u32[]{:S(2)}) collective-permute-start(bf16[4,640,384]{2,1,0:T(8,128)(2,1)} %add_convert_fusion.12), channel_id=1, source_target_pairs={{0,1},{1,0},{2,3},{3,2},{4,5},{5,4},{6,7},{7,6}} | collective-permute-start | bytes 5898248 | tf_op jit(solution)/shard_map/ppermute | solution.py:432
  1017.1 126.4 %collective-permute-start.28 = (bf16[4,640,384]{2,1,0:T(8,128)(2,1)}, bf16[4,640,384]{2,1,0:T(8,128)(2,1)}, u32[]{:S(2)}, u32[]{:S(2)}) collective-permute-start(bf16[4,640,384]{2,1,0:T(8,128)(2,1)} %get-tuple-element.190), channel_id=1, source_target_pairs={{0,4},{4,0},{1,5},{5,1},{2,6},{6,2},{3,7},{7,3}} | collective-permute-start | bytes 5898248 | tf_op jit(solution)/shard_map/ppermute | solution.py:435
  1079.6 4.0 copy-start.21
  1090.5 121.0 %collective-permute-start.22 = (bf16[4,640,384]{2,1,0:T(8,128)(2,1)}, bf16[4,640,384]{2,1,0:T(8,128)(2,1)}, u32[]{:S(2)}, u32[]{:S(2)}) collective-permute-start(bf16[4,640,384]{2,1,0:T(8,128)(2,1)} %add_convert_fusion.11), channel_id=1, source_target_pairs={{0,2},{1,3},{2,0},{3,1},{4,6},{5,7},{6,4},{7,5}} | collective-permute-start | bytes 5898248 | tf_op jit(solution)/shard_map/ppermute | solution.py:432
  1101.4 122.3 %collective-permute-start.24 = (bf16[4,640,384]{2,1,0:T(8,128)(2,1)}, bf16[4,640,384]{2,1,0:T(8,128)(2,1)}, u32[]{:S(2)}, u32[]{:S(2)}) collective-permute-start(bf16[4,640,384]{2,1,0:T(8,128)(2,1)} %add_convert_fusion.10), channel_id=1, source_target_pairs={{0,2},{1,3},{2,0},{3,1},{4,6},{5,7},{6,4},{7,5}} | collective-permute-start | bytes 5898248 | tf_op jit(solution)/shard_map/ppermute | solution.py:432
  1101.9 122.2 %collective-permute-start.43 = (bf16[4,640,384]{2,1,0:T(8,128)(2,1)}, bf16[4,640,384]{2,1,0:T(8,128)(2,1)}, u32[]{:S(2)}, u32[]{:S(2)}) collective-permute-start(bf16[4,640,384]{2,1,0:T(8,128)(2,1)} %get-tuple-element.217), channel_id=1, source_target_pairs={{0,4},{4,0},{1,5},{5,1},{2,6},{6,2},{3,7},{7,3}} | collective-permute-start | bytes 5898248 | tf_op jit(solution)/shard_map/ppermute | solution.py:435
  1102.2 125.3 %collective-permute-start.45 = (bf16[4,640,384]{2,1,0:T(8,128)(2,1)}, bf16[4,640,384]{2,1,0:T(8,128)(2,1)}, u32[]{:S(2)}, u32[]{:S(2)}) collective-permute-start(bf16[4,640,384]{2,1,0:T(8,128)(2,1)} %get-tuple-element.221), channel_id=1, source_target_pairs={{0,4},{4,0},{1,5},{5,1},{2,6},{6,2},{3,7},{7,3}} | collective-permute-start | bytes 5898248 | tf_op jit(solution)/shard_map/ppermute | solution.py:435
  1143.5 84.7 %collective-permute-start.27 = (bf16[4,640,384]{2,1,0:T(8,128)(2,1)}, bf16[4,640,384]{2,1,0:T(8,128)(2,1)}, u32[]{:S(2)}, u32[]{:S(2)}) collective-permute-start(bf16[4,640,384]{2,1,0:T(8,128)(2,1)} %add_convert_fusion.9), channel_id=1, source_target_pairs={{0,3},{1,2},{2,1},{3,0},{4,7},{5,6},{6,5},{7,4}} | collective-permute-start | bytes 5898248 | tf_op jit(solution)/shard_map/ppermute | solution.py:432
  1211.6 5.1 copy-start.10
  1211.6 45.6 %collective-permute-start.29 = (bf16[4,640,384]{2,1,0:T(8,128)(2,1)S(1)}, bf16[4,640,384]{2,1,0:T(8,128)(2,1)}, u32[]{:S(2)}, u32[]{:S(2)}) collective-permute-start(bf16[4,640,384]{2,1,0:T(8,128)(2,1)S(1)} %add_convert_fusion.8), channel_id=1, source_target_pairs={{0,3},{1,2},{2,1},{3,0},{4,7},{5,6},{6,5},{7,4}} | collective-permute-start | bytes 5898248 | tf_op jit(solution)/shard_map/ppermute | solution.py:432
  1220.2 11.2 copy-start.18
  1223.7 11.1 copy-start.23
  1223.7 100.6 %collective-permute-start.34 = (bf16[4,640,384]{2,1,0:T(8,128)(2,1)}, bf16[4,640,384]{2,1,0:T(8,128)(2,1)}, u32[]{:S(2)}, u32[]{:S(2)}) collective-permute-start(bf16[4,640,384]{2,1,0:T(8,128)(2,1)} %get-tuple-element.200), channel_id=1, source_target_pairs={{0,4},{4,0},{1,5},{5,1},{2,6},{6,2},{3,7},{7,3}} | collective-permute-start | bytes 5898248 | tf_op jit(solution)/shard_map/ppermute | solution.py:435
  1224.2 100.5 %collective-permute-start.35 = (bf16[4,640,384]{2,1,0:T(8,128)(2,1)}, bf16[4,640,384]{2,1,0:T(8,128)(2,1)}, u32[]{:S(2)}, u32[]{:S(2)}) collective-permute-start(bf16[4,640,384]{2,1,0:T(8,128)(2,1)} %get-tuple-element.203), channel_id=1, source_target_pairs={{0,4},{4,0},{1,5},{5,1},{2,6},{6,2},{3,7},{7,3}} | collective-permute-start | bytes 5898248 | tf_op jit(solution)/shard_map/ppermute | solution.py:435
  1227.5 126.4 %collective-permute-start.36 = (bf16[4,640,384]{2,1,0:T(8,128)(2,1)}, bf16[4,640,384]{2,1,0:T(8,128)(2,1)}, u32[]{:S(2)}, u32[]{:S(2)}) collective-permute-start(bf16[4,640,384]{2,1,0:T(8,128)(2,1)} %get-tuple-element.206), channel_id=1, source_target_pairs={{0,4},{4,0},{1,5},{5,1},{2,6},{6,2},{3,7},{7,3}} | collective-permute-start | bytes 5898248 | tf_op jit(solution)/shard_map/ppermute | solution.py:435
  1228.3 166.9 %collective-permute-start.38 = (bf16[4,640,384]{2,1,0:T(8,128)(2,1)}, bf16[4,640,384]{2,1,0:T(8,128)(2,1)}, u32[]{:S(2)}, u32[]{:S(2)}) collective-permute-start(bf16[4,640,384]{2,1,0:T(8,128)(2,1)} %get-tuple-element.209), channel_id=1, source_target_pairs={{0,4},{4,0},{1,5},{5,1},{2,6},{6,2},{3,7},{7,3}} | collective-permute-start | bytes 5898248 | tf_op jit(solution)/shard_map/ppermute | solution.py:435
  1257.1 157.8 %collective-permute-start.41 = (bf16[4,640,384]{2,1,0:T(8,128)(2,1)}, bf16[4,640,384]{2,1,0:T(8,128)(2,1)}, u32[]{:S(2)}, u32[]{:S(2)}) collective-permute-start(bf16[4,640,384]{2,1,0:T(8,128)(2,1)} %add_convert_fusion.3), channel_id=1, source_target_pairs={{0,2},{1,3},{2,0},{3,1},{4,6},{5,7},{6,4},{7,5}} | collective-permute-start | bytes 5898248 | tf_op jit(solution)/shard_map/ppermute | solution.py:432
  1324.3 97.1 %collective-permute-start.42 = (bf16[4,640,384]{2,1,0:T(8,128)(2,1)}, bf16[4,640,384]{2,1,0:T(8,128)(2,1)}, u32[]{:S(2)}, u32[]{:S(2)}) collective-permute-start(bf16[4,640,384]{2,1,0:T(8,128)(2,1)} %add_convert_fusion.2), channel_id=1, source_target_pairs={{0,2},{1,3},{2,0},{3,1},{4,6},{5,7},{6,4},{7,5}} | collective-permute-start | bytes 5898248 | tf_op jit(solution)/shard_map/ppermute | solution.py:432
  1324.6 96.7 %collective-permute-start.44 = (bf16[4,640,384]{2,1,0:T(8,128)(2,1)}, bf16[4,640,384]{2,1,0:T(8,128)(2,1)}, u32[]{:S(2)}, u32[]{:S(2)}) collective-permute-start(bf16[4,640,384]{2,1,0:T(8,128)(2,1)} %add_convert_fusion.1), channel_id=1, source_target_pairs={{0,3},{1,2},{2,1},{3,0},{4,7},{5,6},{6,5},{7,4}} | collective-permute-start | bytes 5898248 | tf_op jit(solution)/shard_map/ppermute | solution.py:432
  1353.9 100.2 %collective-permute-start.46 = (bf16[4,640,384]{2,1,0:T(8,128)(2,1)}, bf16[4,640,384]{2,1,0:T(8,128)(2,1)}, u32[]{:S(2)}, u32[]{:S(2)}) collective-permute-start(bf16[4,640,384]{2,1,0:T(8,128)(2,1)} %add_convert_fusion), channel_id=1, source_target_pairs={{0,3},{1,2},{2,1},{3,0},{4,7},{5,6},{6,5},{7,4}} | collective-permute-start | bytes 5898248 | tf_op jit(solution)/shard_map/ppermute | solution.py:432
  1398.0 14.3 collective-permute-start.47
  1412.3 41.8 %collective-permute-start.37 = (bf16[4,640,384]{2,1,0:T(8,128)(2,1)}, bf16[4,640,384]{2,1,0:T(8,128)(2,1)S(1)}, u32[]{:S(2)}, u32[]{:S(2)}) collective-permute-start(bf16[4,640,384]{2,1,0:T(8,128)(2,1)} %add_convert_fusion.5), channel_id=1, source_target_pairs={{0,1},{1,0},{2,3},{3,2},{4,5},{5,4},{6,7},{7,6}} | collective-permute-start | bytes 5898248 | tf_op jit(solution)/shard_map/ppermute | solution.py:432
  1415.0 39.2 %collective-permute-start.39 = (bf16[4,640,384]{2,1,0:T(8,128)(2,1)}, bf16[4,640,384]{2,1,0:T(8,128)(2,1)}, u32[]{:S(2)}, u32[]{:S(2)}) collective-permute-start(bf16[4,640,384]{2,1,0:T(8,128)(2,1)} %add_convert_fusion.4), channel_id=1, source_target_pairs={{0,1},{1,0},{2,3},{3,2},{4,5},{5,4},{6,7},{7,6}} | collective-permute-start | bytes 5898248 | tf_op jit(solution)/shard_map/ppermute | solution.py:432
  1537.0 3.9 collective-permute-start.48
  1540.7 140.0 %collective-permute-start.30 = (bf16[8192,384]{1,0:T(8,128)(2,1)}, bf16[8192,384]{1,0:T(8,128)(2,1)}, u32[]{:S(2)}, u32[]{:S(2)}) collective-permute-start(bf16[8192,384]{1,0:T(8,128)(2,1)} %get-tuple-element.194.own_ref), channel_id=1, source_target_pairs={{0,4},{4,0},{1,5},{5,1},{2,6},{6,2},{3,7},{7,3}} | collective-permute-start | bytes 18874376 | tf_op jit(solution)/shard_map/ppermute | solution.py:435
  1558.7 255.8 %collective-permute-start.49 = (bf16[8192,384]{1,0:T(8,128)(2,1)}, bf16[8192,384]{1,0:T(8,128)(2,1)}, u32[]{:S(2)}, u32[]{:S(2)}) collective-permute-start(bf16[8192,384]{1,0:T(8,128)(2,1)} %shard_map.146.own_ref), channel_id=1, source_target_pairs={{0,4},{4,0},{1,5},{5,1},{2,6},{6,2},{3,7},{7,3}} | collective-permute-start | bytes 18874376 | tf_op jit(solution)/shard_map/ppermute | solution.py:435
  1560.6 61.7 %copy-start.40 = (f32[1,384]{1,0:T(1,128)S(1)}, f32[1,384]{1,0:T(1,128)}, u32[]{:S(2)}) copy-start(f32[1,384]{1,0:T(1,128)} %get-tuple-element.229) | copy-start | bytes 4612
  1560.6 61.8 %copy-start.37 = (f32[384,32]{1,0:T(8,128)S(1)}, f32[384,32]{1,0:T(8,128)}, u32[]{:S(2)}) copy-start(f32[384,32]{1,0:T(8,128)} %get-tuple-element.228) | copy-start | bytes 147460
  (28 other events, 59.0 us)
Sparse Core Ops, SparseCore 0:
  1624.2 40.3 all-reduce.1
